TPU v7x, 16 devices: a whole 2x2x2 slice. The times are simulated.
16 devices in a mesh: stage: 2 (over z), expert: 8 (over y, x, core).
Axes of the slice: x: 2, y: 2, z: 2, core: 2. Of those that a mesh axis runs over, the one named last changes fastest.
Arguments:
- x_acts: bfloat16 [2, 2, 8192, 640], P(None, 'stage', 'expert')
- expert_ids: int32 [2, 2, 8192, 4], P(None, 'stage', 'expert')
- gate_wts: float32 [2, 2, 8192, 4], P(None, 'stage', 'expert')
- w_in: bfloat16 [2, 32, 640, 640], P('stage', 'expert')
- w_up: bfloat16 [2, 32, 640, 640], P('stage', 'expert')
- w_out: bfloat16 [2, 32, 640, 640], P('stage', 'expert')
- d_out: bfloat16 [2, 8192, 640], P('stage', 'expert')
Outputs:
- output 1: bfloat16 [2, 8192, 640], P('stage', 'expert')
- output 2: bfloat16 [2, 8192, 640], P('stage', 'expert')
- output 3: bfloat16 [2, 32, 640, 640], P('stage', 'expert')
- output 4: bfloat16 [2, 32, 640, 640], P('stage', 'expert')
- output 5: bfloat16 [2, 32, 640, 640], P('stage', 'expert')
All inputs are finite; a program needn't handle non-finite values.
Results may differ from a plain program's by a relative error of at most 0.001.
Values are sent between devices in bfloat16 or wider.
A program may use at most 1 GiB of HBM per device.

v0:
```python
import jax
import jax.numpy as jnp
from jax import lax
from jax.sharding import PartitionSpec as P


def slot_onehot(expert_ids, gate_wts, num_experts, capacity):
    chosen = expert_ids[..., None] == jnp.arange(num_experts, dtype=jnp.int32)
    taken = jnp.any(chosen, axis=-2)
    gate_tok = jnp.sum(jnp.where(chosen, gate_wts[..., None], 0.0), axis=-2)
    slot_rank = jnp.cumsum(taken.astype(jnp.int32), axis=-2) - 1
    slot_hit = taken[..., None] & (slot_rank[..., None] == jnp.arange(capacity, dtype=jnp.int32))
    gate_slot = jnp.sum(jnp.where(slot_hit, gate_tok[..., None], 0.0), axis=-3)
    return slot_hit.astype(jnp.bfloat16), gate_slot


def expert_forward(x_rows, gate_rows, w_in, w_up, w_out):
    pre_in = jnp.einsum('ecd,edf->ecf', x_rows, w_in, preferred_element_type=jnp.float32)
    pre_up = jnp.einsum('ecd,edf->ecf', x_rows, w_up, preferred_element_type=jnp.float32)
    hidden = (jax.nn.silu(pre_in) * pre_up).astype(jnp.bfloat16)
    expert_out = jnp.einsum('ecf,efd->ecd', hidden, w_out, preferred_element_type=jnp.float32)
    return (gate_rows[..., None] * expert_out).astype(jnp.bfloat16)


def expert_backward(x_rows, dy_rows, gate_rows, w_in, w_up, w_out):
    pre_in = jnp.einsum('ecd,edf->ecf', x_rows, w_in, preferred_element_type=jnp.float32)
    pre_up = jnp.einsum('ecd,edf->ecf', x_rows, w_up, preferred_element_type=jnp.float32)
    sig_in = jax.nn.sigmoid(pre_in)
    act_in = pre_in * sig_in
    hidden = (act_in * pre_up).astype(jnp.bfloat16)
    gated_dy = (gate_rows[..., None] * dy_rows).astype(jnp.bfloat16)
    d_hidden = jnp.einsum('ecd,efd->ecf', gated_dy, w_out, preferred_element_type=jnp.float32)
    d_pre_in = (d_hidden * pre_up * sig_in * (1.0 + pre_in * (1.0 - sig_in))).astype(jnp.bfloat16)
    d_pre_up = (d_hidden * act_in).astype(jnp.bfloat16)
    dw_out = jnp.einsum('ecf,ecd->efd', hidden, gated_dy, preferred_element_type=jnp.float32)
    dw_in = jnp.einsum('ecd,ecf->edf', x_rows, d_pre_in, preferred_element_type=jnp.float32)
    dw_up = jnp.einsum('ecd,ecf->edf', x_rows, d_pre_up, preferred_element_type=jnp.float32)
    dx_rows = (jnp.einsum('ecf,edf->ecd', d_pre_in, w_in, preferred_element_type=jnp.float32)
               + jnp.einsum('ecf,edf->ecd', d_pre_up, w_up, preferred_element_type=jnp.float32))
    return (dx_rows.astype(jnp.bfloat16), dw_in.astype(jnp.bfloat16),
            dw_up.astype(jnp.bfloat16), dw_out.astype(jnp.bfloat16))


def solution(mesh):
    group_size = mesh.shape['expert']
    num_stages = mesh.shape['stage']
    to_next = [(src_idx, (src_idx + 1) % num_stages) for src_idx in range(num_stages)]
    to_prev = [((src_idx + 1) % num_stages, src_idx) for src_idx in range(num_stages)]

    def device_fn(x_acts, expert_ids, gate_wts, w_in, w_up, w_out, d_out):
        local_experts = w_in.shape[1]
        num_experts = local_experts * group_size
        tokens = x_acts.shape[2]
        top_k = expert_ids.shape[3]
        capacity = 3 * top_k * tokens // (2 * num_experts)
        w_in_loc, w_up_loc, w_out_loc = w_in[0], w_up[0], w_out[0]

        def dispatch(slot_buf):
            row_tail = slot_buf.shape[2:]
            split_buf = slot_buf.reshape((group_size, local_experts, capacity) + row_tail)
            received = lax.all_to_all(split_buf, 'expert', 0, 2, tiled=True)
            return received.reshape((local_experts, group_size * capacity) + row_tail)

        def collect(slot_buf):
            row_tail = slot_buf.shape[2:]
            split_buf = slot_buf.reshape((1, local_experts, group_size * capacity) + row_tail)
            received = lax.all_to_all(split_buf, 'expert', 2, 0, tiled=True)
            return received.reshape((num_experts, capacity) + row_tail)

        def to_slots(slot_hit, tok_rows):
            slot_buf = jnp.einsum('uec,ud->ecd', slot_hit, tok_rows, preferred_element_type=jnp.float32)
            return slot_buf.astype(jnp.bfloat16)

        def to_tokens(slot_hit, slot_buf):
            tok_rows = jnp.einsum('uec,ecd->ud', slot_hit, slot_buf, preferred_element_type=jnp.float32)
            return tok_rows.astype(jnp.bfloat16)

        x_fwd = lax.ppermute(x_acts[1, 0], 'stage', to_next)
        ids_fwd = lax.ppermute(expert_ids[1, 0], 'stage', to_next)
        gate_fwd = lax.ppermute(gate_wts[1, 0], 'stage', to_next)
        hit_fwd, gslot_fwd = slot_onehot(ids_fwd, gate_fwd, num_experts, capacity)
        x_recv = dispatch(to_slots(hit_fwd, x_fwd))
        gate_recv = dispatch(gslot_fwd)
        y_back = collect(expert_forward(x_recv, gate_recv, w_in_loc, w_up_loc, w_out_loc))
        y_dev = to_tokens(hit_fwd, y_back)

        x_bwd = lax.ppermute(x_acts[0, 0], 'stage', to_next)
        ids_bwd = lax.ppermute(expert_ids[0, 0], 'stage', to_next)
        gate_bwd = lax.ppermute(gate_wts[0, 0], 'stage', to_next)
        hit_bwd, gslot_bwd = slot_onehot(ids_bwd, gate_bwd, num_experts, capacity)
        x_recv_b = dispatch(to_slots(hit_bwd, x_bwd))
        dy_recv = dispatch(to_slots(hit_bwd, d_out[0]))
        gate_recv_b = dispatch(gslot_bwd)
        dx_rows, dw_in, dw_up, dw_out = expert_backward(
            x_recv_b, dy_recv, gate_recv_b, w_in_loc, w_up_loc, w_out_loc)
        dx_here = to_tokens(hit_bwd, collect(dx_rows))
        dx_dev = lax.ppermute(dx_here, 'stage', to_prev)
        return y_dev[None], dx_dev[None], dw_in[None], dw_up[None], dw_out[None]

    tok_spec = P(None, 'stage', 'expert', None)
    w_spec = P('stage', 'expert', None, None)
    row_spec = P('stage', 'expert', None)
    return jax.shard_map(device_fn, mesh=mesh,
                         in_specs=(tok_spec, tok_spec, tok_spec, w_spec, w_spec, w_spec, row_spec),
                         out_specs=(row_spec, row_spec, w_spec, w_spec, w_spec), check_vma=False)
```

profile of v0, /device:TPU:0, one launch (start us, length us, event | category | flops | bytes accessed | tf_op | source)
XLA Modules:
  0.0 568.1 jit_solution(3764369677323368023)
XLA Ops:
  0.6 1.5 slice_bitcast_fusion.3
  2.1 3.3 collective-permute-start.3
  7.8 9.0 %reduce-window.16 = s32[32,8,128]{2,1,0:T(8,128)S(1)} reduce-window(s32[32,8,128]{2,1,0:T(8,128)S(1)} %bitcast.156, s32[]{:T(128)} %constant.13.clone.1), window={size=1x1x128 pad=0_0x0_0x127_0}, to_apply=%region_6.7 | reduce-window | flops 4161536 | bytes 262148 | tf_op jit(solution)/shard_map/reduce-window.2
  19.4 6.2 %select_reduce_fusion = f32[32,192]{1,0:T(8,128)S(1)} fusion(f32[1024,32]{0,1:T(8,128)S(1)} %select_reduce_fusion.2, s32[1024,32]{0,1:T(8,128)S(1)} %bitcast.147, pred[1024,32]{0,1:T(8,128)(4,1)} %copy-done.6), kind=kLoop, calls=%fused_computation | loop fusion | flops 25159680 | bytes 319488 | tf_op jit(solution)/shard_map/reduce_sum | solution.py:13
  26.3 4.2 all-to-all-start.3
  30.4 15.3 %fusion.25 = bf16[32,192,640]{2,1,0:T(8,128)(2,1)} fusion(s32[1024,32]{0,1:T(8,128)S(1)} %bitcast.148, pred[1024,32]{0,1:T(8,128)(4,1)} %copy-done.6, bf16[1,1024,640]{2,1,0:T(8,128)(2,1)} %param.13), kind=kOutput, calls=%fused_computation.33 | convolution fusion | flops 8069578752 | bytes 9338880 | tf_op jit(solution)/shard_map/uec,ud->ecd/dot_general | solution.py:71
  46.4 5.3 all-to-all-start.4
  51.6 3.0 slice_bitcast_fusion
  54.6 1.6 collective-permute-start.5
  56.2 29.6 %collective-permute-done.5 = bf16[1024,640]{1,0:T(8,128)(2,1)S(1)} collective-permute-done((bf16[1024,640]{1,0:T(8,128)(2,1)S(1)}, bf16[1024,640]{1,0:T(8,128)(2,1)S(1)}, u32[]{:S(2)}, u32[]{:S(2)}) %collective-permute-start.5) | collective-permute-done | bytes 1310752 | tf_op jit(solution)/shard_map/ppermute | solution.py:87
  85.8 14.0 %fusion.28 = bf16[32,192,640]{2,1,0:T(8,128)(2,1)} fusion(s32[1024,32]{0,1:T(8,128)S(1)} %bitcast.149, pred[1024,32]{0,1:T(8,128)(4,1)S(1)} %copy-done.7, bf16[1024,640]{1,0:T(8,128)(2,1)S(1)} %collective-permute-done.5), kind=kOutput, calls=%fused_computation.34 | convolution fusion | flops 8069578752 | bytes 9338880 | tf_op jit(solution)/shard_map/uec,ud->ecd/dot_general | solution.py:71
  99.8 40.2 %all-to-all-done.4 = bf16[8,4,192,640]{3,2,1,0:T(8,128)(2,1)} async-done(((bf16[8,4,192,640]{3,2,1,0:T(8,128)(2,1)}), bf16[8,4,192,640]{3,2,1,0:T(8,128)(2,1)}, u32[]{:S(2)}, u32[]{:S(2)}) %all-to-all-start.4) | async-done | bytes 7864352 | tf_op jit(solution)/shard_map/all_to_all | solution.py:61
  140.0 5.0 all-to-all-start.5
  145.1 1.6 collective-permute-start
  147.1 1.6 collective-permute-start.2
  149.5 9.0 %reduce-window.14 = s32[32,8,128]{2,1,0:T(8,128)S(1)} reduce-window(s32[32,8,128]{2,1,0:T(8,128)S(1)} %bitcast.157, s32[]{:T(128)} %constant.13.clone.1), window={size=1x1x128 pad=0_0x0_0x127_0}, to_apply=%region_1.2 | reduce-window | flops 4161536 | bytes 262148 | tf_op jit(solution)/shard_map/reduce-window
  161.1 6.2 %select_reduce_fusion.1 = f32[32,192]{1,0:T(8,128)S(1)} fusion(f32[1024,32]{0,1:T(8,128)S(1)} %select_reduce_fusion.3, s32[1024,32]{0,1:T(8,128)S(1)} %bitcast.151, pred[1024,32]{0,1:T(8,128)(4,1)} %copy-done.9), kind=kLoop, calls=%fused_computation.2 | loop fusion | flops 25159680 | bytes 319488 | tf_op jit(solution)/shard_map/reduce_sum | solution.py:13
  168.8 9.0 %collective-permute-done.2 = bf16[1024,640]{1,0:T(8,128)(2,1)} collective-permute-done((bf16[1024,640]{1,0:T(8,128)(2,1)}, bf16[1024,640]{1,0:T(8,128)(2,1)}, u32[]{:S(2)}, u32[]{:S(2)}) %collective-permute-start.2) | collective-permute-done | bytes 1310752 | tf_op jit(solution)/shard_map/ppermute | solution.py:78
  177.8 26.7 %fusion.31 = bf16[32,192,640]{2,1,0:T(8,128)(2,1)} fusion(s32[1024,32]{0,1:T(8,128)S(1)} %bitcast.152, pred[1024,32]{0,1:T(8,128)(4,1)} %copy-done.9, bf16[1024,640]{1,0:T(8,128)(2,1)} %collective-permute-done.2), kind=kOutput, calls=%fused_computation.35 | convolution fusion | flops 8069578752 | bytes 9338880 | tf_op jit(solution)/shard_map/uec,ud->ecd/dot_general | solution.py:71
  204.5 10.7 %convert_bitcast_fusion = f32[1,4,8,192,640]{4,3,1,2,0:T(8,128)} fusion(bf16[8,4,192,640]{3,2,1,0:T(8,128)(2,1)} %all-to-all-done.4), kind=kLoop, calls=%fused_computation.11 | loop fusion | flops 3932160 | bytes 23592960 | tf_op jit(solution)/shard_map/convert_element_type | solution.py:31
  215.2 12.7 %copy.87 = f32[1,4,8,192,640]{4,3,2,1,0:T(8,128)} copy(f32[1,4,8,192,640]{4,3,1,2,0:T(8,128)} %convert_bitcast_fusion) | data formatting | bytes 31457280 | tf_op jit(solution)/shard_map/convert_element_type | solution.py:31
  227.9 5.5 all-to-all-done.5
  233.4 3.3 all-to-all-start
  236.8 7.1 %copy.88 = bf16[1,4,8,192,640]{4,3,2,1,0:T(8,128)(2,1)} copy(bf16[1,4,8,192,640]{4,3,1,2,0:T(8,128)(2,1)} %bitcast.39) | data formatting | bytes 15728640 | tf_op jit(solution)/shard_map/all_to_all | solution.py:61
  243.9 13.0 %fusion.45 = f32[4,1536,640]{2,1,0:T(8,128)} fusion(bf16[4,1536,640]{2,1,0:T(8,128)(2,1)} %bitcast.137, bf16[1,4,640,640]{3,2,1,0:T(8,128)(2,1)S(1)} %copy-done), kind=kOutput, calls=%fused_computation.46 | convolution fusion | flops 5033164800 | bytes 26869760 | tf_op jit(solution)/shard_map/ecd,edf->ecf/dot_general | solution.py:26
  256.9 4.9 all-to-all-start.1
  261.8 13.5 %fusion.39 = f32[4,1536,640]{2,1,0:T(8,128)} fusion(bf16[4,1536,640]{2,1,0:T(8,128)(2,1)} %bitcast.138, bf16[1,4,640,640]{3,2,1,0:T(8,128)(2,1)} %param.11), kind=kOutput, calls=%fused_computation.41 | convolution fusion | flops 5033164800 | bytes 26869760 | tf_op jit(solution)/shard_map/ecd,edf->ecf/dot_general | solution.py:27
  275.3 25.3 %multiply_convert_fusion.1 = (bf16[4,1536,640]{2,1,0:T(8,128)(2,1)}, bf16[4,1536,640]{2,1,0:T(8,128)(2,1)}) fusion(f32[4,1536,640]{2,1,0:T(8,128)} %fusion.45, f32[4,1536,640]{2,1,0:T(8,128)} %fusion.39, bf16[1,4,640,640]{3,2,1,0:T(8,128)(2,1)} %param.12, f32[4,1536,640]{2,1,0:T(8,128)} %bitcast.134, f32[4,1536]{1,0:T(4,128)S(1)} %mul.53), kind=kOutput, calls=%fused_computation.14 | convolution fusion | flops 5092147200 | bytes 66215936 | tf_op jit(solution)/shard_map/ecd,efd->ecf/dot_general | solution.py:32
  300.6 13.0 %fusion.43 = f32[4,1536,640]{2,1,0:T(8,128)} fusion(bf16[4,1536,640]{2,1,0:T(8,128)(2,1)} %get-tuple-element.6, bf16[1,4,640,640]{3,2,1,0:T(8,128)(2,1)S(1)} %copy-done), kind=kOutput, calls=%fused_computation.44 | convolution fusion | flops 5033164800 | bytes 26869760 | tf_op jit(solution)/shard_map/ecf,edf->ecd/dot_general | solution.py:38
  313.6 14.7 %fusion.23 = bf16[1,4,1536,640]{3,2,1,0:T(8,128)(2,1)} fusion(f32[4,1536,640]{2,1,0:T(8,128)} %fusion.43, bf16[4,1536,640]{2,1,0:T(8,128)(2,1)} %get-tuple-element.5, bf16[1,4,640,640]{3,2,1,0:T(8,128)(2,1)} %param.11), kind=kOutput, calls=%fused_computation.31 | convolution fusion | flops 5041029120 | bytes 34734080 | tf_op jit(solution)/shard_map/ecf,edf->ecd/dot_general | solution.py:39
  328.3 27.6 %copy.89 = bf16[1,4,1536,640]{3,1,0,2:T(4,128)(2,1)} copy(bf16[1,4,1536,640]{3,2,1,0:T(8,128)(2,1)} %fusion.23) | data formatting | bytes 15728640 | tf_op jit(solution)/shard_map/reshape | solution.py:66
  356.0 5.0 all-to-all-start.6
  361.0 7.2 %copy.81 = bf16[1,4,8,192,640]{4,3,2,1,0:T(8,128)(2,1)} copy(bf16[1,4,8,192,640]{4,3,1,2,0:T(8,128)(2,1)} %bitcast.11) | data formatting | bytes 15728640 | tf_op jit(solution)/shard_map/all_to_all | solution.py:61
  368.2 13.0 %fusion.47 = f32[4,1536,640]{2,1,0:T(8,128)} fusion(bf16[4,1536,640]{2,1,0:T(8,128)(2,1)} %bitcast.143, bf16[1,4,640,640]{3,2,1,0:T(8,128)(2,1)S(1)} %copy-done), kind=kOutput, calls=%fused_computation.48 | convolution fusion | flops 5033164800 | bytes 26869760 | tf_op jit(solution)/shard_map/ecd,edf->ecf/dot_general | solution.py:18
  381.2 19.5 %fusion.34 = bf16[1,4,1536,640]{3,2,1,0:T(8,128)(2,1)} fusion(f32[4,1536,640]{2,1,0:T(8,128)} %fusion.47, bf16[4,1536,640]{2,1,0:T(8,128)(2,1)} %bitcast.144, f32[4,1536]{1,0:T(4,128)S(1)} %mul.48, bf16[1,4,640,640]{3,2,1,0:T(8,128)(2,1)} %param.12, bf16[1,4,640,640]{3,2,1,0:T(8,128)(2,1)} %param.11), kind=kOutput, calls=%fused_computation.36 | convolution fusion | flops 10097786880 | bytes 38035456 | tf_op jit(solution)/shard_map/ecf,efd->ecd/dot_general | solution.py:21
  400.6 27.3 %copy.82 = bf16[1,4,1536,640]{3,1,0,2:T(4,128)(2,1)} copy(bf16[1,4,1536,640]{3,2,1,0:T(8,128)(2,1)} %fusion.34) | data formatting | bytes 15728640 | tf_op jit(solution)/shard_map/reshape | solution.py:66
  427.9 21.4 %all-to-all-done.6 = bf16[1,4,1536,640]{3,1,0,2:T(4,128)(2,1)} async-done(((bf16[1,4,1536,640]{3,1,0,2:T(4,128)(2,1)}), bf16[1,4,1536,640]{3,1,0,2:T(4,128)(2,1)}, u32[]{:S(2)}, u32[]{:S(2)}) %all-to-all-start.6) | async-done | bytes 7864352 | tf_op jit(solution)/shard_map/all_to_all | solution.py:67
  449.3 5.1 all-to-all-start.2
  454.4 13.6 %convert_bitcast_fusion.2 = bf16[1,4,640,640]{3,2,1,0:T(8,128)(2,1)} fusion(bf16[4,1536,640]{2,1,0:T(8,128)(2,1)} %bitcast.139, bf16[4,1536,640]{2,1,0:T(8,128)(2,1)} %get-tuple-element.5), kind=kOutput, calls=%fused_computation.51 | convolution fusion | flops 5034803200 | bytes 19005440 | tf_op jit(solution)/shard_map/ecd,ecf->edf/dot_general | solution.py:37
  467.9 13.8 %convert_bitcast_fusion.3 = bf16[1,4,640,640]{3,2,1,0:T(8,128)(2,1)} fusion(bf16[4,1536,640]{2,1,0:T(8,128)(2,1)} %bitcast.140, bf16[4,1536,640]{2,1,0:T(8,128)(2,1)} %get-tuple-element.6), kind=kOutput, calls=%fused_computation.52 | convolution fusion | flops 5034803200 | bytes 19005440 | tf_op jit(solution)/shard_map/ecd,ecf->edf/dot_general | solution.py:36
  481.7 19.4 %convert_bitcast_fusion.1 = bf16[1,4,640,640]{3,2,1,0:T(8,128)(2,1)} fusion(f32[4,1536,640]{2,1,0:T(8,128)} %bitcast.135, f32[4,1536]{1,0:T(4,128)S(1)} %mul.53, f32[4,1536,640]{2,1,0:T(8,128)} %fusion.39, f32[4,1536,640]{2,1,0:T(8,128)} %fusion.45), kind=kOutput, calls=%fused_computation.50 | convolution fusion | flops 5066260480 | bytes 50487296 | tf_op jit(solution)/shard_map/ecf,ecd->efd/dot_general | solution.py:35
  501.2 7.9 %copy.90 = bf16[1,4,8,192,640]{4,3,1,2,0:T(8,128)(2,1)} copy(bf16[1,4,8,192,640]{4,1,3,2,0:T(4,128)(2,1)} %bitcast.42) | data formatting | bytes 15728640 | tf_op jit(solution)/shard_map/all_to_all | solution.py:67
  509.1 14.2 %bitcast_convert_fusion = bf16[1024,640]{1,0:T(8,128)(2,1)} fusion(bf16[32,192,640]{2,1,0:T(8,128)(2,1)} %bitcast.145, s32[1024,32]{0,1:T(8,128)S(1)} %bitcast.150, pred[1024,32]{0,1:T(8,128)(4,1)S(1)} %copy-done.8), kind=kOutput, calls=%fused_computation.53 | convolution fusion | flops 8066301952 | bytes 9338880 | tf_op jit(solution)/shard_map/uec,ecd->ud/dot_general | solution.py:75
  523.3 1.6 collective-permute-start.6
  524.9 17.7 %all-to-all-done.2 = bf16[1,4,1536,640]{3,1,0,2:T(4,128)(2,1)} async-done(((bf16[1,4,1536,640]{3,1,0,2:T(4,128)(2,1)}), bf16[1,4,1536,640]{3,1,0,2:T(4,128)(2,1)}, u32[]{:S(2)}, u32[]{:S(2)}) %all-to-all-start.2) | async-done | bytes 7864352 | tf_op jit(solution)/shard_map/all_to_all | solution.py:67
  542.6 7.9 %copy.83 = bf16[1,4,8,192,640]{4,3,1,2,0:T(8,128)(2,1)} copy(bf16[1,4,8,192,640]{4,1,3,2,0:T(4,128)(2,1)} %bitcast.17) | data formatting | bytes 15728640 | tf_op jit(solution)/shard_map/all_to_all | solution.py:67
  550.5 14.7 %fusion.54 = bf16[1,1024,640]{2,1,0:T(8,128)(2,1)} fusion(bf16[32,192,640]{2,1,0:T(8,128)(2,1)} %bitcast.146, s32[1024,32]{0,1:T(8,128)S(1)} %bitcast.153, pred[1024,32]{0,1:T(8,128)(4,1)S(1)} %copy-done.10), kind=kOutput, calls=%fused_computation.55 | convolution fusion | flops 8066301952 | bytes 9338880 | tf_op jit(solution)/shard_map/uec,ecd->ud/dot_general | solution.py:75
  565.2 2.5 copy.106
  (65 shorter events, 11.6 us)
Async XLA Ops:
  0.6 243.3 %copy-start = (bf16[1,4,640,640]{3,2,1,0:T(8,128)(2,1)S(1)}, bf16[1,4,640,640]{3,2,1,0:T(8,128)(2,1)}, u32[]{:S(2)}) copy-start(bf16[1,4,640,640]{3,2,1,0:T(8,128)(2,1)} %param.10) | copy-start | bytes 9830404
  2.1 5.0 collective-permute-start.3
  6.8 11.8 %collective-permute-start.4 = (f32[1024,4]{0,1:T(4,128)}, f32[1024,4]{0,1:T(4,128)}, u32[]{:S(2)}, u32[]{:S(2)}) collective-permute-start(f32[1024,4]{0,1:T(4,128)} %get-tuple-element.9), channel_id=1, source_target_pairs={{0,8},{8,0},{1,9},{9,1},{2,10},{10,2},{3,11},{11,3},{4,12},{12,4},... | collective-permute-start | bytes 49160 | tf_op jit(solution)/shard_map/ppermute | solution.py:89
  7.2 0.6 copy-start.6
  18.6 67.3 %copy-start.2 = (s32[4,8,8,128]{3,1,2,0:T(8,128)}, s32[4,8,8,128]{3,1,2,0:T(8,128)S(1)}, u32[]{:S(2)}) copy-start(s32[4,8,8,128]{3,1,2,0:T(8,128)S(1)} %copy.103) | copy-start | bytes 393220
  26.3 19.5 %all-to-all-start.3 = ((f32[8,4,192]{2,1,0:T(4,128)}), f32[8,4,192]{2,1,0:T(4,128)S(1)}, u32[]{:S(2)}, u32[]{:S(2)}) async-start(f32[8,4,192]{2,1,0:T(4,128)} %reshape.102), calls=%async_computation.3 | async-start | bytes 65536 | tf_op jit(solution)/shard_map/all_to_all | solution.py:61
  45.7 0.6 copy-start.11
  46.4 39.5 %copy-start.7 = (pred[1024,32]{0,1:T(8,128)(4,1)S(1)}, pred[1024,32]{0,1:T(8,128)(4,1)}, u32[]{:S(2)}) copy-start(pred[1024,32]{0,1:T(8,128)(4,1)} %copy-done.6) | copy-start | bytes 98308
  46.4 93.7 %all-to-all-start.4 = ((bf16[8,4,192,640]{3,2,1,0:T(8,128)(2,1)}), bf16[8,4,192,640]{3,2,1,0:T(8,128)(2,1)}, u32[]{:S(2)}, u32[]{:S(2)}) async-start(bf16[8,4,192,640]{3,2,1,0:T(8,128)(2,1)} %bitcast.142), calls=%async_computation.4 | async-start | bytes 15728640 | tf_op jit(solution)/shard_map/all_to_all | solution.py:61
  54.6 31.2 %collective-permute-start.5 = (bf16[1024,640]{1,0:T(8,128)(2,1)S(1)}, bf16[1024,640]{1,0:T(8,128)(2,1)S(1)}, u32[]{:S(2)}, u32[]{:S(2)}) collective-permute-start(bf16[1024,640]{1,0:T(8,128)(2,1)S(1)} %get-tuple-element.7), channel_id=1, source_target_pairs={{0,8},{8,0},{1,9},{9,1},{2,10},{10,2},{3,11},{11,3},{4,12},{12,4},... | collective-permute-start | bytes 3932168 | tf_op jit(solution)/shard_map/ppermute | solution.py:87
  140.0 5.0 copy-start.12
  140.0 93.4 %all-to-all-start.5 = ((bf16[8,4,192,640]{3,2,1,0:T(8,128)(2,1)}), bf16[8,4,192,640]{3,2,1,0:T(8,128)(2,1)}, u32[]{:S(2)}, u32[]{:S(2)}) async-start(bf16[8,4,192,640]{3,2,1,0:T(8,128)(2,1)} %bitcast.136), calls=%async_computation.5 | async-start | bytes 15728640 | tf_op jit(solution)/shard_map/all_to_all | solution.py:61
  145.1 3.8 collective-permute-start
  146.7 13.6 %collective-permute-start.1 = (f32[1024,4]{0,1:T(4,128)}, f32[1024,4]{0,1:T(4,128)}, u32[]{:S(2)}, u32[]{:S(2)}) collective-permute-start(f32[1024,4]{0,1:T(4,128)} %get-tuple-element.10), channel_id=1, source_target_pairs={{0,8},{8,0},{1,9},{9,1},{2,10},{10,2},{3,11},{11,3},{4,12},{12,4},... | collective-permute-start | bytes 49160 | tf_op jit(solution)/shard_map/ppermute | solution.py:80
  147.1 30.6 %collective-permute-start.2 = (bf16[1024,640]{1,0:T(8,128)(2,1)}, bf16[1024,640]{1,0:T(8,128)(2,1)}, u32[]{:S(2)}, u32[]{:S(2)}) collective-permute-start(bf16[1024,640]{1,0:T(8,128)(2,1)} %get-tuple-element.8), channel_id=1, source_target_pairs={{0,8},{8,0},{1,9},{9,1},{2,10},{10,2},{3,11},{11,3},{4,12},{12,4},... | collective-permute-start | bytes 3932168 | tf_op jit(solution)/shard_map/ppermute | solution.py:78
  148.9 0.6 copy-start.9
  160.3 44.2 %copy-start.4 = (s32[4,8,8,128]{3,1,2,0:T(8,128)}, s32[4,8,8,128]{3,1,2,0:T(8,128)S(1)}, u32[]{:S(2)}) copy-start(s32[4,8,8,128]{3,1,2,0:T(8,128)S(1)} %copy.104) | copy-start | bytes 393220
  233.4 23.5 %all-to-all-start = ((f32[8,4,192]{2,1,0:T(4,128)}), f32[8,4,192]{2,1,0:T(4,128)S(1)}, u32[]{:S(2)}, u32[]{:S(2)}) async-start(f32[8,4,192]{2,1,0:T(4,128)} %reshape.95), calls=%async_computation | async-start | bytes 65536 | tf_op jit(solution)/shard_map/all_to_all | solution.py:61
  256.9 99.1 %all-to-all-start.1 = ((bf16[8,4,192,640]{3,2,1,0:T(8,128)(2,1)}), bf16[8,4,192,640]{3,2,1,0:T(8,128)(2,1)}, u32[]{:S(2)}, u32[]{:S(2)}) async-start(bf16[8,4,192,640]{3,2,1,0:T(8,128)(2,1)} %bitcast.141), calls=%async_computation.1 | async-start | bytes 15728640 | tf_op jit(solution)/shard_map/all_to_all | solution.py:61
  356.0 93.3 %all-to-all-start.6 = ((bf16[1,4,1536,640]{3,1,0,2:T(4,128)(2,1)}), bf16[1,4,1536,640]{3,1,0,2:T(4,128)(2,1)}, u32[]{:S(2)}, u32[]{:S(2)}) async-start(bf16[1,4,1536,640]{3,1,0,2:T(4,128)(2,1)} %copy.89), calls=%async_computation.6 | async-start | bytes 15728640 | tf_op jit(solution)/shard_map/all_to_all | solution.py:67
  449.3 93.3 %all-to-all-start.2 = ((bf16[1,4,1536,640]{3,1,0,2:T(4,128)(2,1)}), bf16[1,4,1536,640]{3,1,0,2:T(4,128)(2,1)}, u32[]{:S(2)}, u32[]{:S(2)}) async-start(bf16[1,4,1536,640]{3,1,0,2:T(4,128)(2,1)} %copy.82), calls=%async_computation.2 | async-start | bytes 15728640 | tf_op jit(solution)/shard_map/all_to_all | solution.py:67
  501.2 7.9 %copy-start.3 = (s32[4,8,8,128]{3,1,2,0:T(8,128)S(1)}, s32[4,8,8,128]{3,1,2,0:T(8,128)}, u32[]{:S(2)}) copy-start(s32[4,8,8,128]{3,1,2,0:T(8,128)} %copy-done.2) | copy-start | bytes 393220
  501.2 7.9 %copy-start.8 = (pred[1024,32]{0,1:T(8,128)(4,1)S(1)}, pred[1024,32]{0,1:T(8,128)(4,1)}, u32[]{:S(2)}) copy-start(pred[1024,32]{0,1:T(8,128)(4,1)} %copy-done.6) | copy-start | bytes 98308
  523.3 41.9 %collective-permute-start.6 = (bf16[1024,640]{1,0:T(8,128)(2,1)}, bf16[1024,640]{1,0:T(8,128)(2,1)}, u32[]{:S(2)}, u32[]{:S(2)}) collective-permute-start(bf16[1024,640]{1,0:T(8,128)(2,1)} %bitcast_convert_fusion), channel_id=1, source_target_pairs={{8,0},{0,8},{9,1},{1,9},{10,2},{2,10},{11,3},{3,11},{12,4},{4,12},... | collective-permute-start | bytes 3932168 | tf_op jit(solution)/shard_map/ppermute | solution.py:97
  542.6 7.9 %copy-start.5 = (s32[4,8,8,128]{3,1,2,0:T(8,128)S(1)}, s32[4,8,8,128]{3,1,2,0:T(8,128)}, u32[]{:S(2)}) copy-start(s32[4,8,8,128]{3,1,2,0:T(8,128)} %copy-done.4) | copy-start | bytes 393220
  542.6 7.9 %copy-start.10 = (pred[1024,32]{0,1:T(8,128)(4,1)S(1)}, pred[1024,32]{0,1:T(8,128)(4,1)}, u32[]{:S(2)}) copy-start(pred[1024,32]{0,1:T(8,128)(4,1)} %copy-done.9) | copy-start | bytes 98308
  550.5 17.2 %copy-start.1 = (bf16[1,4,640,640]{3,2,1,0:T(8,128)(2,1)S(1)}, bf16[1,4,640,640]{3,2,1,0:T(8,128)(2,1)}, u32[]{:S(2)}) copy-start(bf16[1,4,640,640]{3,2,1,0:T(8,128)(2,1)} %param.10) | copy-start | bytes 9830404
where the time goes:
time: 578 us; the launch traced here: 568 us
  matrix products  244 us (42%)
  waiting for transfers between devices  124 us (21%)
  local copies, waits for them, and re-layouts  112 us (19%)
  other arithmetic  44.5 us (8%)
  starting transfers between devices  42.9 us (7%)
    dot_general x3, matrix products, to_slots(): jnp.einsum('uec,ud->ecd', slot_hit, tok_rows, preferred_element_type=jnp....  56 us
    reshape x2, local copies, waits for them, and re-layouts, collect(): slot_buf.reshape((1, local_experts, group_size * capacity) + row_tail)  54.9 us
    all_to_all x5, waiting for transfers between devices, dispatch(): received = lax.all_to_all(split_buf, 'expert', 0, 2, tiled=True)  45.7 us
    all_to_all x2, waiting for transfers between devices, collect(): received = lax.all_to_all(split_buf, 'expert', 2, 0, tiled=True)  39 us
    ppermute x1, waiting for transfers between devices, device_fn(): x_bwd = lax.ppermute(x_acts[0, 0], 'stage', to_next)  29.6 us
    dot_general x2, matrix products, to_tokens(): jnp.einsum('uec,ecd->ud', slot_hit, slot_buf, preferred_element_type=jnp....  28.9 us
    dot_general x1, matrix products, expert_backward(): jnp.einsum('ecd,efd->ecf', gated_dy, w_out, preferred_element_type=jnp.fl...  25.3 us
    all_to_all x5, starting transfers between devices, dispatch(): received = lax.all_to_all(split_buf, 'expert', 0, 2, tiled=True)  22.7 us
  transfers between devices with their start and end apart: 14, of which 8 were waited for; matrix products, arithmetic and copies ran while one was open for 68% of the time, Pallas kernels for 0%

commit v1 on v0

v1 whole, which is shorter than its diff:
```python
import functools

import jax
import jax.numpy as jnp
from jax import lax
from jax.experimental import pallas as pl
from jax.experimental.pallas import tpu as pltpu
from jax.sharding import PartitionSpec as P

MESH = pl.DeviceIdType.MESH
F32, BF16 = jnp.float32, jnp.bfloat16
DY, XF, XB, TAB = 0, 1, 2, 3
NG, NE, CAP = 8, 4, 192


def dot(lhs, rhs, dims=((1,), (0,))):
    return lax.dot_general(lhs, rhs, (dims, ((), ())), preferred_element_type=F32)


def slot_hits(code_rows, tokens):
    slot = lax.broadcasted_iota(jnp.int32, (CAP, tokens), 0).astype(F32)
    return [slot == code_rows[e:e + 1, :] for e in range(NE)]


def dispatch_kernel(x_ref, dy_ref, tab_ref, win_ref, wup_ref, wout_ref,
                    c_ref, xb_ref, q_ref, code_ref,
                    buf, tabs, codes, gates, gslot, xs, st, cst, wbuf,
                    ssem, rsem, lsem, wsem, stsem, csem):
    stage = lax.axis_index('stage')
    me = lax.axis_index('expert')
    other = 1 - stage
    sib = me + 1 - 2 * (me % 2)
    xn = me + 2 - 4 * ((me // 2) % 2)
    yn = me + 4 - 8 * (me // 4)
    dg = xn + 4 - 8 * (xn // 4)
    sib_of = lambda h: h + 1 - 2 * (h % 2)
    tokens = x_ref.shape[2]
    half = tokens // 2
    sends = []

    barrier = pltpu.get_barrier_semaphore()
    for peer in ((other, me), (stage, sib), (stage, xn), (stage, yn)):
        pl.semaphore_signal(barrier, inc=1, device_id=peer, device_id_type=MESH)
    pl.semaphore_wait(barrier, 4)

    def place(arr, h, part):
        if arr == TAB:
            return tabs.at[h]
        if arr == XB:
            return xb_ref.at[h, pl.ds(part * half, half)]
        return buf.at[arr, h, pl.ds(part * half, half)]

    def remote(arr, h, part, slot, peer, src=None):
        return pltpu.make_async_remote_copy(
            src_ref=place(arr, h, part) if src is None else src, dst_ref=place(arr, h, part),
            send_sem=ssem.at[arr, slot], recv_sem=rsem.at[arr, h, part],
            device_id=peer, device_id_type=MESH)

    def send(arr, h, part, slot, peer, src=None):
        copy = remote(arr, h, part, slot, peer, src)
        copy.start()
        sends.append(copy)

    def arrived(arr, h, part):
        remote(arr, h, part, 0, (stage, sib)).wait_recv()

    to_x, to_y, to_sib, to_z = (stage, xn), (stage, yn), (stage, sib), (other, me)

    send(TAB, me, 0, 14, to_z, tab_ref)
    for part in range(2):
        send(XF, me, part, 14 + part, to_z, x_ref.at[1, 0, pl.ds(part * half, half)])
    for part in range(2):
        send(XB, me, part, 14 + part, to_z, x_ref.at[0, 0, pl.ds(part * half, half)])
    dy_half = lambda part: dy_ref.at[0, pl.ds(part * half, half)]
    send(DY, me, 0, 0, to_x, dy_half(0))
    send(DY, me, 1, 2, to_y, dy_half(1))
    send(DY, me, 0, 4, to_sib, dy_half(0))
    send(DY, me, 1, 5, to_sib, dy_half(1))
    own_dy = pltpu.make_async_copy(dy_ref.at[0], buf.at[DY, me], lsem)
    own_dy.start()

    def weights(e):
        return [pltpu.make_async_copy(w.at[0, e], wbuf.at[e % 2, k], wsem.at[e % 2, k])
                for k, w in enumerate((win_ref, wup_ref, wout_ref))]

    for e in range(2):
        for copy in weights(e):
            copy.start()

    arrived(TAB, me, 0)
    send(TAB, me, 0, 0, to_x)
    send(TAB, me, 0, 2, to_y)
    send(TAB, me, 0, 4, to_sib)
    send(DY, me, 1, 1, to_x, dy_half(1))
    send(DY, me, 0, 3, to_y, dy_half(0))

    def first_halves(arr):
        arrived(arr, xn, 0)
        arrived(arr, yn, 1)
        send(arr, xn, 0, 6, to_y)
        send(arr, yn, 1, 7, to_x)
        send(arr, xn, 0, 8, to_sib)
        send(arr, yn, 1, 11, to_sib)

    def second_halves(arr):
        arrived(arr, xn, 1)
        arrived(arr, yn, 0)
        send(arr, xn, 1, 9, to_sib)
        send(arr, yn, 0, 10, to_sib)

    def diagonal(arr):
        for part in range(2):
            arrived(arr, dg, part)
            send(arr, dg, part, 12 + part, to_sib)

    def own_sends(arr):
        for part in range(2):
            arrived(arr, me, part)
        send(arr, me, 0, 0, to_x)
        send(arr, me, 1, 2, to_y)
        send(arr, me, 1, 1, to_x)
        send(arr, me, 0, 3, to_y)
        send(arr, me, 0, 4, to_sib)
        send(arr, me, 1, 5, to_sib)

    arrived(TAB, xn, 0)
    arrived(TAB, yn, 0)
    send(TAB, xn, 0, 6, to_y)
    first_halves(DY)
    send(TAB, xn, 0, 8, to_sib)
    send(TAB, yn, 0, 10, to_sib)
    own_sends(XF)
    second_halves(DY)
    arrived(TAB, dg, 0)
    send(TAB, dg, 0, 12, to_sib)
    for h in (sib, sib_of(xn), sib_of(yn), sib_of(dg)):
        arrived(TAB, h, 0)

    upper = (lax.broadcasted_iota(jnp.int32, (tokens, tokens), 0)
             <= lax.broadcasted_iota(jnp.int32, (tokens, tokens), 1)).astype(F32).astype(BF16)
    top_k = 4
    for kind in range(2):
        taken = []
        for h in range(NG):
            ids = tabs[h, 8 * kind:8 * kind + top_k, :]
            gts = tabs[h, 8 * kind + top_k:8 * kind + 2 * top_k, :]
            for e in range(NE):
                eq = ids == (me * NE + e).astype(F32)
                taken.append(jnp.sum(jnp.where(eq, 1.0, 0.0), axis=0, keepdims=True))
                gates[kind, h, e:e + 1, :] = jnp.sum(jnp.where(eq, gts, 0.0), axis=0, keepdims=True)
        taken = jnp.concatenate(taken, axis=0)
        rank = dot(taken.astype(BF16), upper) - 1.0
        code = jnp.where(taken > 0.5, rank, -1.0)
        for h in range(NG):
            codes[kind, h, 0:NE, :] = code[h * NE:(h + 1) * NE, :]
            codes[kind, h, NE:8, :] = jnp.full((8 - NE, tokens), -1.0, F32)
    code_copy = pltpu.make_async_copy(codes.at[1], code_ref, lsem)

    def gather(kind, h, tok_rows):
        hits = slot_hits(codes[kind, h], tokens)
        gate_rows = gates[kind, h]
        onehot = jnp.concatenate([jnp.where(hit, 1.0, 0.0).astype(BF16) for hit in hits], axis=0)
        slot_gate = [jnp.sum(jnp.where(hits[e], gate_rows[e:e + 1, :], 0.0), axis=1, keepdims=True)
                     for e in range(NE)]
        return dot(onehot, tok_rows), slot_gate

    def q_copy(slot, h):
        return pltpu.make_async_copy(st.at[slot], q_ref.at[:, h], stsem.at[slot])

    def gather_dy(n, h, wait_slot):
        slot = n % 2
        if wait_slot:
            q_copy(slot, h).wait()
        rows, slot_gate = gather(1, h, buf[DY, h])
        for e in range(NE):
            st[slot, e] = (slot_gate[e] * rows[e * CAP:(e + 1) * CAP]).astype(BF16)
        q_copy(slot, h).start()

    def gather_xf(h):
        rows, slot_gate = gather(0, h, buf[XF, h])
        for e in range(NE):
            xs[e, h] = rows[e * CAP:(e + 1) * CAP].astype(BF16)
            gslot[e, h] = jnp.broadcast_to(slot_gate[e], (CAP, 128))

    own_dy.wait()
    code_copy.start()
    code_copy.wait()

    def pick(i, *choices):
        out = choices[-1]
        for k in range(len(choices) - 2, -1, -1):
            out = jnp.where(i == k, choices[k], out)
        return out

    def dy_pair(i, h, wait_slot):
        gather_dy(0, h, wait_slot)
        h2 = sib_of(h)
        arrived(DY, h2, 0)
        arrived(DY, h2, 1)
        gather_dy(1, h2, wait_slot)

    dy_pair(0, me, False)

    @pl.loop(0, 2)
    def _(i):
        dy_pair(0, xn + i * (yn - xn), True)

    diagonal(DY)
    dy_pair(0, dg, True)
    first_halves(XF)
    own_sends(XB)

    def xf_pair(h):
        gather_xf(h)
        h2 = sib_of(h)
        arrived(XF, h2, 0)
        arrived(XF, h2, 1)
        gather_xf(h2)

    xf_pair(me)
    second_halves(XF)

    @pl.loop(0, 2)
    def _(i):
        xf_pair(xn + i * (yn - xn))

    diagonal(XF)
    xf_pair(dg)

    chunk = 2
    rows_chunk = chunk * CAP

    def c_copy(slot, e, h0):
        return pltpu.make_async_copy(cst.at[slot], c_ref.at[pl.ds(h0, chunk), e], csem.at[slot])

    def ffn(e, first):
        for copy in weights(e):
            copy.wait()

        def body(i, wait_slot):
            slot = i % 2
            h0 = i * chunk
            rows = xs[e, pl.ds(h0, chunk)].reshape(rows_chunk, -1)
            pre = dot(rows, wbuf[e % 2, 0])
            act = pre * jax.nn.sigmoid(pre)
            hidden = (act * dot(rows, wbuf[e % 2, 1])).astype(BF16)
            out = dot(hidden, wbuf[e % 2, 2])
            gate = gslot[e, pl.ds(h0, chunk)].reshape(rows_chunk, 128)[:, 0:1]
            if wait_slot:
                c_copy(slot, e, h0).wait()
            cst[slot] = (gate * out).astype(BF16).reshape(chunk, CAP, -1)
            c_copy(slot, e, h0).start()

        if first:
            body(0, False)
            body(1, False)
            pl.loop(2, NG // chunk)(lambda i: body(i, True))
        else:
            pl.loop(0, NG // chunk)(lambda i: body(i, True))
        if e + 2 < NE:
            for copy in weights(e + 2):
                copy.start()

    ffn(0, True)
    first_halves(XB)
    ffn(1, False)
    ffn(2, False)
    second_halves(XB)
    ffn(3, False)
    diagonal(XB)
    for h in (sib, sib_of(xn), sib_of(yn), sib_of(dg)):
        arrived(XB, h, 0)
        arrived(XB, h, 1)
    for slot in range(2):
        c_copy(slot, NE - 1, 0).wait()
        q_copy(slot, 0).wait()
    for copy in sends:
        copy.wait_send()


def run_dispatch(x_acts, d_out, table, w_in, w_up, w_out):
    tokens, dim = x_acts.shape[2:]
    hid = w_in.shape[3]
    any_spec = pl.BlockSpec(memory_space=pl.ANY)
    flops = 2 * NG * NE * CAP * (2 * tokens * dim + 3 * dim * hid)
    return pl.pallas_call(
        dispatch_kernel,
        name='dispatch',
        out_shape=(jax.ShapeDtypeStruct((NG, NE, CAP, dim), BF16),
                   jax.ShapeDtypeStruct((NG, tokens, dim), BF16),
                   jax.ShapeDtypeStruct((NE, NG, CAP, dim), BF16),
                   jax.ShapeDtypeStruct((NG, 8, tokens), F32)),
        in_specs=[any_spec] * 6,
        out_specs=[any_spec] * 4,
        scratch_shapes=[
            pltpu.VMEM((2, NG, tokens, dim), BF16),
            pltpu.VMEM((NG, 16, tokens), F32),
            pltpu.VMEM((2, NG, 8, tokens), F32),
            pltpu.VMEM((2, NG, 8, tokens), F32),
            pltpu.VMEM((NE, NG, CAP, 128), F32),
            pltpu.VMEM((NE, NG, CAP, dim), BF16),
            pltpu.VMEM((2, NE, CAP, dim), BF16),
            pltpu.VMEM((2, 2, CAP, dim), BF16),
            pltpu.VMEM((2, 3, dim, hid), BF16),
            pltpu.SemaphoreType.DMA((4, 16)),
            pltpu.SemaphoreType.DMA((4, NG, 2)),
            pltpu.SemaphoreType.DMA,
            pltpu.SemaphoreType.DMA((2, 3)),
            pltpu.SemaphoreType.DMA((2,)),
            pltpu.SemaphoreType.DMA((2,)),
        ],
        cost_estimate=pl.CostEstimate(flops=flops, bytes_accessed=60_000_000, transcendentals=0),
        compiler_params=pltpu.CompilerParams(collective_id=0, has_side_effects=True,
                                             vmem_limit_bytes=67_043_328),
    )(x_acts, d_out, table, w_in, w_up, w_out)


def backward_kernel(code_ref, xb_ref, q_ref, win_ref, wup_ref, wout_ref,
                    dx_ref, dwin_ref, dwup_ref, dwout_ref,
                    xs, acc_in, acc_up, acc_out):
    step = pl.program_id(0)
    tokens, dim = xb_ref.shape[1:]

    @pl.when(step < NG)
    def _():
        hits = slot_hits(code_ref[0], tokens)
        onehot = jnp.concatenate([jnp.where(hit, 1.0, 0.0).astype(BF16) for hit in hits], axis=0)
        rows = dot(onehot, xb_ref[0]).astype(BF16)
        for e in range(NE):
            xs[e, step] = rows[e * CAP:(e + 1) * CAP]

    @pl.when(step >= NG)
    def _():
        e = step - NG
        chunk = 4
        rows_chunk = chunk * CAP

        def body(i):
            hs = pl.ds(i * chunk, chunk)
            x = xs[e, hs].reshape(rows_chunk, dim)
            q = q_ref[0, hs].reshape(rows_chunk, dim)
            pre_in = dot(x, win_ref[0, 0])
            pre_up = dot(x, wup_ref[0, 0])
            d_hid = dot(q, wout_ref[0, 0], ((1,), (1,)))
            sig = jax.nn.sigmoid(pre_in)
            act = pre_in * sig
            hidden = (act * pre_up).astype(BF16)
            d_in = (d_hid * pre_up * sig * (1.0 + pre_in * (1.0 - sig))).astype(BF16)
            d_up = (d_hid * act).astype(BF16)
            dx = dot(d_in, win_ref[0, 0], ((1,), (1,))) + dot(d_up, wup_ref[0, 0], ((1,), (1,)))
            dx_ref[hs, 0] = dx.astype(BF16).reshape(chunk, CAP, dim)
            return (dot(x, d_in, ((0,), (0,))), dot(x, d_up, ((0,), (0,))),
                    dot(hidden, q, ((0,), (0,))))

        steps = NG // chunk

        def loop(i, carry):
            parts = body(i)
            first = i == 0
            for acc, part in zip((acc_in, acc_up, acc_out), parts):
                acc[...] = jnp.where(first, part, acc[...] + part)
            return carry

        lax.fori_loop(0, steps, loop, 0)
        dwin_ref[0, 0] = acc_in[...].astype(BF16)
        dwup_ref[0, 0] = acc_up[...].astype(BF16)
        dwout_ref[0, 0] = acc_out[...].astype(BF16)


def run_backward(code, xb, q, w_in, w_up, w_out):
    tokens, dim = xb.shape[1:]
    hid = w_in.shape[3]
    exp = lambda i: jnp.maximum(i - NG, 0)
    src = lambda i: jnp.minimum(i, NG - 1)
    w_spec = lambda rows, cols: pl.BlockSpec((1, 1, rows, cols), lambda i: (0, exp(i), 0, 0))
    flops = 2 * NG * NE * CAP * (tokens * dim + 8 * dim * hid)
    return pl.pallas_call(
        backward_kernel,
        name='backward',
        grid=(NG + NE,),
        out_shape=(jax.ShapeDtypeStruct((NG, NE, CAP, dim), BF16),
                   jax.ShapeDtypeStruct(w_in.shape, BF16),
                   jax.ShapeDtypeStruct(w_up.shape, BF16),
                   jax.ShapeDtypeStruct(w_out.shape, BF16)),
        in_specs=[pl.BlockSpec((1, 8, tokens), lambda i: (src(i), 0, 0)),
                  pl.BlockSpec((1, tokens, dim), lambda i: (src(i), 0, 0)),
                  pl.BlockSpec((1, NG, CAP, dim), lambda i: (exp(i), 0, 0, 0)),
                  w_spec(dim, hid), w_spec(dim, hid), w_spec(hid, dim)],
        out_specs=[pl.BlockSpec((NG, 1, CAP, dim), lambda i: (0, exp(i), 0, 0)),
                   w_spec(dim, hid), w_spec(dim, hid), w_spec(hid, dim)],
        scratch_shapes=[pltpu.VMEM((NE, NG, CAP, dim), BF16),
                        pltpu.VMEM((dim, hid), F32), pltpu.VMEM((dim, hid), F32),
                        pltpu.VMEM((hid, dim), F32)],
        cost_estimate=pl.CostEstimate(flops=flops, bytes_accessed=60_000_000, transcendentals=0),
        compiler_params=pltpu.CompilerParams(dimension_semantics=('arbitrary',),
                                             vmem_limit_bytes=64_000_000),
    )(code, xb, q, w_in, w_up, w_out)


def token_codes(ids, num_experts):
    tokens, top_k = ids.shape
    experts = lax.broadcasted_iota(jnp.int32, (tokens, num_experts), 1)
    taken = jnp.zeros((tokens, num_experts), F32)
    for j in range(top_k):
        taken += jnp.where(ids[:, j:j + 1] == experts, 1.0, 0.0)
    lower = (lax.broadcasted_iota(jnp.int32, (tokens, tokens), 0)
             >= lax.broadcasted_iota(jnp.int32, (tokens, tokens), 1)).astype(F32).astype(BF16)
    rank = dot(lower, taken.astype(BF16)) - 1.0
    return jnp.where(taken > 0.5, rank, -10000.0)


def slot_matrix(code):
    tokens = code.shape[0]
    lane = lax.broadcasted_iota(jnp.int32, (tokens, 128), 1).astype(F32)
    blocks = []
    for b in range(NE * CAP // 128):
        hit = None
        for e in range(NE):
            if e * CAP < (b + 1) * 128 and (e + 1) * CAP > b * 128:
                eq = lane == code[:, e:e + 1] + float(e * CAP - b * 128)
                hit = eq if hit is None else hit | eq
        blocks.append(jnp.where(hit, 1.0, 0.0).astype(BF16))
    return jnp.concatenate(blocks, axis=1)


def combine_kernel(ids_ref, rows_ref, out_ref, acc, codes):
    step = pl.program_id(0)

    @pl.when(step == 0)
    def _():
        code = token_codes(ids_ref[...], NG * NE)
        for s in range(NG):
            codes[s] = code[:, s * NE:(s + 1) * NE]

    part = dot(slot_matrix(codes[step]), rows_ref[0])

    @pl.when(step == 0)
    def _():
        acc[...] = part

    @pl.when(step > 0)
    def _():
        acc[...] += part

    @pl.when(step == NG - 1)
    def _():
        out_ref[...] = acc[...].astype(BF16)


def run_combine(ids, rows):
    tokens, top_k = ids.shape
    dim = rows.shape[2]
    return pl.pallas_call(
        combine_kernel,
        name='combine',
        grid=(NG,),
        out_shape=jax.ShapeDtypeStruct((tokens, dim), BF16),
        in_specs=[pl.BlockSpec((tokens, top_k), lambda i: (0, 0)),
                  pl.BlockSpec((1, NE * CAP, dim), lambda i: (i, 0, 0))],
        out_specs=pl.BlockSpec((tokens, dim), lambda i: (0, 0)),
        scratch_shapes=[pltpu.VMEM((tokens, dim), F32), pltpu.VMEM((NG, tokens, NE), F32)],
        cost_estimate=pl.CostEstimate(flops=2 * tokens * NG * NE * CAP * dim,
                                      bytes_accessed=10_000_000, transcendentals=0),
        compiler_params=pltpu.CompilerParams(dimension_semantics=('arbitrary',),
                                             vmem_limit_bytes=48_000_000),
    )(ids, rows)


def solution(mesh):
    to_next = [(0, 1), (1, 0)]

    def device_fn(x_acts, expert_ids, gate_wts, w_in, w_up, w_out, d_out):
        dim = x_acts.shape[3]
        ids_t = jnp.swapaxes(expert_ids[:, 0], 1, 2).astype(F32)
        gates_t = jnp.swapaxes(gate_wts[:, 0], 1, 2)
        table = jnp.concatenate([ids_t[1], gates_t[1], ids_t[0], gates_t[0]], axis=0)
        ids_here = lax.ppermute(expert_ids[:, 0], 'stage', to_next)

        c_rows, xb, q_rows, code = run_dispatch(x_acts, d_out, table, w_in, w_up, w_out)

        def give_back(rows):
            return lax.all_to_all(rows.reshape(NG, NE * CAP, dim), 'expert', 0, 0, tiled=True)

        y_back = give_back(c_rows)
        dx_rows, dw_in, dw_up, dw_out = run_backward(code, xb, q_rows, w_in, w_up, w_out)
        dx_back = give_back(dx_rows)
        y_dev = run_combine(ids_here[1], y_back)
        dx_here = run_combine(ids_here[0], dx_back)
        dx_dev = lax.ppermute(dx_here, 'stage', to_next)
        return y_dev[None], dx_dev[None], dw_in, dw_up, dw_out

    tok_spec = P(None, 'stage', 'expert', None)
    w_spec = P('stage', 'expert', None, None)
    row_spec = P('stage', 'expert', None)
    return jax.shard_map(device_fn, mesh=mesh,
                         in_specs=(tok_spec, tok_spec, tok_spec, w_spec, w_spec, w_spec, row_spec),
                         out_specs=(row_spec, row_spec, w_spec, w_spec, w_spec), check_vma=False)
```

time: 578 us -> 434 us (0.75)
  Pallas kernels: 0 us -> 263 us
  matrix products: 244 us -> 0 us
  local copies, waits for them, and re-layouts: 112 us -> 2.25 us
  blocking collectives: 0 us -> 93.6 us
  waiting for transfers between devices: 124 us -> 59.9 us
  other arithmetic: 44.5 us -> 1.41 us
  starting transfers between devices: 42.9 us -> 8.33 us
    pallas_call x0 -> x4, Pallas kernels: none -> 263 us  [the longest x1 138 us: run_dispatch(): pl.pallas_call(dispatch_kernel, name='dispatch', out_shape=(jax.ShapeDtyp...]
    dot_general x15 -> x0, matrix products: 244 us -> none  [the longest x3 56 us: to_slots(): jnp.einsum('uec,ud->ecd', slot_hit, tok_rows, preferred_element_type=jnp....]
    all_to_all x0 -> x1, blocking collectives: none -> 93.6 us  [give_back(): lax.all_to_all(rows.reshape(NG, NE * CAP, dim), 'expert', 0, 0, tiled=True)]
    reshape x4 -> x0, local copies, waits for them, and re-layouts: 56.2 us -> none  [the longest x2 54.9 us: collect(): slot_buf.reshape((1, local_experts, group_size * capacity) + row_tail)]
    ppermute x7 -> x2, waiting for transfers between devices: 39.1 us -> 2.42 us  [the longest x1 2.42 us: device_fn(): ids_here = lax.ppermute(expert_ids[:, 0], 'stage', to_next)]
    all_to_all x6 -> x0, local copies, waits for them, and re-layouts: 30.9 us -> none  [the longest x2 15.8 us: collect(): received = lax.all_to_all(split_buf, 'expert', 2, 0, tiled=True)]
    all_to_all x7 -> x1, starting transfers between devices: 32.8 us -> 5.28 us  [give_back(): lax.all_to_all(rows.reshape(NG, NE * CAP, dim), 'expert', 0, 0, tiled=True)]
    all_to_all x7 -> x1, waiting for transfers between devices: 84.7 us -> 57.5 us  [give_back(): lax.all_to_all(rows.reshape(NG, NE * CAP, dim), 'expert', 0, 0, tiled=True)]
  transfers between devices with their start and end apart: 14 -> 3, of which waited for: 8 -> 2; matrix products, arithmetic and copies ran while one was open for 68% -> 0% of each run, Pallas kernels for 0% -> 12%
where the time goes in v1:
time: 434 us; the launch traced here: 430 us
  Pallas kernels  263 us (61%)
  blocking collectives  93.6 us (22%)
  waiting for transfers between devices  59.9 us (14%)
  starting transfers between devices  8.33 us (2%)
    pallas_call x1, Pallas kernels, run_dispatch(): pl.pallas_call(dispatch_kernel, name='dispatch', out_shape=(jax.ShapeDtyp...  138 us
    all_to_all x1, blocking collectives, give_back(): lax.all_to_all(rows.reshape(NG, NE * CAP, dim), 'expert', 0, 0, tiled=True)  93.6 us
    pallas_call x1, Pallas kernels, run_backward(): pl.pallas_call(backward_kernel, name='backward', grid=(NG + NE,), out_sha...  73.8 us
    all_to_all x1, waiting for transfers between devices, give_back(): lax.all_to_all(rows.reshape(NG, NE * CAP, dim), 'expert', 0, 0, tiled=True)  57.5 us
    pallas_call x2, Pallas kernels, run_combine(): pl.pallas_call(combine_kernel, name='combine', grid=(NG,), out_shape=jax....  50.9 us
  transfers between devices with their start and end apart: 3, of which 2 were waited for; matrix products, arithmetic and copies ran while one was open for 0% of the time, Pallas kernels for 12%

profile of v1, /device:TPU:0, one launch (start us, length us, event | category | flops | bytes accessed | tf_op | source)
XLA Modules:
  0.0 429.6 jit_solution(11142700599644332867)
XLA Ops:
  0.6 0.8 convert_bitcast_fusion
  1.4 0.7 slice_bitcast_fusion.2
  2.1 0.6 pad_maximum_fusion.tab_ref
  2.8 138.3 %dispatch.1 = (bf16[8,4,192,640]{3,2,1,0:T(8,128)(2,1)}, bf16[8,1024,640]{2,1,0:T(8,128)(2,1)}, bf16[4,8,192,640]{3,2,1,0:T(8,128)(2,1)}, f32[8,8,1024]{2,1,0:T(8,128)}) custom-call(bf16[2,1,1024,640]{3,2,1,0:T(8,128)(2,1)} %x_ref.1, bf16[1,1024,640]{2,1,0:T(8,128)(2,1)} %dy_ref.1, f32[16,1024]{1,0:T(8,128)} %pad_maximum_fusion.tab_ref, ...), custom_call_target="tpu_custom_call" | custom-call | flops 31205621760 | bytes 60000000 | tf_op jit(solution)/shard_map/dispatch/pallas_call | solution.py:286
  141.2 73.8 %backward.1 = (bf16[8,4,192,640]{3,2,1,0:T(8,128)(2,1)}, bf16[1,4,640,640]{3,2,1,0:T(8,128)(2,1)}, bf16[1,4,640,640]{3,2,1,0:T(8,128)(2,1)}, bf16[1,4,640,640]{3,2,1,0:T(8,128)(2,1)}) custom-call(f32[8,8,1024]{2,1,0:T(8,128)} %get-tuple-element.14.code_ref, bf16[8,1024,640]{2,1,0:T(8,128)(2,1)} %get-tuple-element.15.xb_ref, ...), custom_call_target="tpu_custom_call" | custom-call | flops 48318382080 | bytes 60000000 | tf_op jit(solution)/shard_map/backward/pallas_call | solution.py:377
  215.0 93.6 %all_to_all.10.rows_ref = bf16[8,768,640]{2,1,0:T(8,128)(2,1)} all-to-all(bf16[8,768,640]{2,1,0:T(8,128)(2,1)} %bitcast.24), channel_id=1, replica_groups=mesh['stage'=2,'expert'=8] {'expert'}, dimensions={0} | all-to-all | bytes 15728640 | tf_op jit(solution)/shard_map/all_to_all | solution.py:482
  308.6 0.0 copy-start
  308.6 5.3 %all-to-all-start = ((bf16[8,768,640]{2,1,0:T(8,128)(2,1)}), bf16[8,768,640]{2,1,0:T(8,128)(2,1)}, u32[]{:S(2)}, u32[]{:S(2)}) async-start(bf16[8,768,640]{2,1,0:T(8,128)(2,1)} %bitcast.23), calls=%async_computation | async-start | bytes 15728640 | tf_op jit(solution)/shard_map/all_to_all | solution.py:482
  313.9 0.0 copy-done
  313.9 1.5 collective-permute-start
  315.4 2.4 collective-permute-done
  317.9 0.2 copy.18
  318.1 24.9 %combine.3 = bf16[1024,640]{1,0:T(8,128)(2,1)S(1)} custom-call(s32[1024,4]{1,0:T(8,128)S(1)} %bitcast.22, bf16[8,768,640]{2,1,0:T(8,128)(2,1)} %all_to_all.10.rows_ref), custom_call_target="tpu_custom_call" | custom-call | flops 8053063680 | bytes 10000000 | tf_op jit(solution)/shard_map/combine/pallas_call | solution.py:453
  343.0 1.5 collective-permute-start.1
  344.5 0.2 copy.17
  344.8 57.5 %all-to-all-done.rows_ref = bf16[8,768,640]{2,1,0:T(8,128)(2,1)} async-done(((bf16[8,768,640]{2,1,0:T(8,128)(2,1)}), bf16[8,768,640]{2,1,0:T(8,128)(2,1)}, u32[]{:S(2)}, u32[]{:S(2)}) %all-to-all-start) | async-done | bytes 7864352 | tf_op jit(solution)/shard_map/all_to_all | solution.py:482
  402.3 26.0 %combine.2 = bf16[1024,640]{1,0:T(8,128)(2,1)} custom-call(s32[1024,4]{1,0:T(8,128)S(1)} %bitcast.21, bf16[8,768,640]{2,1,0:T(8,128)(2,1)} %all-to-all-done.rows_ref), custom_call_target="tpu_custom_call" | custom-call | flops 8053063680 | bytes 10000000 | tf_op jit(solution)/shard_map/combine/pallas_call | solution.py:453
  428.2 0.0 collective-permute-done.1
  428.2 1.1 copy.20
  (2 shorter events, 0.0 us)
Async XLA Ops:
  308.6 5.3 %copy-start = (s32[2,1,1024,4]{2,3,1,0:T(4,128)S(1)}, s32[2,1,1024,4]{2,3,1,0:T(4,128)}, u32[]{:S(2)}) copy-start(s32[2,1,1024,4]{2,3,1,0:T(4,128)} %param.8) | copy-start | bytes 98308
  308.6 93.7 %all-to-all-start = ((bf16[8,768,640]{2,1,0:T(8,128)(2,1)}), bf16[8,768,640]{2,1,0:T(8,128)(2,1)}, u32[]{:S(2)}, u32[]{:S(2)}) async-start(bf16[8,768,640]{2,1,0:T(8,128)(2,1)} %bitcast.23), calls=%async_computation | async-start | bytes 15728640 | tf_op jit(solution)/shard_map/all_to_all | solution.py:482
  313.9 4.0 collective-permute-start
  343.0 85.2 %collective-permute-start.1 = (bf16[1024,640]{1,0:T(8,128)(2,1)S(1)}, bf16[1024,640]{1,0:T(8,128)(2,1)S(1)}, u32[]{:S(2)}, u32[]{:S(2)}) collective-permute-start(bf16[1024,640]{1,0:T(8,128)(2,1)S(1)} %combine.3), channel_id=1, source_target_pairs={{0,8},{8,0},{1,9},{9,1},{2,10},{10,2},{3,11},{11,3},{4,12},{12,4},... | collective-permute-start | bytes 3932168 | tf_op jit(solution)/shard_map/ppermute | solution.py:489

commit v2 on v1

--- a/solution.py
+++ b/solution.py
@@ -1,5 +1,3 @@
-import functools
-
 import jax
 import jax.numpy as jnp
 from jax import lax
@@ -23,9 +21,9 @@
 
 
 def dispatch_kernel(x_ref, dy_ref, tab_ref, win_ref, wup_ref, wout_ref,
-                    c_ref, xb_ref, q_ref, code_ref,
+                    c_ref, xb_ref, q_ref, code_ref, tab_out,
                     buf, tabs, codes, gates, gslot, xs, st, cst, wbuf,
-                    ssem, rsem, lsem, wsem, stsem, csem):
+                    ssem, rsem, lsem, wsem, stsem, csem, tsem):
     stage = lax.axis_index('stage')
     me = lax.axis_index('expert')
     other = 1 - stage
@@ -135,6 +133,11 @@
     send(TAB, dg, 0, 12, to_sib)
     for h in (sib, sib_of(xn), sib_of(yn), sib_of(dg)):
         arrived(TAB, h, 0)
+    core = me % 2
+    tab_copies = [pltpu.make_async_copy(tabs.at[h], tab_out.at[k], tsem.at[k])
+                  for k, h in enumerate((me, yn + core * (xn - yn)))]
+    for copy in tab_copies:
+        copy.start()
 
     upper = (lax.broadcasted_iota(jnp.int32, (tokens, tokens), 0)
              <= lax.broadcasted_iota(jnp.int32, (tokens, tokens), 1)).astype(F32).astype(BF16)
@@ -274,6 +277,8 @@
     for slot in range(2):
         c_copy(slot, NE - 1, 0).wait()
         q_copy(slot, 0).wait()
+    for copy in tab_copies:
+        copy.wait()
     for copy in sends:
         copy.wait_send()
 
@@ -289,9 +294,10 @@
         out_shape=(jax.ShapeDtypeStruct((NG, NE, CAP, dim), BF16),
                    jax.ShapeDtypeStruct((NG, tokens, dim), BF16),
                    jax.ShapeDtypeStruct((NE, NG, CAP, dim), BF16),
-                   jax.ShapeDtypeStruct((NG, 8, tokens), F32)),
+                   jax.ShapeDtypeStruct((NG, 8, tokens), F32),
+                   jax.ShapeDtypeStruct((2, 16, tokens), F32)),
         in_specs=[any_spec] * 6,
-        out_specs=[any_spec] * 4,
+        out_specs=[any_spec] * 5,
         scratch_shapes=[
             pltpu.VMEM((2, NG, tokens, dim), BF16),
             pltpu.VMEM((NG, 16, tokens), F32),
@@ -308,6 +314,7 @@
             pltpu.SemaphoreType.DMA((2, 3)),
             pltpu.SemaphoreType.DMA((2,)),
             pltpu.SemaphoreType.DMA((2,)),
+            pltpu.SemaphoreType.DMA((2,)),
         ],
         cost_estimate=pl.CostEstimate(flops=flops, bytes_accessed=60_000_000, transcendentals=0),
         compiler_params=pltpu.CompilerParams(collective_id=0, has_side_effects=True,
@@ -315,11 +322,34 @@
     )(x_acts, d_out, table, w_in, w_up, w_out)
 
 
-def backward_kernel(code_ref, xb_ref, q_ref, win_ref, wup_ref, wout_ref,
-                    dx_ref, dwin_ref, dwup_ref, dwout_ref,
-                    xs, acc_in, acc_up, acc_out):
+def backward_kernel(code_ref, xb_ref, q_ref, win_ref, wup_ref, wout_ref, c_ref,
+                    dx_ref, dwin_ref, dwup_ref, dwout_ref, back_ref,
+                    xs, acc_in, acc_up, acc_out, ssem, rsem):
     step = pl.program_id(0)
     tokens, dim = xb_ref.shape[1:]
+    stage = lax.axis_index('stage')
+    me = lax.axis_index('expert')
+
+    def give(k):
+        peer = (me + k) % NG
+        return pltpu.make_async_remote_copy(
+            src_ref=c_ref.at[peer], dst_ref=back_ref.at[me], send_sem=ssem.at[k], recv_sem=rsem.at[me],
+            device_id=(stage, peer), device_id_type=MESH)
+
+    def take(k):
+        peer = (me + k) % NG
+        return pltpu.make_async_remote_copy(
+            src_ref=c_ref.at[peer], dst_ref=back_ref.at[peer], send_sem=ssem.at[k],
+            recv_sem=rsem.at[peer], device_id=(stage, peer), device_id_type=MESH)
+
+    @pl.when(step == 0)
+    def _():
+        barrier = pltpu.get_barrier_semaphore()
+        for k in range(1, NG):
+            pl.semaphore_signal(barrier, inc=1, device_id=(stage, (me + k) % NG), device_id_type=MESH)
+        pl.semaphore_wait(barrier, NG - 1)
+        for k in range(1, NG):
+            give(k).start()
 
     @pl.when(step < NG)
     def _():
@@ -366,8 +396,15 @@
         dwup_ref[0, 0] = acc_up[...].astype(BF16)
         dwout_ref[0, 0] = acc_out[...].astype(BF16)
 
-
-def run_backward(code, xb, q, w_in, w_up, w_out):
+    @pl.when(step == NG + NE - 1)
+    def _():
+        for k in range(1, NG):
+            take(k).wait_recv()
+        for k in range(1, NG):
+            give(k).wait_send()
+
+
+def run_backward(code, xb, q, w_in, w_up, w_out, c_rows):
     tokens, dim = xb.shape[1:]
     hid = w_in.shape[3]
     exp = lambda i: jnp.maximum(i - NG, 0)
@@ -381,25 +418,30 @@
         out_shape=(jax.ShapeDtypeStruct((NG, NE, CAP, dim), BF16),
                    jax.ShapeDtypeStruct(w_in.shape, BF16),
                    jax.ShapeDtypeStruct(w_up.shape, BF16),
-                   jax.ShapeDtypeStruct(w_out.shape, BF16)),
+                   jax.ShapeDtypeStruct(w_out.shape, BF16),
+                   jax.ShapeDtypeStruct((NG, NE, CAP, dim), BF16)),
         in_specs=[pl.BlockSpec((1, 8, tokens), lambda i: (src(i), 0, 0)),
                   pl.BlockSpec((1, tokens, dim), lambda i: (src(i), 0, 0)),
                   pl.BlockSpec((1, NG, CAP, dim), lambda i: (exp(i), 0, 0, 0)),
-                  w_spec(dim, hid), w_spec(dim, hid), w_spec(hid, dim)],
+                  w_spec(dim, hid), w_spec(dim, hid), w_spec(hid, dim),
+                  pl.BlockSpec(memory_space=pl.ANY)],
         out_specs=[pl.BlockSpec((NG, 1, CAP, dim), lambda i: (0, exp(i), 0, 0)),
-                   w_spec(dim, hid), w_spec(dim, hid), w_spec(hid, dim)],
+                   w_spec(dim, hid), w_spec(dim, hid), w_spec(hid, dim),
+                   pl.BlockSpec(memory_space=pl.ANY)],
         scratch_shapes=[pltpu.VMEM((NE, NG, CAP, dim), BF16),
                         pltpu.VMEM((dim, hid), F32), pltpu.VMEM((dim, hid), F32),
-                        pltpu.VMEM((hid, dim), F32)],
+                        pltpu.VMEM((hid, dim), F32),
+                        pltpu.SemaphoreType.DMA((NG,)), pltpu.SemaphoreType.DMA((NG,))],
         cost_estimate=pl.CostEstimate(flops=flops, bytes_accessed=60_000_000, transcendentals=0),
-        compiler_params=pltpu.CompilerParams(dimension_semantics=('arbitrary',),
-                                             vmem_limit_bytes=64_000_000),
-    )(code, xb, q, w_in, w_up, w_out)
-
-
-def token_codes(ids, num_experts):
+        compiler_params=pltpu.CompilerParams(dimension_semantics=('arbitrary',), collective_id=1,
+                                             has_side_effects=True, vmem_limit_bytes=64_000_000),
+    )(code, xb, q, w_in, w_up, w_out, c_rows)
+
+
+def token_codes(ids):
     tokens, top_k = ids.shape
-    experts = lax.broadcasted_iota(jnp.int32, (tokens, num_experts), 1)
+    num_experts = NG * NE
+    experts = lax.broadcasted_iota(jnp.int32, (tokens, num_experts), 1).astype(F32)
     taken = jnp.zeros((tokens, num_experts), F32)
     for j in range(top_k):
         taken += jnp.where(ids[:, j:j + 1] == experts, 1.0, 0.0)
@@ -423,70 +465,171 @@
     return jnp.concatenate(blocks, axis=1)
 
 
-def combine_kernel(ids_ref, rows_ref, out_ref, acc, codes):
-    step = pl.program_id(0)
-
-    @pl.when(step == 0)
-    def _():
-        code = token_codes(ids_ref[...], NG * NE)
+def collect_kernel(tab_ref, c_ref, back_ref, rows_ref,
+                   y_ref, dx_ref,
+                   codes, ybuf, rbuf, acc, part_out, part_in, out_buf,
+                   ysem, osem, ssem, rsem, psem, prsem, zsem, zrsem):
+    stage = lax.axis_index('stage')
+    me = lax.axis_index('expert')
+    core = me % 2
+    sib_of = lambda h: h + 1 - 2 * (h % 2)
+    sib = sib_of(me)
+    xn = me + 2 - 4 * ((me // 2) % 2)
+    yn = me + 4 - 8 * (me // 4)
+    dg = xn + 4 - 8 * (xn // 4)
+    partner = yn + core * (xn - yn)
+    line = xn + core * (yn - xn)
+    line0 = 2 * (line // 2)
+    tokens, dim = acc.shape
+    chunks = part_out.shape[0]
+    tchunk = tokens // chunks
+
+    barrier = pltpu.get_barrier_semaphore()
+    for peer in ((1 - stage, me), (stage, sib), (stage, xn), (stage, yn), (stage, sib_of(xn)),
+                 (stage, sib_of(yn))):
+        pl.semaphore_signal(barrier, inc=1, device_id=peer, device_id_type=MESH)
+    pl.semaphore_wait(barrier, 6)
+
+    targets = ((2 * (xn // 2), 2 * (dg // 2), 1 + core), (2 * (yn // 2) + 1, 2 * (dg // 2) + 1, 1 + core),
+               (sib, sib_of(xn) + core * (sib_of(yn) - sib_of(xn)), 0))
+    sends = []
+    for role in range(2):
+        for k, (target, via, slot) in enumerate(targets):
+            sends.append(pltpu.make_async_remote_copy(
+                src_ref=rows_ref.at[via if role == 0 else target], dst_ref=rbuf.at[role, slot],
+                send_sem=ssem.at[role, k], recv_sem=rsem.at[role, slot],
+                device_id=(stage, target), device_id_type=MESH))
+            sends[-1].start()
+    own = [pltpu.make_async_copy(rows_ref.at[h], rbuf.at[role, 3], osem.at[role])
+           for role, h in enumerate((partner, me))]
+    for copy in own:
+        copy.start()
+
+    def arrived(role, slot):
+        pltpu.make_async_remote_copy(
+            src_ref=rows_ref.at[me], dst_ref=rbuf.at[role, slot], send_sem=ssem.at[role, 0],
+            recv_sem=rsem.at[role, slot], device_id=(stage, sib), device_id_type=MESH).wait_recv()
+
+    def y_fetch(k):
+        src = c_ref if k == 0 else back_ref
+        return pltpu.make_async_copy(src.at[(me + k) % NG], ybuf.at[k % 2], ysem.at[k % 2])
+
+    y_fetch(0).start()
+
+    for n, (row, kind) in enumerate(((0, 0), (1, 1), (0, 1))):
+        code = token_codes(tab_ref[row].T[:, 8 * kind:8 * kind + 4])
         for s in range(NG):
-            codes[s] = code[:, s * NE:(s + 1) * NE]
-
-    part = dot(slot_matrix(codes[step]), rows_ref[0])
-
-    @pl.when(step == 0)
-    def _():
-        acc[...] = part
-
-    @pl.when(step > 0)
-    def _():
-        acc[...] += part
-
-    @pl.when(step == NG - 1)
-    def _():
-        out_ref[...] = acc[...].astype(BF16)
-
-
-def run_combine(ids, rows):
-    tokens, top_k = ids.shape
-    dim = rows.shape[2]
+            codes[n, s] = code[:, s * NE:(s + 1) * NE]
+
+    def rows_of(ref):
+        return ref.reshape(NE * CAP, dim)
+
+    def y_part(k):
+        if k + 1 < NG:
+            y_fetch(k + 1).start()
+        y_fetch(k).wait()
+        part = dot(slot_matrix(codes[0, (me + k) % NG]), rows_of(ybuf[k % 2]))
+        acc[...] = part if k == 0 else acc[...] + part
+
+    sources = (sib, line0, line0 + 1, me)
+
+    def partial_copy(i):
+        return pltpu.make_async_remote_copy(
+            src_ref=part_out.at[i], dst_ref=part_in.at[i], send_sem=psem.at[i], recv_sem=prsem.at[i],
+            device_id=(stage, partner), device_id_type=MESH)
+
+    def z_copy(i):
+        return pltpu.make_async_remote_copy(
+            src_ref=out_buf.at[i], dst_ref=dx_ref.at[pl.ds(i * tchunk, tchunk)], send_sem=zsem.at[i],
+            recv_sem=zrsem.at[i], device_id=(1 - stage, me), device_id_type=MESH)
+
+    for k in range(0, 4):
+        y_part(k)
+    for slot in range(3):
+        arrived(0, slot)
+    own[0].wait()
+
+    @pl.loop(0, chunks)
+    def _(i):
+        toks = pl.ds(i * tchunk, tchunk)
+        total = None
+        for slot, d in enumerate(sources):
+            part = dot(slot_matrix(codes[1, d, toks]), rows_of(rbuf[0, slot]))
+            total = part if total is None else total + part
+        part_out[i] = total
+        partial_copy(i).start()
+
+    for k in range(4, NG):
+        y_part(k)
+    out_buf[...] = acc[...].astype(BF16).reshape(out_buf.shape)
+    y_out = [pltpu.make_async_copy(out_buf.at[i], y_ref.at[pl.ds(i * tchunk, tchunk)], zsem.at[i])
+             for i in range(chunks)]
+    for copy in y_out:
+        copy.start()
+    for slot in range(3):
+        arrived(1, slot)
+    own[1].wait()
+    for slot, d in enumerate(sources):
+        part = dot(slot_matrix(codes[2, d]), rows_of(rbuf[1, slot]))
+        acc[...] = part if slot == 0 else acc[...] + part
+    for copy in y_out:
+        copy.wait()
+
+    for i in range(chunks):
+        partial_copy(i).wait_recv()
+        out_buf[i] = (acc[i * tchunk:(i + 1) * tchunk] + part_in[i]).astype(BF16)
+        z_copy(i).start()
+    for copy in sends:
+        copy.wait_send()
+    for i in range(chunks):
+        partial_copy(i).wait_send()
+        z_copy(i).wait()
+
+
+def run_collect(tables, c_rows, y_back, dx_rows):
+    tokens = tables.shape[2]
+    dim = c_rows.shape[3]
+    chunks = 4
+    any_spec = pl.BlockSpec(memory_space=pl.ANY)
     return pl.pallas_call(
-        combine_kernel,
-        name='combine',
-        grid=(NG,),
-        out_shape=jax.ShapeDtypeStruct((tokens, dim), BF16),
-        in_specs=[pl.BlockSpec((tokens, top_k), lambda i: (0, 0)),
-                  pl.BlockSpec((1, NE * CAP, dim), lambda i: (i, 0, 0))],
-        out_specs=pl.BlockSpec((tokens, dim), lambda i: (0, 0)),
-        scratch_shapes=[pltpu.VMEM((tokens, dim), F32), pltpu.VMEM((NG, tokens, NE), F32)],
-        cost_estimate=pl.CostEstimate(flops=2 * tokens * NG * NE * CAP * dim,
-                                      bytes_accessed=10_000_000, transcendentals=0),
-        compiler_params=pltpu.CompilerParams(dimension_semantics=('arbitrary',),
-                                             vmem_limit_bytes=48_000_000),
-    )(ids, rows)
+        collect_kernel,
+        name='collect',
+        out_shape=(jax.ShapeDtypeStruct((tokens, dim), BF16), jax.ShapeDtypeStruct((tokens, dim), BF16)),
+        in_specs=[pl.BlockSpec(memory_space=pltpu.VMEM)] + [any_spec] * 3,
+        out_specs=[any_spec] * 2,
+        scratch_shapes=[
+            pltpu.VMEM((3, NG, tokens, NE), F32),
+            pltpu.VMEM((2, NE, CAP, dim), BF16),
+            pltpu.VMEM((2, 4, NE, CAP, dim), BF16),
+            pltpu.VMEM((tokens, dim), F32),
+            pltpu.VMEM((chunks, tokens // chunks, dim), F32),
+            pltpu.VMEM((chunks, tokens // chunks, dim), F32),
+            pltpu.VMEM((chunks, tokens // chunks, dim), BF16),
+            pltpu.SemaphoreType.DMA((2,)),
+            pltpu.SemaphoreType.DMA((2,)),
+            pltpu.SemaphoreType.DMA((2, 3)),
+            pltpu.SemaphoreType.DMA((2, 3)),
+            pltpu.SemaphoreType.DMA((chunks,)),
+            pltpu.SemaphoreType.DMA((chunks,)),
+            pltpu.SemaphoreType.DMA((chunks,)),
+            pltpu.SemaphoreType.DMA((chunks,)),
+        ],
+        cost_estimate=pl.CostEstimate(flops=4 * tokens * NG * NE * CAP * dim,
+                                      bytes_accessed=20_000_000, transcendentals=0),
+        compiler_params=pltpu.CompilerParams(collective_id=2, has_side_effects=True,
+                                             vmem_limit_bytes=64_000_000),
+    )(tables, c_rows, y_back, dx_rows)
 
 
 def solution(mesh):
-    to_next = [(0, 1), (1, 0)]
-
     def device_fn(x_acts, expert_ids, gate_wts, w_in, w_up, w_out, d_out):
-        dim = x_acts.shape[3]
         ids_t = jnp.swapaxes(expert_ids[:, 0], 1, 2).astype(F32)
         gates_t = jnp.swapaxes(gate_wts[:, 0], 1, 2)
         table = jnp.concatenate([ids_t[1], gates_t[1], ids_t[0], gates_t[0]], axis=0)
-        ids_here = lax.ppermute(expert_ids[:, 0], 'stage', to_next)
-
-        c_rows, xb, q_rows, code = run_dispatch(x_acts, d_out, table, w_in, w_up, w_out)
-
-        def give_back(rows):
-            return lax.all_to_all(rows.reshape(NG, NE * CAP, dim), 'expert', 0, 0, tiled=True)
-
-        y_back = give_back(c_rows)
-        dx_rows, dw_in, dw_up, dw_out = run_backward(code, xb, q_rows, w_in, w_up, w_out)
-        dx_back = give_back(dx_rows)
-        y_dev = run_combine(ids_here[1], y_back)
-        dx_here = run_combine(ids_here[0], dx_back)
-        dx_dev = lax.ppermute(dx_here, 'stage', to_next)
+
+        c_rows, xb, q_rows, code, tables = run_dispatch(x_acts, d_out, table, w_in, w_up, w_out)
+        dx_rows, dw_in, dw_up, dw_out, y_back = run_backward(code, xb, q_rows, w_in, w_up, w_out, c_rows)
+        y_dev, dx_dev = run_collect(tables, c_rows, y_back, dx_rows)
         return y_dev[None], dx_dev[None], dw_in, dw_up, dw_out
 
     tok_spec = P(None, 'stage', 'expert', None)

time: 434 us -> 340 us (0.78)
  blocking collectives: 93.6 us -> 0 us
  waiting for transfers between devices: 59.9 us -> 0 us
  Pallas kernels: 263 us -> 320 us
  local copies, waits for them, and re-layouts: 2.25 us -> 13.8 us
  starting transfers between devices: 8.33 us -> 0 us
    all_to_all x1 -> x0, blocking collectives: 93.6 us -> none  [give_back(): lax.all_to_all(rows.reshape(NG, NE * CAP, dim), 'expert', 0, 0, tiled=True)]
    all_to_all x1 -> x0, waiting for transfers between devices: 57.5 us -> none  [give_back(): lax.all_to_all(rows.reshape(NG, NE * CAP, dim), 'expert', 0, 0, tiled=True)]
    pallas_call x2 -> x1, Pallas kernels: 50.9 us -> 89.8 us  [run_collect(): pl.pallas_call(collect_kernel, name='collect', out_shape=(jax.ShapeDtypeS...]
    pallas_call x1, Pallas kernels: 73.8 us -> 92 us  [run_backward(): pl.pallas_call(backward_kernel, name='backward', grid=(NG + NE,), out_sha...]
    unnamed x5 -> x11, local copies, waits for them, and re-layouts: 1.5 us -> 13 us
    all_to_all x1 -> x0, starting transfers between devices: 5.28 us -> none  [give_back(): lax.all_to_all(rows.reshape(NG, NE * CAP, dim), 'expert', 0, 0, tiled=True)]
  transfers between devices with their start and end apart: 3 -> 0, of which waited for: 2 -> 0; matrix products, arithmetic and copies ran while one was open for 0% -> 0% of each run, Pallas kernels for 12% -> 0%
where the time goes in v2:
time: 340 us; the launch traced here: 336 us
  Pallas kernels  320 us (94%)
  local copies, waits for them, and re-layouts  13.8 us (4%)
    pallas_call x1, Pallas kernels, run_dispatch(): pl.pallas_call(dispatch_kernel, name='dispatch', out_shape=(jax.ShapeDtyp...  138 us
    pallas_call x1, Pallas kernels, run_backward(): pl.pallas_call(backward_kernel, name='backward', grid=(NG + NE,), out_sha...  92 us
    pallas_call x1, Pallas kernels, run_collect(): pl.pallas_call(collect_kernel, name='collect', out_shape=(jax.ShapeDtypeS...  89.8 us
    unnamed x11, local copies, waits for them, and re-layouts  13 us

profile of v2, /device:TPU:0, one launch (start us, length us, event | category | flops | bytes accessed | tf_op | source)
XLA Modules:
  0.0 336.2 jit_solution(16056874082008542986)
XLA Ops:
  0.6 0.8 fusion
  1.4 0.7 slice_bitcast_fusion.2
  2.1 0.6 pad_maximum_fusion.tab_ref
  2.8 138.4 %dispatch.1 = (bf16[8,4,192,640]{3,2,1,0:T(8,128)(2,1)}, bf16[8,1024,640]{2,1,0:T(8,128)(2,1)}, bf16[4,8,192,640]{3,2,1,0:T(8,128)(2,1)}, f32[8,8,1024]{2,1,0:T(8,128)}, f32[2,16,1024]{2,1,0:T(8,128)}) custom-call(bf16[2,1,1024,640]{3,2,1,0:T(8,128)(2,1)} %x_ref.1, bf16[1,1024,640]{2,1,0:T(8,128)(2,1)} %dy_ref.1, f32[16,1024]{1,0:T(8,128)} %pad_maximum_fusion.tab_ref, ...), custom_call_target="tpu_custom_call" | custom-call | flops 31205621760 | bytes 60000000 | tf_op jit(solution)/shard_map/dispatch/pallas_call | solution.py:291
  141.2 92.0 %backward.1 = (bf16[8,4,192,640]{3,2,1,0:T(8,128)(2,1)}, bf16[1,4,640,640]{3,2,1,0:T(8,128)(2,1)}, bf16[1,4,640,640]{3,2,1,0:T(8,128)(2,1)}, bf16[1,4,640,640]{3,2,1,0:T(8,128)(2,1)}, bf16[8,4,192,640]{3,2,1,0:T(8,128)(2,1)}) custom-call(f32[8,8,1024]{2,1,0:T(8,128)} %get-tuple-element.19.code_ref, bf16[8,1024,640]{2,1,0:T(8,128)(2,1)} %get-tuple-element.20.xb_ref, ...), custom_call_target="tpu_custom_call" | custom-call | flops 48318382080 | bytes 60000000 | tf_op jit(solution)/shard_map/backward/pallas_call | solution.py:414
  233.1 89.8 %collect.1 = (bf16[1024,640]{1,0:T(8,128)(2,1)}, bf16[1024,640]{1,0:T(8,128)(2,1)}) custom-call(f32[2,16,1024]{2,1,0:T(8,128)} %get-tuple-element.17.tab_ref, bf16[8,4,192,640]{3,2,1,0:T(8,128)(2,1)} %get-tuple-element.18.c_ref, bf16[8,4,192,640]{3,2,1,0:T(8,128)(2,1)} %get-tuple-element.22.back_ref, bf16[8,4,192,640]{3,2,1,0:T(8,128)(2,1)} %get-tuple-element.23.rows_ref), custom_call_target="tpu_custom_call" | custom-call | flops 16106127360 | bytes 20000000 | tf_op jit(solution)/shard_map/collect/pallas_call | solution.py:594
  322.9 0.0 copy-start.2
  322.9 2.6 copy.18
  325.5 2.5 copy.19
  328.0 0.0 copy-done.2
  328.0 0.0 copy-start.1
  328.0 1.7 copy.20
  329.7 1.4 copy-done.1
  331.1 0.0 copy-start
  331.1 1.7 copy.21
  332.9 1.4 copy-done
  334.3 1.7 copy.22
Async XLA Ops:
  322.9 5.1 %copy-start.2 = (bf16[1,4,640,640]{3,2,1,0:T(8,128)(2,1)S(1)}, bf16[1,4,640,640]{3,2,1,0:T(8,128)(2,1)}, u32[]{:S(2)}) copy-start(bf16[1,4,640,640]{3,2,1,0:T(8,128)(2,1)} %get-tuple-element.42) | copy-start | bytes 9830404
  328.0 3.1 copy-start.1
  331.1 3.1 copy-start

commit v3 on v2

--- a/solution.py
+++ b/solution.py
@@ -21,9 +21,9 @@
 
 
 def dispatch_kernel(x_ref, dy_ref, tab_ref, win_ref, wup_ref, wout_ref,
-                    c_ref, xb_ref, q_ref, code_ref, tab_out,
+                    c_ref, xb_ref, q_ref, code_ref, tok_ref,
                     buf, tabs, codes, gates, gslot, xs, st, cst, wbuf,
-                    ssem, rsem, lsem, wsem, stsem, csem, tsem):
+                    ssem, rsem, lsem, wsem, stsem, csem, tsem, tok):
     stage = lax.axis_index('stage')
     me = lax.axis_index('expert')
     other = 1 - stage
@@ -133,12 +133,6 @@
     send(TAB, dg, 0, 12, to_sib)
     for h in (sib, sib_of(xn), sib_of(yn), sib_of(dg)):
         arrived(TAB, h, 0)
-    core = me % 2
-    tab_copies = [pltpu.make_async_copy(tabs.at[h], tab_out.at[k], tsem.at[k])
-                  for k, h in enumerate((me, yn + core * (xn - yn)))]
-    for copy in tab_copies:
-        copy.start()
-
     upper = (lax.broadcasted_iota(jnp.int32, (tokens, tokens), 0)
              <= lax.broadcasted_iota(jnp.int32, (tokens, tokens), 1)).astype(F32).astype(BF16)
     top_k = 4
@@ -202,6 +196,15 @@
         arrived(DY, h2, 1)
         gather_dy(1, h2, wait_slot)
 
+    core = me % 2
+    partner = yn + core * (xn - yn)
+    lower = (lax.broadcasted_iota(jnp.int32, (tokens, tokens), 0)
+             >= lax.broadcasted_iota(jnp.int32, (tokens, tokens), 1)).astype(F32).astype(BF16)
+    for n, (h, kind) in enumerate(((me, 0), (partner, 1), (me, 1))):
+        tok[n] = token_codes(tabs[h].T[:, 8 * kind:8 * kind + top_k], lower)
+    tok_copy = pltpu.make_async_copy(tok, tok_ref, tsem)
+    tok_copy.start()
+
     dy_pair(0, me, False)
 
     @pl.loop(0, 2)
@@ -277,8 +280,7 @@
     for slot in range(2):
         c_copy(slot, NE - 1, 0).wait()
         q_copy(slot, 0).wait()
-    for copy in tab_copies:
-        copy.wait()
+    tok_copy.wait()
     for copy in sends:
         copy.wait_send()
 
@@ -295,7 +297,7 @@
                    jax.ShapeDtypeStruct((NG, tokens, dim), BF16),
                    jax.ShapeDtypeStruct((NE, NG, CAP, dim), BF16),
                    jax.ShapeDtypeStruct((NG, 8, tokens), F32),
-                   jax.ShapeDtypeStruct((2, 16, tokens), F32)),
+                   jax.ShapeDtypeStruct((3, tokens, 128), F32)),
         in_specs=[any_spec] * 6,
         out_specs=[any_spec] * 5,
         scratch_shapes=[
@@ -314,7 +316,8 @@
             pltpu.SemaphoreType.DMA((2, 3)),
             pltpu.SemaphoreType.DMA((2,)),
             pltpu.SemaphoreType.DMA((2,)),
-            pltpu.SemaphoreType.DMA((2,)),
+            pltpu.SemaphoreType.DMA,
+            pltpu.VMEM((3, tokens, 128), F32),
         ],
         cost_estimate=pl.CostEstimate(flops=flops, bytes_accessed=60_000_000, transcendentals=0),
         compiler_params=pltpu.CompilerParams(collective_id=0, has_side_effects=True,
@@ -322,34 +325,11 @@
     )(x_acts, d_out, table, w_in, w_up, w_out)
 
 
-def backward_kernel(code_ref, xb_ref, q_ref, win_ref, wup_ref, wout_ref, c_ref,
-                    dx_ref, dwin_ref, dwup_ref, dwout_ref, back_ref,
-                    xs, acc_in, acc_up, acc_out, ssem, rsem):
+def backward_kernel(code_ref, xb_ref, q_ref, win_ref, wup_ref, wout_ref,
+                    dx_ref, dwin_ref, dwup_ref, dwout_ref,
+                    xs, acc_in, acc_up, acc_out):
     step = pl.program_id(0)
     tokens, dim = xb_ref.shape[1:]
-    stage = lax.axis_index('stage')
-    me = lax.axis_index('expert')
-
-    def give(k):
-        peer = (me + k) % NG
-        return pltpu.make_async_remote_copy(
-            src_ref=c_ref.at[peer], dst_ref=back_ref.at[me], send_sem=ssem.at[k], recv_sem=rsem.at[me],
-            device_id=(stage, peer), device_id_type=MESH)
-
-    def take(k):
-        peer = (me + k) % NG
-        return pltpu.make_async_remote_copy(
-            src_ref=c_ref.at[peer], dst_ref=back_ref.at[peer], send_sem=ssem.at[k],
-            recv_sem=rsem.at[peer], device_id=(stage, peer), device_id_type=MESH)
-
-    @pl.when(step == 0)
-    def _():
-        barrier = pltpu.get_barrier_semaphore()
-        for k in range(1, NG):
-            pl.semaphore_signal(barrier, inc=1, device_id=(stage, (me + k) % NG), device_id_type=MESH)
-        pl.semaphore_wait(barrier, NG - 1)
-        for k in range(1, NG):
-            give(k).start()
 
     @pl.when(step < NG)
     def _():
@@ -396,15 +376,8 @@
         dwup_ref[0, 0] = acc_up[...].astype(BF16)
         dwout_ref[0, 0] = acc_out[...].astype(BF16)
 
-    @pl.when(step == NG + NE - 1)
-    def _():
-        for k in range(1, NG):
-            take(k).wait_recv()
-        for k in range(1, NG):
-            give(k).wait_send()
-
-
-def run_backward(code, xb, q, w_in, w_up, w_out, c_rows):
+
+def run_backward(code, xb, q, w_in, w_up, w_out):
     tokens, dim = xb.shape[1:]
     hid = w_in.shape[3]
     exp = lambda i: jnp.maximum(i - NG, 0)
@@ -418,41 +391,35 @@
         out_shape=(jax.ShapeDtypeStruct((NG, NE, CAP, dim), BF16),
                    jax.ShapeDtypeStruct(w_in.shape, BF16),
                    jax.ShapeDtypeStruct(w_up.shape, BF16),
-                   jax.ShapeDtypeStruct(w_out.shape, BF16),
-                   jax.ShapeDtypeStruct((NG, NE, CAP, dim), BF16)),
+                   jax.ShapeDtypeStruct(w_out.shape, BF16)),
         in_specs=[pl.BlockSpec((1, 8, tokens), lambda i: (src(i), 0, 0)),
                   pl.BlockSpec((1, tokens, dim), lambda i: (src(i), 0, 0)),
                   pl.BlockSpec((1, NG, CAP, dim), lambda i: (exp(i), 0, 0, 0)),
-                  w_spec(dim, hid), w_spec(dim, hid), w_spec(hid, dim),
-                  pl.BlockSpec(memory_space=pl.ANY)],
+                  w_spec(dim, hid), w_spec(dim, hid), w_spec(hid, dim)],
         out_specs=[pl.BlockSpec((NG, 1, CAP, dim), lambda i: (0, exp(i), 0, 0)),
-                   w_spec(dim, hid), w_spec(dim, hid), w_spec(hid, dim),
-                   pl.BlockSpec(memory_space=pl.ANY)],
+                   w_spec(dim, hid), w_spec(dim, hid), w_spec(hid, dim)],
         scratch_shapes=[pltpu.VMEM((NE, NG, CAP, dim), BF16),
                         pltpu.VMEM((dim, hid), F32), pltpu.VMEM((dim, hid), F32),
-                        pltpu.VMEM((hid, dim), F32),
-                        pltpu.SemaphoreType.DMA((NG,)), pltpu.SemaphoreType.DMA((NG,))],
+                        pltpu.VMEM((hid, dim), F32)],
         cost_estimate=pl.CostEstimate(flops=flops, bytes_accessed=60_000_000, transcendentals=0),
-        compiler_params=pltpu.CompilerParams(dimension_semantics=('arbitrary',), collective_id=1,
-                                             has_side_effects=True, vmem_limit_bytes=64_000_000),
-    )(code, xb, q, w_in, w_up, w_out, c_rows)
-
-
-def token_codes(ids):
+        compiler_params=pltpu.CompilerParams(dimension_semantics=('arbitrary',),
+                                             vmem_limit_bytes=64_000_000),
+    )(code, xb, q, w_in, w_up, w_out)
+
+
+def token_codes(ids, lower):
     tokens, top_k = ids.shape
-    num_experts = NG * NE
-    experts = lax.broadcasted_iota(jnp.int32, (tokens, num_experts), 1).astype(F32)
-    taken = jnp.zeros((tokens, num_experts), F32)
+    experts = lax.broadcasted_iota(jnp.int32, (tokens, 128), 1).astype(F32)
+    taken = jnp.zeros((tokens, 128), F32)
     for j in range(top_k):
         taken += jnp.where(ids[:, j:j + 1] == experts, 1.0, 0.0)
-    lower = (lax.broadcasted_iota(jnp.int32, (tokens, tokens), 0)
-             >= lax.broadcasted_iota(jnp.int32, (tokens, tokens), 1)).astype(F32).astype(BF16)
     rank = dot(lower, taken.astype(BF16)) - 1.0
     return jnp.where(taken > 0.5, rank, -10000.0)
 
 
-def slot_matrix(code):
+def slot_matrix(code, device):
     tokens = code.shape[0]
+    code = pltpu.roll(code, (128 - NE * device) % 128, 1)
     lane = lax.broadcasted_iota(jnp.int32, (tokens, 128), 1).astype(F32)
     blocks = []
     for b in range(NE * CAP // 128):
@@ -465,9 +432,9 @@
     return jnp.concatenate(blocks, axis=1)
 
 
-def collect_kernel(tab_ref, c_ref, back_ref, rows_ref,
+def collect_kernel(tok_ref, c_ref, back_ref, rows_ref,
                    y_ref, dx_ref,
-                   codes, ybuf, rbuf, acc, part_out, part_in, out_buf,
+                   ybuf, rbuf, acc, part_out, part_in, out_buf, y_buf,
                    ysem, osem, ssem, rsem, psem, prsem, zsem, zrsem):
     stage = lax.axis_index('stage')
     me = lax.axis_index('expert')
@@ -481,8 +448,9 @@
     line = xn + core * (yn - xn)
     line0 = 2 * (line // 2)
     tokens, dim = acc.shape
-    chunks = part_out.shape[0]
-    tchunk = tokens // chunks
+    pieces, piece = part_out.shape[:2]
+    tchunk = 256
+    per_chunk = tchunk // piece
 
     barrier = pltpu.get_barrier_semaphore()
     for peer in ((1 - stage, me), (stage, sib), (stage, xn), (stage, yn), (stage, sib_of(xn)),
@@ -516,11 +484,6 @@
 
     y_fetch(0).start()
 
-    for n, (row, kind) in enumerate(((0, 0), (1, 1), (0, 1))):
-        code = token_codes(tab_ref[row].T[:, 8 * kind:8 * kind + 4])
-        for s in range(NG):
-            codes[n, s] = code[:, s * NE:(s + 1) * NE]
-
     def rows_of(ref):
         return ref.reshape(NE * CAP, dim)
 
@@ -528,7 +491,7 @@
         if k + 1 < NG:
             y_fetch(k + 1).start()
         y_fetch(k).wait()
-        part = dot(slot_matrix(codes[0, (me + k) % NG]), rows_of(ybuf[k % 2]))
+        part = dot(slot_matrix(tok_ref[0], (me + k) % NG), rows_of(ybuf[k % 2]))
         acc[...] = part if k == 0 else acc[...] + part
 
     sources = (sib, line0, line0 + 1, me)
@@ -540,56 +503,64 @@
 
     def z_copy(i):
         return pltpu.make_async_remote_copy(
-            src_ref=out_buf.at[i], dst_ref=dx_ref.at[pl.ds(i * tchunk, tchunk)], send_sem=zsem.at[i],
+            src_ref=out_buf.at[i], dst_ref=dx_ref.at[pl.ds(i * piece, piece)], send_sem=zsem.at[i],
             recv_sem=zrsem.at[i], device_id=(1 - stage, me), device_id_type=MESH)
 
-    for k in range(0, 4):
+    def combine(table, role, chunk):
+        toks = pl.ds(chunk * tchunk, tchunk)
+        code = tok_ref[table, toks]
+        total = None
+        for slot, d in enumerate(sources):
+            part = dot(slot_matrix(code, d), rows_of(rbuf[role, slot]))
+            total = part if total is None else total + part
+        return total
+
+    for k in range(0, 5):
         y_part(k)
     for slot in range(3):
         arrived(0, slot)
     own[0].wait()
 
-    @pl.loop(0, chunks)
-    def _(i):
-        toks = pl.ds(i * tchunk, tchunk)
-        total = None
-        for slot, d in enumerate(sources):
-            part = dot(slot_matrix(codes[1, d, toks]), rows_of(rbuf[0, slot]))
-            total = part if total is None else total + part
-        part_out[i] = total
-        partial_copy(i).start()
-
-    for k in range(4, NG):
+    @pl.loop(0, tokens // tchunk)
+    def _(chunk):
+        total = combine(1, 0, chunk)
+        for p in range(per_chunk):
+            part_out[chunk * per_chunk + p] = total[p * piece:(p + 1) * piece]
+        for p in range(per_chunk):
+            partial_copy(chunk * per_chunk + p).start()
+
+    for k in range(5, NG):
         y_part(k)
-    out_buf[...] = acc[...].astype(BF16).reshape(out_buf.shape)
-    y_out = [pltpu.make_async_copy(out_buf.at[i], y_ref.at[pl.ds(i * tchunk, tchunk)], zsem.at[i])
-             for i in range(chunks)]
-    for copy in y_out:
-        copy.start()
+    y_buf[...] = acc[...].astype(BF16)
+    y_out = pltpu.make_async_copy(y_buf, y_ref, osem.at[0])
+    y_out.start()
     for slot in range(3):
         arrived(1, slot)
     own[1].wait()
-    for slot, d in enumerate(sources):
-        part = dot(slot_matrix(codes[2, d]), rows_of(rbuf[1, slot]))
-        acc[...] = part if slot == 0 else acc[...] + part
-    for copy in y_out:
-        copy.wait()
-
-    for i in range(chunks):
-        partial_copy(i).wait_recv()
-        out_buf[i] = (acc[i * tchunk:(i + 1) * tchunk] + part_in[i]).astype(BF16)
-        z_copy(i).start()
+
+    @pl.loop(0, tokens // tchunk)
+    def _(chunk):
+        total = combine(2, 1, chunk)
+        for p in range(per_chunk):
+            i = chunk * per_chunk + p
+            partial_copy(i).wait_recv()
+            out_buf[i] = (total[p * piece:(p + 1) * piece] + part_in[i]).astype(BF16)
+            z_copy(i).start()
+
+    y_out.wait()
     for copy in sends:
         copy.wait_send()
-    for i in range(chunks):
+
+    @pl.loop(0, pieces)
+    def _(i):
         partial_copy(i).wait_send()
         z_copy(i).wait()
 
 
-def run_collect(tables, c_rows, y_back, dx_rows):
-    tokens = tables.shape[2]
+def run_collect(tok, c_rows, y_back, dx_rows):
+    tokens = tok.shape[1]
     dim = c_rows.shape[3]
-    chunks = 4
+    pieces = 16
     any_spec = pl.BlockSpec(memory_space=pl.ANY)
     return pl.pallas_call(
         collect_kernel,
@@ -598,38 +569,41 @@
         in_specs=[pl.BlockSpec(memory_space=pltpu.VMEM)] + [any_spec] * 3,
         out_specs=[any_spec] * 2,
         scratch_shapes=[
-            pltpu.VMEM((3, NG, tokens, NE), F32),
             pltpu.VMEM((2, NE, CAP, dim), BF16),
             pltpu.VMEM((2, 4, NE, CAP, dim), BF16),
             pltpu.VMEM((tokens, dim), F32),
-            pltpu.VMEM((chunks, tokens // chunks, dim), F32),
-            pltpu.VMEM((chunks, tokens // chunks, dim), F32),
-            pltpu.VMEM((chunks, tokens // chunks, dim), BF16),
+            pltpu.VMEM((pieces, tokens // pieces, dim), F32),
+            pltpu.VMEM((pieces, tokens // pieces, dim), F32),
+            pltpu.VMEM((pieces, tokens // pieces, dim), BF16),
+            pltpu.VMEM((tokens, dim), BF16),
             pltpu.SemaphoreType.DMA((2,)),
             pltpu.SemaphoreType.DMA((2,)),
             pltpu.SemaphoreType.DMA((2, 3)),
             pltpu.SemaphoreType.DMA((2, 3)),
-            pltpu.SemaphoreType.DMA((chunks,)),
-            pltpu.SemaphoreType.DMA((chunks,)),
-            pltpu.SemaphoreType.DMA((chunks,)),
-            pltpu.SemaphoreType.DMA((chunks,)),
+            pltpu.SemaphoreType.DMA((pieces,)),
+            pltpu.SemaphoreType.DMA((pieces,)),
+            pltpu.SemaphoreType.DMA((pieces,)),
+            pltpu.SemaphoreType.DMA((pieces,)),
         ],
         cost_estimate=pl.CostEstimate(flops=4 * tokens * NG * NE * CAP * dim,
                                       bytes_accessed=20_000_000, transcendentals=0),
         compiler_params=pltpu.CompilerParams(collective_id=2, has_side_effects=True,
                                              vmem_limit_bytes=64_000_000),
-    )(tables, c_rows, y_back, dx_rows)
+    )(tok, c_rows, y_back, dx_rows)
 
 
 def solution(mesh):
     def device_fn(x_acts, expert_ids, gate_wts, w_in, w_up, w_out, d_out):
+        dim = x_acts.shape[3]
         ids_t = jnp.swapaxes(expert_ids[:, 0], 1, 2).astype(F32)
         gates_t = jnp.swapaxes(gate_wts[:, 0], 1, 2)
         table = jnp.concatenate([ids_t[1], gates_t[1], ids_t[0], gates_t[0]], axis=0)
 
-        c_rows, xb, q_rows, code, tables = run_dispatch(x_acts, d_out, table, w_in, w_up, w_out)
-        dx_rows, dw_in, dw_up, dw_out, y_back = run_backward(code, xb, q_rows, w_in, w_up, w_out, c_rows)
-        y_dev, dx_dev = run_collect(tables, c_rows, y_back, dx_rows)
+        c_rows, xb, q_rows, code, tok = run_dispatch(x_acts, d_out, table, w_in, w_up, w_out)
+        y_back = lax.all_to_all(c_rows.reshape(NG, NE * CAP, dim), 'expert', 0, 0, tiled=True)
+        dx_rows, dw_in, dw_up, dw_out = run_backward(code, xb, q_rows, w_in, w_up, w_out)
+        y_back = y_back.reshape(c_rows.shape)
+        y_dev, dx_dev = run_collect(tok, c_rows, y_back, dx_rows)
         return y_dev[None], dx_dev[None], dw_in, dw_up, dw_out
 
     tok_spec = P(None, 'stage', 'expert', None)

time: 340 us -> 325 us (0.956)
  Pallas kernels: 320 us -> 292 us
  waiting for transfers between devices: 0 us -> 14.6 us
  local copies, waits for them, and re-layouts: 13.8 us -> 4.39 us
  starting transfers between devices: 0 us -> 5.31 us
    pallas_call x1, Pallas kernels: 92 us -> 73.8 us  [run_backward(): pl.pallas_call(backward_kernel, name='backward', grid=(NG + NE,), out_sha...]
    all_to_all x0 -> x1, waiting for transfers between devices: none -> 14.6 us  [device_fn(): lax.all_to_all(c_rows.reshape(NG, NE * CAP, dim), 'expert', 0, 0, tiled=T...]
    pallas_call x1, Pallas kernels: 89.8 us -> 80.3 us  [run_collect(): pl.pallas_call(collect_kernel, name='collect', out_shape=(jax.ShapeDtypeS...]
    unnamed x11 -> x4, local copies, waits for them, and re-layouts: 13 us -> 3.65 us
    all_to_all x0 -> x1, starting transfers between devices: none -> 5.31 us  [device_fn(): lax.all_to_all(c_rows.reshape(NG, NE * CAP, dim), 'expert', 0, 0, tiled=T...]
  transfers between devices with their start and end apart: 0 -> 1, of which waited for: 0 -> 1; matrix products, arithmetic and copies ran while one was open for 0% -> 0% of each run, Pallas kernels for 0% -> 23%
where the time goes in v3:
time: 325 us; the launch traced here: 319 us
  Pallas kernels  292 us (90%)
  waiting for transfers between devices  14.6 us (4%)
  starting transfers between devices  5.31 us (2%)
  local copies, waits for them, and re-layouts  4.39 us (1%)
    pallas_call x1, Pallas kernels, run_dispatch(): pl.pallas_call(dispatch_kernel, name='dispatch', out_shape=(jax.ShapeDtyp...  138 us
    pallas_call x1, Pallas kernels, run_collect(): pl.pallas_call(collect_kernel, name='collect', out_shape=(jax.ShapeDtypeS...  80.3 us
    pallas_call x1, Pallas kernels, run_backward(): pl.pallas_call(backward_kernel, name='backward', grid=(NG + NE,), out_sha...  73.8 us
    all_to_all x1, waiting for transfers between devices, device_fn(): lax.all_to_all(c_rows.reshape(NG, NE * CAP, dim), 'expert', 0, 0, tiled=T...  14.6 us
  transfers between devices with their start and end apart: 1, of which 1 were waited for; matrix products, arithmetic and copies ran while one was open for 0% of the time, Pallas kernels for 23%

profile of v3, /device:TPU:0, one launch (start us, length us, event | category | flops | bytes accessed | tf_op | source)
XLA Modules:
  0.0 319.0 jit_solution(8285600307684053853)
XLA Ops:
  0.6 0.8 fusion
  1.4 0.7 slice_bitcast_fusion.2
  2.1 0.6 pad_maximum_fusion.tab_ref
  2.8 138.4 %dispatch.1 = (bf16[8,4,192,640]{3,2,1,0:T(8,128)(2,1)}, bf16[8,1024,640]{2,1,0:T(8,128)(2,1)}, bf16[4,8,192,640]{3,2,1,0:T(8,128)(2,1)}, f32[8,8,1024]{2,1,0:T(8,128)}, f32[3,1024,128]{2,1,0:T(8,128)}) custom-call(bf16[2,1,1024,640]{3,2,1,0:T(8,128)(2,1)} %x_ref.1, bf16[1,1024,640]{2,1,0:T(8,128)(2,1)} %dy_ref.1, f32[16,1024]{1,0:T(8,128)} %pad_maximum_fusion.tab_ref, ...), custom_call_target="tpu_custom_call" | custom-call | flops 31205621760 | bytes 60000000 | tf_op jit(solution)/shard_map/dispatch/pallas_call | solution.py:293
  141.2 5.3 %all-to-all-start = ((bf16[8,768,640]{2,1,0:T(8,128)(2,1)}), bf16[8,768,640]{2,1,0:T(8,128)(2,1)}, u32[]{:S(2)}, u32[]{:S(2)}) async-start(bf16[8,768,640]{2,1,0:T(8,128)(2,1)} %bitcast.23), calls=%async_computation | async-start | bytes 15728640 | tf_op jit(solution)/shard_map/all_to_all | solution.py:603
  146.5 73.8 %backward.1 = (bf16[8,4,192,640]{3,2,1,0:T(8,128)(2,1)}, bf16[1,4,640,640]{3,2,1,0:T(8,128)(2,1)}, bf16[1,4,640,640]{3,2,1,0:T(8,128)(2,1)}, bf16[1,4,640,640]{3,2,1,0:T(8,128)(2,1)}) custom-call(f32[8,8,1024]{2,1,0:T(8,128)} %get-tuple-element.18.code_ref, bf16[8,1024,640]{2,1,0:T(8,128)(2,1)} %get-tuple-element.19.xb_ref, ...), custom_call_target="tpu_custom_call" | custom-call | flops 48318382080 | bytes 60000000 | tf_op jit(solution)/shard_map/backward/pallas_call | solution.py:387
  220.2 14.6 %all-to-all-done = bf16[8,768,640]{2,1,0:T(8,128)(2,1)} async-done(((bf16[8,768,640]{2,1,0:T(8,128)(2,1)}), bf16[8,768,640]{2,1,0:T(8,128)(2,1)}, u32[]{:S(2)}, u32[]{:S(2)}) %all-to-all-start) | async-done | bytes 7864352 | tf_op jit(solution)/shard_map/all_to_all | solution.py:603
  234.8 80.3 %collect.1 = (bf16[1024,640]{1,0:T(8,128)(2,1)}, bf16[1024,640]{1,0:T(8,128)(2,1)}) custom-call(f32[3,1024,128]{2,1,0:T(8,128)} %get-tuple-element.16.tok_ref, bf16[8,4,192,640]{3,2,1,0:T(8,128)(2,1)} %get-tuple-element.17.c_ref, bf16[8,4,192,640]{3,2,1,0:T(8,128)(2,1)} %bitcast.12.back_ref, bf16[8,4,192,640]{3,2,1,0:T(8,128)(2,1)} %get-tuple-element.21.rows_ref), custom_call_target="tpu_custom_call" | custom-call | flops 16106127360 | bytes 20000000 | tf_op jit(solution)/shard_map/collect/pallas_call | solution.py:565
  315.1 0.0 copy-start
  315.1 2.6 copy.15
  317.7 0.0 copy-done
  317.7 1.1 copy.16
Async XLA Ops:
  141.2 93.7 %all-to-all-start = ((bf16[8,768,640]{2,1,0:T(8,128)(2,1)}), bf16[8,768,640]{2,1,0:T(8,128)(2,1)}, u32[]{:S(2)}, u32[]{:S(2)}) async-start(bf16[8,768,640]{2,1,0:T(8,128)(2,1)} %bitcast.23), calls=%async_computation | async-start | bytes 15728640 | tf_op jit(solution)/shard_map/all_to_all | solution.py:603
  315.1 2.6 copy-start

commit v4 on v3

--- a/solution.py
+++ b/solution.py
@@ -7,7 +7,7 @@
 
 MESH = pl.DeviceIdType.MESH
 F32, BF16 = jnp.float32, jnp.bfloat16
-DY, XF, XB, TAB = 0, 1, 2, 3
+DY, XF, XB, IDS, GTS = 0, 1, 2, 3, 4
 NG, NE, CAP = 8, 4, 192
 
 
@@ -20,18 +20,19 @@
     return [slot == code_rows[e:e + 1, :] for e in range(NE)]
 
 
-def dispatch_kernel(x_ref, dy_ref, tab_ref, win_ref, wup_ref, wout_ref,
+def dispatch_kernel(x_ref, dy_ref, ids_ref, gts_ref, win_ref, wup_ref, wout_ref,
                     c_ref, xb_ref, q_ref, code_ref, tok_ref,
-                    buf, tabs, codes, gates, gslot, xs, st, cst, wbuf,
-                    ssem, rsem, lsem, wsem, stsem, csem, tsem, tok):
+                    buf, tab_ids, tab_gts, codes, gates, gslot, xs, st, cst, wbuf, tok,
+                    ssem, rsem, lsem, wsem, stsem, csem, tsem):
     stage = lax.axis_index('stage')
     me = lax.axis_index('expert')
     other = 1 - stage
-    sib = me + 1 - 2 * (me % 2)
+    core = me % 2
     xn = me + 2 - 4 * ((me // 2) % 2)
     yn = me + 4 - 8 * (me // 4)
     dg = xn + 4 - 8 * (xn // 4)
-    sib_of = lambda h: h + 1 - 2 * (h % 2)
+    sib_of = lambda h: h + 1 - 2 * core
+    sib = sib_of(me)
     tokens = x_ref.shape[2]
     half = tokens // 2
     sends = []
@@ -42,8 +43,10 @@
     pl.semaphore_wait(barrier, 4)
 
     def place(arr, h, part):
-        if arr == TAB:
-            return tabs.at[h]
+        if arr == IDS:
+            return tab_ids.at[h]
+        if arr == GTS:
+            return tab_gts.at[h]
         if arr == XB:
             return xb_ref.at[h, pl.ds(part * half, half)]
         return buf.at[arr, h, pl.ds(part * half, half)]
@@ -55,16 +58,16 @@
             device_id=peer, device_id_type=MESH)
 
     def send(arr, h, part, slot, peer, src=None):
-        copy = remote(arr, h, part, slot, peer, src)
-        copy.start()
-        sends.append(copy)
+        remote(arr, h, part, slot, peer, src).start()
+        sends.append((arr, h, part, slot, peer, src))
 
     def arrived(arr, h, part):
         remote(arr, h, part, 0, (stage, sib)).wait_recv()
 
     to_x, to_y, to_sib, to_z = (stage, xn), (stage, yn), (stage, sib), (other, me)
 
-    send(TAB, me, 0, 14, to_z, tab_ref)
+    send(IDS, me, 0, 14, to_z, ids_ref)
+    send(GTS, me, 0, 14, to_z, gts_ref)
     for part in range(2):
         send(XF, me, part, 14 + part, to_z, x_ref.at[1, 0, pl.ds(part * half, half)])
     for part in range(2):
@@ -85,10 +88,11 @@
         for copy in weights(e):
             copy.start()
 
-    arrived(TAB, me, 0)
-    send(TAB, me, 0, 0, to_x)
-    send(TAB, me, 0, 2, to_y)
-    send(TAB, me, 0, 4, to_sib)
+    for arr in (IDS, GTS):
+        arrived(arr, me, 0)
+        send(arr, me, 0, 0, to_x)
+        send(arr, me, 0, 2, to_y)
+        send(arr, me, 0, 4, to_sib)
     send(DY, me, 1, 1, to_x, dy_half(1))
     send(DY, me, 0, 3, to_y, dy_half(0))
 
@@ -121,129 +125,114 @@
         send(arr, me, 0, 4, to_sib)
         send(arr, me, 1, 5, to_sib)
 
-    arrived(TAB, xn, 0)
-    arrived(TAB, yn, 0)
-    send(TAB, xn, 0, 6, to_y)
+    for arr in (IDS, GTS):
+        arrived(arr, xn, 0)
+        arrived(arr, yn, 0)
+        send(arr, xn, 0, 6, to_y)
     first_halves(DY)
-    send(TAB, xn, 0, 8, to_sib)
-    send(TAB, yn, 0, 10, to_sib)
+    for arr in (IDS, GTS):
+        send(arr, xn, 0, 8, to_sib)
+        send(arr, yn, 0, 10, to_sib)
     own_sends(XF)
     second_halves(DY)
-    arrived(TAB, dg, 0)
-    send(TAB, dg, 0, 12, to_sib)
-    for h in (sib, sib_of(xn), sib_of(yn), sib_of(dg)):
-        arrived(TAB, h, 0)
+    for arr in (IDS, GTS):
+        arrived(arr, dg, 0)
+        send(arr, dg, 0, 12, to_sib)
+        for h in (sib, sib_of(xn), sib_of(yn), sib_of(dg)):
+            arrived(arr, h, 0)
+
     upper = (lax.broadcasted_iota(jnp.int32, (tokens, tokens), 0)
              <= lax.broadcasted_iota(jnp.int32, (tokens, tokens), 1)).astype(F32).astype(BF16)
-    top_k = 4
     for kind in range(2):
         taken = []
         for h in range(NG):
-            ids = tabs[h, 8 * kind:8 * kind + top_k, :]
-            gts = tabs[h, 8 * kind + top_k:8 * kind + 2 * top_k, :]
             for e in range(NE):
-                eq = ids == (me * NE + e).astype(F32)
+                eq = tab_ids[h, 1 - kind] == me * NE + e
                 taken.append(jnp.sum(jnp.where(eq, 1.0, 0.0), axis=0, keepdims=True))
-                gates[kind, h, e:e + 1, :] = jnp.sum(jnp.where(eq, gts, 0.0), axis=0, keepdims=True)
+                gates[kind, h, e:e + 1, :] = jnp.sum(jnp.where(eq, tab_gts[h, 1 - kind], 0.0), axis=0,
+                                                     keepdims=True)
         taken = jnp.concatenate(taken, axis=0)
         rank = dot(taken.astype(BF16), upper) - 1.0
         code = jnp.where(taken > 0.5, rank, -1.0)
         for h in range(NG):
             codes[kind, h, 0:NE, :] = code[h * NE:(h + 1) * NE, :]
             codes[kind, h, NE:8, :] = jnp.full((8 - NE, tokens), -1.0, F32)
-    code_copy = pltpu.make_async_copy(codes.at[1], code_ref, lsem)
-
-    def gather(kind, h, tok_rows):
+    code_copy = pltpu.make_async_copy(codes.at[1], code_ref, tsem.at[0])
+    code_copy.start()
+
+    partner = yn + core * (xn - yn)
+    lower = (lax.broadcasted_iota(jnp.int32, (tokens, tokens), 0)
+             >= lax.broadcasted_iota(jnp.int32, (tokens, tokens), 1)).astype(F32).astype(BF16)
+    for n, (h, kind) in enumerate(((me, 1), (partner, 0), (me, 0))):
+        both = jnp.concatenate([tab_ids[h, 0], tab_ids[h, 1]], axis=0).astype(F32)
+        tok[n] = token_codes(both.T[:, 4 * kind:4 * kind + 4], lower)
+    tok_copy = pltpu.make_async_copy(tok, tok_ref, tsem.at[1])
+    tok_copy.start()
+
+    def shard(i):
+        j, odd = i // 2, i % 2
+        return me + (j % 2) * (xn - me) + (j // 2) * (yn - me) + odd * (1 - 2 * core)
+
+    def gather(kind, arr, h):
         hits = slot_hits(codes[kind, h], tokens)
         gate_rows = gates[kind, h]
         onehot = jnp.concatenate([jnp.where(hit, 1.0, 0.0).astype(BF16) for hit in hits], axis=0)
         slot_gate = [jnp.sum(jnp.where(hits[e], gate_rows[e:e + 1, :], 0.0), axis=1, keepdims=True)
                      for e in range(NE)]
-        return dot(onehot, tok_rows), slot_gate
+        return dot(onehot, buf[arr, h]), slot_gate
 
     def q_copy(slot, h):
         return pltpu.make_async_copy(st.at[slot], q_ref.at[:, h], stsem.at[slot])
 
-    def gather_dy(n, h, wait_slot):
-        slot = n % 2
-        if wait_slot:
-            q_copy(slot, h).wait()
-        rows, slot_gate = gather(1, h, buf[DY, h])
+    def sibling_part(arr, i):
+        @pl.when(i % 2 == 1)
+        def _():
+            arrived(arr, shard(i), 0)
+            arrived(arr, shard(i), 1)
+
+    own_dy.wait()
+
+    @pl.loop(0, NG)
+    def _(i):
+        pl.when(i == 6)(lambda: diagonal(DY))
+        sibling_part(DY, i)
+        h, slot = shard(i), i % 2
+        pl.when(i >= 2)(lambda: q_copy(slot, h).wait())
+        rows, slot_gate = gather(1, DY, h)
         for e in range(NE):
             st[slot, e] = (slot_gate[e] * rows[e * CAP:(e + 1) * CAP]).astype(BF16)
         q_copy(slot, h).start()
 
-    def gather_xf(h):
-        rows, slot_gate = gather(0, h, buf[XF, h])
+    first_halves(XF)
+    own_sends(XB)
+
+    @pl.loop(0, NG)
+    def _(i):
+        pl.when(i == 2)(lambda: second_halves(XF))
+        pl.when(i == 6)(lambda: diagonal(XF))
+        sibling_part(XF, i)
+        h = shard(i)
+        rows, slot_gate = gather(0, XF, h)
         for e in range(NE):
             xs[e, h] = rows[e * CAP:(e + 1) * CAP].astype(BF16)
             gslot[e, h] = jnp.broadcast_to(slot_gate[e], (CAP, 128))
 
-    own_dy.wait()
-    code_copy.start()
-    code_copy.wait()
-
-    def pick(i, *choices):
-        out = choices[-1]
-        for k in range(len(choices) - 2, -1, -1):
-            out = jnp.where(i == k, choices[k], out)
-        return out
-
-    def dy_pair(i, h, wait_slot):
-        gather_dy(0, h, wait_slot)
-        h2 = sib_of(h)
-        arrived(DY, h2, 0)
-        arrived(DY, h2, 1)
-        gather_dy(1, h2, wait_slot)
-
-    core = me % 2
-    partner = yn + core * (xn - yn)
-    lower = (lax.broadcasted_iota(jnp.int32, (tokens, tokens), 0)
-             >= lax.broadcasted_iota(jnp.int32, (tokens, tokens), 1)).astype(F32).astype(BF16)
-    for n, (h, kind) in enumerate(((me, 0), (partner, 1), (me, 1))):
-        tok[n] = token_codes(tabs[h].T[:, 8 * kind:8 * kind + top_k], lower)
-    tok_copy = pltpu.make_async_copy(tok, tok_ref, tsem)
-    tok_copy.start()
-
-    dy_pair(0, me, False)
-
-    @pl.loop(0, 2)
-    def _(i):
-        dy_pair(0, xn + i * (yn - xn), True)
-
-    diagonal(DY)
-    dy_pair(0, dg, True)
-    first_halves(XF)
-    own_sends(XB)
-
-    def xf_pair(h):
-        gather_xf(h)
-        h2 = sib_of(h)
-        arrived(XF, h2, 0)
-        arrived(XF, h2, 1)
-        gather_xf(h2)
-
-    xf_pair(me)
-    second_halves(XF)
-
-    @pl.loop(0, 2)
-    def _(i):
-        xf_pair(xn + i * (yn - xn))
-
-    diagonal(XF)
-    xf_pair(dg)
-
     chunk = 2
+    steps = NG // chunk
     rows_chunk = chunk * CAP
 
     def c_copy(slot, e, h0):
         return pltpu.make_async_copy(cst.at[slot], c_ref.at[pl.ds(h0, chunk), e], csem.at[slot])
 
-    def ffn(e, first):
+    @pl.loop(0, NE)
+    def _(e):
+        pl.when(e == 1)(lambda: first_halves(XB))
+        pl.when(e == 3)(lambda: second_halves(XB))
         for copy in weights(e):
             copy.wait()
 
-        def body(i, wait_slot):
+        @pl.loop(0, steps)
+        def _(i):
             slot = i % 2
             h0 = i * chunk
             rows = xs[e, pl.ds(h0, chunk)].reshape(rows_chunk, -1)
@@ -252,27 +241,15 @@
             hidden = (act * dot(rows, wbuf[e % 2, 1])).astype(BF16)
             out = dot(hidden, wbuf[e % 2, 2])
             gate = gslot[e, pl.ds(h0, chunk)].reshape(rows_chunk, 128)[:, 0:1]
-            if wait_slot:
-                c_copy(slot, e, h0).wait()
+            pl.when(e * steps + i >= 2)(lambda: c_copy(slot, e, h0).wait())
             cst[slot] = (gate * out).astype(BF16).reshape(chunk, CAP, -1)
             c_copy(slot, e, h0).start()
 
-        if first:
-            body(0, False)
-            body(1, False)
-            pl.loop(2, NG // chunk)(lambda i: body(i, True))
-        else:
-            pl.loop(0, NG // chunk)(lambda i: body(i, True))
-        if e + 2 < NE:
+        @pl.when(e + 2 < NE)
+        def _():
             for copy in weights(e + 2):
                 copy.start()
 
-    ffn(0, True)
-    first_halves(XB)
-    ffn(1, False)
-    ffn(2, False)
-    second_halves(XB)
-    ffn(3, False)
     diagonal(XB)
     for h in (sib, sib_of(xn), sib_of(yn), sib_of(dg)):
         arrived(XB, h, 0)
@@ -280,12 +257,13 @@
     for slot in range(2):
         c_copy(slot, NE - 1, 0).wait()
         q_copy(slot, 0).wait()
+    code_copy.wait()
     tok_copy.wait()
-    for copy in sends:
-        copy.wait_send()
-
-
-def run_dispatch(x_acts, d_out, table, w_in, w_up, w_out):
+    for args in sends:
+        remote(*args).wait_send()
+
+
+def run_dispatch(x_acts, d_out, ids, gts, w_in, w_up, w_out):
     tokens, dim = x_acts.shape[2:]
     hid = w_in.shape[3]
     any_spec = pl.BlockSpec(memory_space=pl.ANY)
@@ -298,11 +276,12 @@
                    jax.ShapeDtypeStruct((NE, NG, CAP, dim), BF16),
                    jax.ShapeDtypeStruct((NG, 8, tokens), F32),
                    jax.ShapeDtypeStruct((3, tokens, 128), F32)),
-        in_specs=[any_spec] * 6,
+        in_specs=[any_spec] * 7,
         out_specs=[any_spec] * 5,
         scratch_shapes=[
             pltpu.VMEM((2, NG, tokens, dim), BF16),
-            pltpu.VMEM((NG, 16, tokens), F32),
+            pltpu.VMEM((NG, 2, 4, tokens), jnp.int32),
+            pltpu.VMEM((NG, 2, 4, tokens), F32),
             pltpu.VMEM((2, NG, 8, tokens), F32),
             pltpu.VMEM((2, NG, 8, tokens), F32),
             pltpu.VMEM((NE, NG, CAP, 128), F32),
@@ -310,19 +289,19 @@
             pltpu.VMEM((2, NE, CAP, dim), BF16),
             pltpu.VMEM((2, 2, CAP, dim), BF16),
             pltpu.VMEM((2, 3, dim, hid), BF16),
-            pltpu.SemaphoreType.DMA((4, 16)),
-            pltpu.SemaphoreType.DMA((4, NG, 2)),
+            pltpu.VMEM((3, tokens, 128), F32),
+            pltpu.SemaphoreType.DMA((5, 16)),
+            pltpu.SemaphoreType.DMA((5, NG, 2)),
             pltpu.SemaphoreType.DMA,
             pltpu.SemaphoreType.DMA((2, 3)),
             pltpu.SemaphoreType.DMA((2,)),
             pltpu.SemaphoreType.DMA((2,)),
-            pltpu.SemaphoreType.DMA,
-            pltpu.VMEM((3, tokens, 128), F32),
+            pltpu.SemaphoreType.DMA((2,)),
         ],
         cost_estimate=pl.CostEstimate(flops=flops, bytes_accessed=60_000_000, transcendentals=0),
         compiler_params=pltpu.CompilerParams(collective_id=0, has_side_effects=True,
                                              vmem_limit_bytes=67_043_328),
-    )(x_acts, d_out, table, w_in, w_up, w_out)
+    )(x_acts, d_out, ids, gts, w_in, w_up, w_out)
 
 
 def backward_kernel(code_ref, xb_ref, q_ref, win_ref, wup_ref, wout_ref,
@@ -432,7 +411,7 @@
     return jnp.concatenate(blocks, axis=1)
 
 
-def collect_kernel(tok_ref, c_ref, back_ref, rows_ref,
+def collect_kernel(tok_ref, back_ref, rows_ref,
                    y_ref, dx_ref,
                    ybuf, rbuf, acc, part_out, part_in, out_buf, y_buf,
                    ysem, osem, ssem, rsem, psem, prsem, zsem, zrsem):
@@ -479,20 +458,18 @@
             recv_sem=rsem.at[role, slot], device_id=(stage, sib), device_id_type=MESH).wait_recv()
 
     def y_fetch(k):
-        src = c_ref if k == 0 else back_ref
-        return pltpu.make_async_copy(src.at[(me + k) % NG], ybuf.at[k % 2], ysem.at[k % 2])
+        return pltpu.make_async_copy(back_ref.at[(me + k) % NG], ybuf.at[k % 2], ysem.at[k % 2])
 
     y_fetch(0).start()
+    acc[...] = jnp.zeros_like(acc)
 
     def rows_of(ref):
         return ref.reshape(NE * CAP, dim)
 
     def y_part(k):
-        if k + 1 < NG:
-            y_fetch(k + 1).start()
+        pl.when(k + 1 < NG)(lambda: y_fetch(k + 1).start())
         y_fetch(k).wait()
-        part = dot(slot_matrix(tok_ref[0], (me + k) % NG), rows_of(ybuf[k % 2]))
-        acc[...] = part if k == 0 else acc[...] + part
+        acc[...] += dot(slot_matrix(tok_ref[0], (me + k) % NG), rows_of(ybuf[k % 2]))
 
     sources = (sib, line0, line0 + 1, me)
 
@@ -515,8 +492,7 @@
             total = part if total is None else total + part
         return total
 
-    for k in range(0, 5):
-        y_part(k)
+    pl.loop(0, 5)(y_part)
     for slot in range(3):
         arrived(0, slot)
     own[0].wait()
@@ -529,8 +505,7 @@
         for p in range(per_chunk):
             partial_copy(chunk * per_chunk + p).start()
 
-    for k in range(5, NG):
-        y_part(k)
+    pl.loop(5, NG)(y_part)
     y_buf[...] = acc[...].astype(BF16)
     y_out = pltpu.make_async_copy(y_buf, y_ref, osem.at[0])
     y_out.start()
@@ -557,16 +532,16 @@
         z_copy(i).wait()
 
 
-def run_collect(tok, c_rows, y_back, dx_rows):
+def run_collect(tok, y_back, dx_rows):
     tokens = tok.shape[1]
-    dim = c_rows.shape[3]
+    dim = dx_rows.shape[3]
     pieces = 16
     any_spec = pl.BlockSpec(memory_space=pl.ANY)
     return pl.pallas_call(
         collect_kernel,
         name='collect',
         out_shape=(jax.ShapeDtypeStruct((tokens, dim), BF16), jax.ShapeDtypeStruct((tokens, dim), BF16)),
-        in_specs=[pl.BlockSpec(memory_space=pltpu.VMEM)] + [any_spec] * 3,
+        in_specs=[pl.BlockSpec(memory_space=pltpu.VMEM)] + [any_spec] * 2,
         out_specs=[any_spec] * 2,
         scratch_shapes=[
             pltpu.VMEM((2, NE, CAP, dim), BF16),
@@ -589,21 +564,19 @@
                                       bytes_accessed=20_000_000, transcendentals=0),
         compiler_params=pltpu.CompilerParams(collective_id=2, has_side_effects=True,
                                              vmem_limit_bytes=64_000_000),
-    )(tok, c_rows, y_back, dx_rows)
+    )(tok, y_back, dx_rows)
 
 
 def solution(mesh):
     def device_fn(x_acts, expert_ids, gate_wts, w_in, w_up, w_out, d_out):
         dim = x_acts.shape[3]
-        ids_t = jnp.swapaxes(expert_ids[:, 0], 1, 2).astype(F32)
+        ids_t = jnp.swapaxes(expert_ids[:, 0], 1, 2)
         gates_t = jnp.swapaxes(gate_wts[:, 0], 1, 2)
-        table = jnp.concatenate([ids_t[1], gates_t[1], ids_t[0], gates_t[0]], axis=0)
-
-        c_rows, xb, q_rows, code, tok = run_dispatch(x_acts, d_out, table, w_in, w_up, w_out)
+        c_rows, xb, q_rows, code, tok = run_dispatch(x_acts, d_out, ids_t, gates_t, w_in, w_up, w_out)
         y_back = lax.all_to_all(c_rows.reshape(NG, NE * CAP, dim), 'expert', 0, 0, tiled=True)
         dx_rows, dw_in, dw_up, dw_out = run_backward(code, xb, q_rows, w_in, w_up, w_out)
         y_back = y_back.reshape(c_rows.shape)
-        y_dev, dx_dev = run_collect(tok, c_rows, y_back, dx_rows)
+        y_dev, dx_dev = run_collect(tok, y_back, dx_rows)
         return y_dev[None], dx_dev[None], dw_in, dw_up, dw_out
 
     tok_spec = P(None, 'stage', 'expert', None)

time: 325 us -> 317 us (0.975); the launches traced: 319 us -> 317 us
  no operation moved by 1% of the time
where the time goes in v4:
time: 317 us
  Pallas kernels  293 us (92%)
  waiting for transfers between devices  14.6 us (5%)
  starting transfers between devices  5.09 us (2%)
  local copies, waits for them, and re-layouts  3.65 us (1%)
    pallas_call x1, Pallas kernels, run_dispatch(): pl.pallas_call(dispatch_kernel, name='dispatch', out_shape=(jax.ShapeDtyp...  139 us
    pallas_call x1, Pallas kernels, run_collect(): pl.pallas_call(collect_kernel, name='collect', out_shape=(jax.ShapeDtypeS...  80.3 us
    pallas_call x1, Pallas kernels, run_backward(): pl.pallas_call(backward_kernel, name='backward', grid=(NG + NE,), out_sha...  73.6 us
    all_to_all x1, waiting for transfers between devices, device_fn(): lax.all_to_all(c_rows.reshape(NG, NE * CAP, dim), 'expert', 0, 0, tiled=T...  14.6 us
  transfers between devices with their start and end apart: 1, of which 1 were waited for; matrix products, arithmetic and copies ran while one was open for 0% of the time, Pallas kernels for 23%

profile of v4, /device:TPU:0, one launch (start us, length us, event | category | flops | bytes accessed | tf_op | source)
XLA Modules:
  0.0 316.6 jit_solution(8445250897765599712)
XLA Ops:
  0.6 138.7 %dispatch.1 = (bf16[8,4,192,640]{3,2,1,0:T(8,128)(2,1)}, bf16[8,1024,640]{2,1,0:T(8,128)(2,1)}, bf16[4,8,192,640]{3,2,1,0:T(8,128)(2,1)}, f32[8,8,1024]{2,1,0:T(8,128)}, f32[3,1024,128]{2,1,0:T(8,128)}) custom-call(bf16[2,1,1024,640]{3,2,1,0:T(8,128)(2,1)} %x_ref.1, bf16[1,1024,640]{2,1,0:T(8,128)(2,1)} %dy_ref.1, s32[2,4,1024]{2,1,0:T(4,128)} %bitcast.13, ...), custom_call_target="tpu_custom_call" | custom-call | flops 31205621760 | bytes 60000000 | tf_op jit(solution)/shard_map/dispatch/pallas_call | solution.py:271
  139.3 5.1 %all-to-all-start = ((bf16[8,768,640]{2,1,0:T(8,128)(2,1)}), bf16[8,768,640]{2,1,0:T(8,128)(2,1)}, u32[]{:S(2)}, u32[]{:S(2)}) async-start(bf16[8,768,640]{2,1,0:T(8,128)(2,1)} %bitcast.10), calls=%async_computation | async-start | bytes 15728640 | tf_op jit(solution)/shard_map/all_to_all | solution.py:576
  144.4 73.6 %backward.1 = (bf16[8,4,192,640]{3,2,1,0:T(8,128)(2,1)}, bf16[1,4,640,640]{3,2,1,0:T(8,128)(2,1)}, bf16[1,4,640,640]{3,2,1,0:T(8,128)(2,1)}, bf16[1,4,640,640]{3,2,1,0:T(8,128)(2,1)}) custom-call(f32[8,8,1024]{2,1,0:T(8,128)} %get-tuple-element.18.code_ref, bf16[8,1024,640]{2,1,0:T(8,128)(2,1)} %get-tuple-element.19.xb_ref, ...), custom_call_target="tpu_custom_call" | custom-call | flops 48318382080 | bytes 60000000 | tf_op jit(solution)/shard_map/backward/pallas_call | solution.py:366
  218.0 14.6 %all-to-all-done = bf16[8,768,640]{2,1,0:T(8,128)(2,1)} async-done(((bf16[8,768,640]{2,1,0:T(8,128)(2,1)}), bf16[8,768,640]{2,1,0:T(8,128)(2,1)}, u32[]{:S(2)}, u32[]{:S(2)}) %all-to-all-start) | async-done | bytes 7864352 | tf_op jit(solution)/shard_map/all_to_all | solution.py:576
  232.6 80.3 %collect.1 = (bf16[1024,640]{1,0:T(8,128)(2,1)}, bf16[1024,640]{1,0:T(8,128)(2,1)}) custom-call(f32[3,1024,128]{2,1,0:T(8,128)} %get-tuple-element.16.tok_ref, bf16[8,4,192,640]{3,2,1,0:T(8,128)(2,1)} %bitcast.5.back_ref, bf16[8,4,192,640]{3,2,1,0:T(8,128)(2,1)} %get-tuple-element.21.rows_ref), custom_call_target="tpu_custom_call" | custom-call | flops 16106127360 | bytes 20000000 | tf_op jit(solution)/shard_map/collect/pallas_call | solution.py:540
  312.9 0.0 copy-start
  312.9 2.6 copy.14
  315.5 0.0 copy-done
  315.5 1.1 copy.15
Async XLA Ops:
  139.3 93.3 %all-to-all-start = ((bf16[8,768,640]{2,1,0:T(8,128)(2,1)}), bf16[8,768,640]{2,1,0:T(8,128)(2,1)}, u32[]{:S(2)}, u32[]{:S(2)}) async-start(bf16[8,768,640]{2,1,0:T(8,128)(2,1)} %bitcast.10), calls=%async_computation | async-start | bytes 15728640 | tf_op jit(solution)/shard_map/all_to_all | solution.py:576
  312.9 2.6 copy-start

commit v5 on v4

--- a/solution.py
+++ b/solution.py
@@ -163,9 +163,10 @@
     partner = yn + core * (xn - yn)
     lower = (lax.broadcasted_iota(jnp.int32, (tokens, tokens), 0)
              >= lax.broadcasted_iota(jnp.int32, (tokens, tokens), 1)).astype(F32).astype(BF16)
-    for n, (h, kind) in enumerate(((me, 1), (partner, 0), (me, 0))):
-        both = jnp.concatenate([tab_ids[h, 0], tab_ids[h, 1]], axis=0).astype(F32)
-        tok[n] = token_codes(both.T[:, 4 * kind:4 * kind + 4], lower)
+    for n, h in enumerate((me, partner)):
+        both = jnp.concatenate([tab_ids[h, 0], tab_ids[h, 1]], axis=0).astype(F32).T
+        for kind in range(2):
+            tok[kind, n] = token_codes(both[:, 4 * (1 - kind):4 * (1 - kind) + 4], lower)
     tok_copy = pltpu.make_async_copy(tok, tok_ref, tsem.at[1])
     tok_copy.start()
 
@@ -275,7 +276,7 @@
                    jax.ShapeDtypeStruct((NG, tokens, dim), BF16),
                    jax.ShapeDtypeStruct((NE, NG, CAP, dim), BF16),
                    jax.ShapeDtypeStruct((NG, 8, tokens), F32),
-                   jax.ShapeDtypeStruct((3, tokens, 128), F32)),
+                   jax.ShapeDtypeStruct((2, 2, tokens, 128), F32)),
         in_specs=[any_spec] * 7,
         out_specs=[any_spec] * 5,
         scratch_shapes=[
@@ -289,7 +290,7 @@
             pltpu.VMEM((2, NE, CAP, dim), BF16),
             pltpu.VMEM((2, 2, CAP, dim), BF16),
             pltpu.VMEM((2, 3, dim, hid), BF16),
-            pltpu.VMEM((3, tokens, 128), F32),
+            pltpu.VMEM((2, 2, tokens, 128), F32),
             pltpu.SemaphoreType.DMA((5, 16)),
             pltpu.SemaphoreType.DMA((5, NG, 2)),
             pltpu.SemaphoreType.DMA,
@@ -304,88 +305,6 @@
     )(x_acts, d_out, ids, gts, w_in, w_up, w_out)
 
 
-def backward_kernel(code_ref, xb_ref, q_ref, win_ref, wup_ref, wout_ref,
-                    dx_ref, dwin_ref, dwup_ref, dwout_ref,
-                    xs, acc_in, acc_up, acc_out):
-    step = pl.program_id(0)
-    tokens, dim = xb_ref.shape[1:]
-
-    @pl.when(step < NG)
-    def _():
-        hits = slot_hits(code_ref[0], tokens)
-        onehot = jnp.concatenate([jnp.where(hit, 1.0, 0.0).astype(BF16) for hit in hits], axis=0)
-        rows = dot(onehot, xb_ref[0]).astype(BF16)
-        for e in range(NE):
-            xs[e, step] = rows[e * CAP:(e + 1) * CAP]
-
-    @pl.when(step >= NG)
-    def _():
-        e = step - NG
-        chunk = 4
-        rows_chunk = chunk * CAP
-
-        def body(i):
-            hs = pl.ds(i * chunk, chunk)
-            x = xs[e, hs].reshape(rows_chunk, dim)
-            q = q_ref[0, hs].reshape(rows_chunk, dim)
-            pre_in = dot(x, win_ref[0, 0])
-            pre_up = dot(x, wup_ref[0, 0])
-            d_hid = dot(q, wout_ref[0, 0], ((1,), (1,)))
-            sig = jax.nn.sigmoid(pre_in)
-            act = pre_in * sig
-            hidden = (act * pre_up).astype(BF16)
-            d_in = (d_hid * pre_up * sig * (1.0 + pre_in * (1.0 - sig))).astype(BF16)
-            d_up = (d_hid * act).astype(BF16)
-            dx = dot(d_in, win_ref[0, 0], ((1,), (1,))) + dot(d_up, wup_ref[0, 0], ((1,), (1,)))
-            dx_ref[hs, 0] = dx.astype(BF16).reshape(chunk, CAP, dim)
-            return (dot(x, d_in, ((0,), (0,))), dot(x, d_up, ((0,), (0,))),
-                    dot(hidden, q, ((0,), (0,))))
-
-        steps = NG // chunk
-
-        def loop(i, carry):
-            parts = body(i)
-            first = i == 0
-            for acc, part in zip((acc_in, acc_up, acc_out), parts):
-                acc[...] = jnp.where(first, part, acc[...] + part)
-            return carry
-
-        lax.fori_loop(0, steps, loop, 0)
-        dwin_ref[0, 0] = acc_in[...].astype(BF16)
-        dwup_ref[0, 0] = acc_up[...].astype(BF16)
-        dwout_ref[0, 0] = acc_out[...].astype(BF16)
-
-
-def run_backward(code, xb, q, w_in, w_up, w_out):
-    tokens, dim = xb.shape[1:]
-    hid = w_in.shape[3]
-    exp = lambda i: jnp.maximum(i - NG, 0)
-    src = lambda i: jnp.minimum(i, NG - 1)
-    w_spec = lambda rows, cols: pl.BlockSpec((1, 1, rows, cols), lambda i: (0, exp(i), 0, 0))
-    flops = 2 * NG * NE * CAP * (tokens * dim + 8 * dim * hid)
-    return pl.pallas_call(
-        backward_kernel,
-        name='backward',
-        grid=(NG + NE,),
-        out_shape=(jax.ShapeDtypeStruct((NG, NE, CAP, dim), BF16),
-                   jax.ShapeDtypeStruct(w_in.shape, BF16),
-                   jax.ShapeDtypeStruct(w_up.shape, BF16),
-                   jax.ShapeDtypeStruct(w_out.shape, BF16)),
-        in_specs=[pl.BlockSpec((1, 8, tokens), lambda i: (src(i), 0, 0)),
-                  pl.BlockSpec((1, tokens, dim), lambda i: (src(i), 0, 0)),
-                  pl.BlockSpec((1, NG, CAP, dim), lambda i: (exp(i), 0, 0, 0)),
-                  w_spec(dim, hid), w_spec(dim, hid), w_spec(hid, dim)],
-        out_specs=[pl.BlockSpec((NG, 1, CAP, dim), lambda i: (0, exp(i), 0, 0)),
-                   w_spec(dim, hid), w_spec(dim, hid), w_spec(hid, dim)],
-        scratch_shapes=[pltpu.VMEM((NE, NG, CAP, dim), BF16),
-                        pltpu.VMEM((dim, hid), F32), pltpu.VMEM((dim, hid), F32),
-                        pltpu.VMEM((hid, dim), F32)],
-        cost_estimate=pl.CostEstimate(flops=flops, bytes_accessed=60_000_000, transcendentals=0),
-        compiler_params=pltpu.CompilerParams(dimension_semantics=('arbitrary',),
-                                             vmem_limit_bytes=64_000_000),
-    )(code, xb, q, w_in, w_up, w_out)
-
-
 def token_codes(ids, lower):
     tokens, top_k = ids.shape
     experts = lax.broadcasted_iota(jnp.int32, (tokens, 128), 1).astype(F32)
@@ -396,25 +315,26 @@
     return jnp.where(taken > 0.5, rank, -10000.0)
 
 
-def slot_matrix(code, device):
-    tokens = code.shape[0]
-    code = pltpu.roll(code, (128 - NE * device) % 128, 1)
+def slot_matrix(cols):
+    tokens = cols[0].shape[0]
     lane = lax.broadcasted_iota(jnp.int32, (tokens, 128), 1).astype(F32)
     blocks = []
-    for b in range(NE * CAP // 128):
+    for b in range(len(cols) * CAP // 128):
         hit = None
-        for e in range(NE):
-            if e * CAP < (b + 1) * 128 and (e + 1) * CAP > b * 128:
-                eq = lane == code[:, e:e + 1] + float(e * CAP - b * 128)
+        for k, col in enumerate(cols):
+            if k * CAP < (b + 1) * 128 and (k + 1) * CAP > b * 128:
+                eq = lane == col + float(k * CAP - b * 128)
                 hit = eq if hit is None else hit | eq
         blocks.append(jnp.where(hit, 1.0, 0.0).astype(BF16))
     return jnp.concatenate(blocks, axis=1)
 
 
-def collect_kernel(tok_ref, back_ref, rows_ref,
-                   y_ref, dx_ref,
-                   ybuf, rbuf, acc, part_out, part_in, out_buf, y_buf,
-                   ysem, osem, ssem, rsem, psem, prsem, zsem, zrsem):
+def finish_kernel(code_ref, tok_ref, xb_ref, q_ref, win_ref, wup_ref, wout_ref, c_ref,
+                  y_ref, dx_ref, dwin_ref, dwup_ref, dwout_ref, yhop_ref, dhop_ref, rows_ref,
+                  xbuf, xs, qbuf, wbuf, acc_in, acc_up, acc_out, dwst, dxst, rbuf, part_out, part_in,
+                  out_buf, y_buf,
+                  xsem, qsem, wsem, dwsem, dxsem, rbsem, rdsem, ysem,
+                  ssem, rsem, dsem, drsem, psem, prsem, zsem, zrsem):
     stage = lax.axis_index('stage')
     me = lax.axis_index('expert')
     core = me % 2
@@ -426,7 +346,7 @@
     partner = yn + core * (xn - yn)
     line = xn + core * (yn - xn)
     line0 = 2 * (line // 2)
-    tokens, dim = acc.shape
+    tokens, dim = y_buf.shape
     pieces, piece = part_out.shape[:2]
     tchunk = 256
     per_chunk = tchunk // piece
@@ -439,144 +359,287 @@
 
     targets = ((2 * (xn // 2), 2 * (dg // 2), 1 + core), (2 * (yn // 2) + 1, 2 * (dg // 2) + 1, 1 + core),
                (sib, sib_of(xn) + core * (sib_of(yn) - sib_of(xn)), 0))
-    sends = []
+
+    def y_hop(role, k):
+        target, via, slot = targets[k]
+        return pltpu.make_async_remote_copy(
+            src_ref=c_ref.at[via if role == 0 else target], dst_ref=yhop_ref.at[role, slot],
+            send_sem=ssem.at[role, k], recv_sem=rsem.at[role, slot],
+            device_id=(stage, target), device_id_type=MESH)
+
+    def y_arrived(role, slot):
+        pltpu.make_async_remote_copy(
+            src_ref=c_ref.at[me], dst_ref=yhop_ref.at[role, slot], send_sem=ssem.at[role, 0],
+            recv_sem=rsem.at[role, slot], device_id=(stage, sib), device_id_type=MESH).wait_recv()
+
+    def d_hop(role, k, e):
+        target, via, slot = targets[k]
+        return pltpu.make_async_remote_copy(
+            src_ref=rows_ref.at[via if role == 0 else target, e], dst_ref=dhop_ref.at[role, slot, e],
+            send_sem=dsem.at[e, role, k], recv_sem=drsem.at[e, role, slot],
+            device_id=(stage, target), device_id_type=MESH)
+
+    def d_arrived(role, slot, e):
+        pltpu.make_async_remote_copy(
+            src_ref=rows_ref.at[me, e], dst_ref=dhop_ref.at[role, slot, e], send_sem=dsem.at[e, role, 0],
+            recv_sem=drsem.at[e, role, slot], device_id=(stage, sib), device_id_type=MESH).wait_recv()
+
     for role in range(2):
-        for k, (target, via, slot) in enumerate(targets):
-            sends.append(pltpu.make_async_remote_copy(
-                src_ref=rows_ref.at[via if role == 0 else target], dst_ref=rbuf.at[role, slot],
-                send_sem=ssem.at[role, k], recv_sem=rsem.at[role, slot],
-                device_id=(stage, target), device_id_type=MESH))
-            sends[-1].start()
-    own = [pltpu.make_async_copy(rows_ref.at[h], rbuf.at[role, 3], osem.at[role])
-           for role, h in enumerate((partner, me))]
-    for copy in own:
-        copy.start()
-
-    def arrived(role, slot):
-        pltpu.make_async_remote_copy(
-            src_ref=rows_ref.at[me], dst_ref=rbuf.at[role, slot], send_sem=ssem.at[role, 0],
-            recv_sem=rsem.at[role, slot], device_id=(stage, sib), device_id_type=MESH).wait_recv()
-
-    def y_fetch(k):
-        return pltpu.make_async_copy(back_ref.at[(me + k) % NG], ybuf.at[k % 2], ysem.at[k % 2])
-
-    y_fetch(0).start()
-    acc[...] = jnp.zeros_like(acc)
-
-    def rows_of(ref):
-        return ref.reshape(NE * CAP, dim)
-
-    def y_part(k):
-        pl.when(k + 1 < NG)(lambda: y_fetch(k + 1).start())
-        y_fetch(k).wait()
-        acc[...] += dot(slot_matrix(tok_ref[0], (me + k) % NG), rows_of(ybuf[k % 2]))
+        for k in range(3):
+            y_hop(role, k).start()
+
+    def weights(e):
+        return [pltpu.make_async_copy(w.at[0, e], wbuf.at[e % 2, k], wsem.at[e % 2, k])
+                for k, w in enumerate((win_ref, wup_ref, wout_ref))] + [
+            pltpu.make_async_copy(q_ref.at[e], qbuf.at[e % 2], qsem.at[e % 2])]
+
+    def x_fetch(h):
+        return pltpu.make_async_copy(xb_ref.at[h], xbuf.at[h % 2], xsem.at[h % 2])
+
+    x_fetch(0).start()
+    for e in range(2):
+        for copy in weights(e):
+            copy.start()
+
+    @pl.loop(0, NG)
+    def _(h):
+        pl.when(h + 1 < NG)(lambda: x_fetch(h + 1).start())
+        hits = slot_hits(code_ref[h], tokens)
+        onehot = jnp.concatenate([jnp.where(hit, 1.0, 0.0).astype(BF16) for hit in hits], axis=0)
+        x_fetch(h).wait()
+        rows = dot(onehot, xbuf[h % 2]).astype(BF16)
+        for e in range(NE):
+            xs[e, h] = rows[e * CAP:(e + 1) * CAP]
 
     sources = (sib, line0, line0 + 1, me)
 
-    def partial_copy(i):
+    def y_load(role):
+        copies = [pltpu.make_async_copy(yhop_ref.at[role, slot], rbuf.at[0, :, slot], rbsem.at[0, slot])
+                  for slot in range(3)]
+        copies.append(pltpu.make_async_copy(c_ref.at[partner if role == 0 else me], rbuf.at[0, :, 3],
+                                            rbsem.at[0, 3]))
+        for copy in copies:
+            copy.start()
+        for copy in copies:
+            copy.wait()
+
+    def d_load(role, e):
+        copies = [pltpu.make_async_copy(dhop_ref.at[role, slot, e], rbuf.at[role, e, slot],
+                                        rdsem.at[role, e, slot])
+                  for slot in range(3)]
+        return copies + [pltpu.make_async_copy(rows_ref.at[partner if role == 0 else me, e],
+                                               rbuf.at[role, e, 3], rdsem.at[role, e, 3])]
+
+    def d_fetch(role, experts):
+        for e in experts:
+            for slot in range(3):
+                d_arrived(role, slot, e)
+            for copy in d_load(role, e):
+                copy.start()
+
+    def combine(kind, role, buf, chunk, experts):
+        code = tok_ref[kind, 1 - role, pl.ds(chunk * tchunk, tchunk)]
+        codes = [pltpu.roll(code, (128 - NE * d) % 128, 1) for d in sources]
+        total = None
+        for e in experts:
+            part = dot(slot_matrix([c[:, e:e + 1] for c in codes]), rbuf[buf, e].reshape(NE * CAP, dim))
+            total = part if total is None else total + part
+        return total
+
+    every = tuple(range(NE))
+
+    def partial_copy(kind, i):
         return pltpu.make_async_remote_copy(
-            src_ref=part_out.at[i], dst_ref=part_in.at[i], send_sem=psem.at[i], recv_sem=prsem.at[i],
-            device_id=(stage, partner), device_id_type=MESH)
+            src_ref=part_out.at[i], dst_ref=part_in.at[kind, i], send_sem=psem.at[kind, i],
+            recv_sem=prsem.at[kind, i], device_id=(stage, partner), device_id_type=MESH)
 
     def z_copy(i):
         return pltpu.make_async_remote_copy(
             src_ref=out_buf.at[i], dst_ref=dx_ref.at[pl.ds(i * piece, piece)], send_sem=zsem.at[i],
             recv_sem=zrsem.at[i], device_id=(1 - stage, me), device_id_type=MESH)
 
-    def combine(table, role, chunk):
-        toks = pl.ds(chunk * tchunk, tchunk)
-        code = tok_ref[table, toks]
-        total = None
-        for slot, d in enumerate(sources):
-            part = dot(slot_matrix(code, d), rows_of(rbuf[role, slot]))
-            total = part if total is None else total + part
-        return total
-
-    pl.loop(0, 5)(y_part)
+    def pass_on(kind, experts, first):
+        @pl.loop(0, tokens // tchunk)
+        def _(chunk):
+            total = combine(kind, 0, 0, chunk, experts)
+            for p in range(per_chunk):
+                i = chunk * per_chunk + p
+                part = total[p * piece:(p + 1) * piece]
+                part_out[i] = part if first else part_out[i] + part
+            if experts[-1] == NE - 1:
+                for p in range(per_chunk):
+                    partial_copy(kind, chunk * per_chunk + p).start()
+
+    def y_pass_on():
+        for slot in range(3):
+            y_arrived(0, slot)
+        y_load(0)
+        pass_on(0, every, True)
+
+    chunk = 4
+    rows_chunk = chunk * CAP
+    grads = ((acc_in, dwin_ref), (acc_up, dwup_ref), (acc_out, dwout_ref))
+
+    def grad_copies(e):
+        return [pltpu.make_async_copy(dwst.at[k], ref.at[0, e], dwsem.at[k])
+                for k, (_, ref) in enumerate(grads)]
+
+    @pl.loop(0, NE)
+    def _(e):
+        pl.when(e == 1)(y_pass_on)
+        for copy in weights(e):
+            copy.wait()
+        w_in, w_up, w_out = (wbuf[e % 2, k] for k in range(3))
+
+        @pl.loop(0, NG // chunk)
+        def _(i):
+            hs = pl.ds(i * chunk, chunk)
+            x = xs[e, hs].reshape(rows_chunk, dim)
+            q = qbuf[e % 2, hs].reshape(rows_chunk, dim)
+            pre_in = dot(x, w_in)
+            pre_up = dot(x, w_up)
+            d_hid = dot(q, w_out, ((1,), (1,)))
+            sig = jax.nn.sigmoid(pre_in)
+            act = pre_in * sig
+            hidden = (act * pre_up).astype(BF16)
+            d_in = (d_hid * pre_up * sig * (1.0 + pre_in * (1.0 - sig))).astype(BF16)
+            d_up = (d_hid * act).astype(BF16)
+            dx = dot(d_in, w_in, ((1,), (1,))) + dot(d_up, w_up, ((1,), (1,)))
+            dxst[hs] = dx.astype(BF16).reshape(chunk, CAP, dim)
+            parts = (dot(x, d_in, ((0,), (0,))), dot(x, d_up, ((0,), (0,))), dot(hidden, q, ((0,), (0,))))
+            for (acc, _), part in zip(grads, parts):
+                acc[...] = jnp.where(i == 0, part, acc[...] + part)
+
+        out = pltpu.make_async_copy(dxst, rows_ref.at[:, e], dxsem)
+        out.start()
+
+        @pl.when(e >= 1)
+        def _():
+            for copy in grad_copies(e - 1):
+                copy.wait()
+
+        for k, (acc, _) in enumerate(grads):
+            dwst[k] = acc[...].astype(BF16)
+        for copy in grad_copies(e):
+            copy.start()
+
+        @pl.when(e + 2 < NE)
+        def _():
+            for copy in weights(e + 2):
+                copy.start()
+
+        out.wait()
+        for role in range(2):
+            for k in range(3):
+                d_hop(role, k, e).start()
+
     for slot in range(3):
-        arrived(0, slot)
-    own[0].wait()
+        y_arrived(1, slot)
+    y_load(1)
 
     @pl.loop(0, tokens // tchunk)
     def _(chunk):
-        total = combine(1, 0, chunk)
+        total = combine(0, 1, 0, chunk, every)
         for p in range(per_chunk):
-            part_out[chunk * per_chunk + p] = total[p * piece:(p + 1) * piece]
-        for p in range(per_chunk):
-            partial_copy(chunk * per_chunk + p).start()
-
-    pl.loop(5, NG)(y_part)
-    y_buf[...] = acc[...].astype(BF16)
-    y_out = pltpu.make_async_copy(y_buf, y_ref, osem.at[0])
+            i = chunk * per_chunk + p
+            partial_copy(0, i).wait_recv()
+            y_buf[pl.ds(i * piece, piece)] = (total[p * piece:(p + 1) * piece] + part_in[0, i]).astype(BF16)
+            partial_copy(0, i).wait_send()
+
+    y_out = pltpu.make_async_copy(y_buf, y_ref, ysem)
     y_out.start()
-    for slot in range(3):
-        arrived(1, slot)
-    own[1].wait()
+
+    def d_ready(role, experts):
+        for e in experts:
+            for copy in d_load(role, e):
+                copy.wait()
+
+    d_fetch(0, every[:-1])
+    d_ready(0, every[:-1])
+    pass_on(1, every[:-1], True)
+    d_fetch(1, every[:-1])
+    d_fetch(0, every[-1:])
+    d_ready(0, every[-1:])
+    pass_on(1, every[-1:], False)
+    d_fetch(1, every[-1:])
+    d_ready(1, every)
 
     @pl.loop(0, tokens // tchunk)
     def _(chunk):
-        total = combine(2, 1, chunk)
+        total = combine(1, 1, 1, chunk, every)
         for p in range(per_chunk):
             i = chunk * per_chunk + p
-            partial_copy(i).wait_recv()
-            out_buf[i] = (total[p * piece:(p + 1) * piece] + part_in[i]).astype(BF16)
+            partial_copy(1, i).wait_recv()
+            out_buf[i] = (total[p * piece:(p + 1) * piece] + part_in[1, i]).astype(BF16)
             z_copy(i).start()
 
     y_out.wait()
-    for copy in sends:
-        copy.wait_send()
+    for copy in grad_copies(NE - 1):
+        copy.wait()
+    for role in range(2):
+        for k in range(3):
+            y_hop(role, k).wait_send()
+
+            @pl.loop(0, NE)
+            def _(e):
+                d_hop(role, k, e).wait_send()
 
     @pl.loop(0, pieces)
     def _(i):
-        partial_copy(i).wait_send()
+        partial_copy(1, i).wait_send()
         z_copy(i).wait()
 
 
-def run_collect(tok, y_back, dx_rows):
-    tokens = tok.shape[1]
-    dim = dx_rows.shape[3]
+def run_finish(code, tok, xb, q_rows, w_in, w_up, w_out, c_rows):
+    tokens, dim = xb.shape[1:]
+    hid = w_in.shape[3]
     pieces = 16
     any_spec = pl.BlockSpec(memory_space=pl.ANY)
+    vmem_spec = pl.BlockSpec(memory_space=pltpu.VMEM)
+    tok_shape = jax.ShapeDtypeStruct((tokens, dim), BF16)
+    hop_shape = jax.ShapeDtypeStruct((2, 3, NE, CAP, dim), BF16)
+    dma = pltpu.SemaphoreType.DMA
+    flops = 2 * NG * NE * CAP * (3 * tokens * dim + 8 * dim * hid)
     return pl.pallas_call(
-        collect_kernel,
-        name='collect',
-        out_shape=(jax.ShapeDtypeStruct((tokens, dim), BF16), jax.ShapeDtypeStruct((tokens, dim), BF16)),
-        in_specs=[pl.BlockSpec(memory_space=pltpu.VMEM)] + [any_spec] * 2,
-        out_specs=[any_spec] * 2,
+        finish_kernel,
+        name='finish',
+        out_shape=(tok_shape, tok_shape, jax.ShapeDtypeStruct(w_in.shape, BF16),
+                   jax.ShapeDtypeStruct(w_up.shape, BF16), jax.ShapeDtypeStruct(w_out.shape, BF16),
+                   hop_shape, hop_shape, jax.ShapeDtypeStruct((NG, NE, CAP, dim), BF16)),
+        in_specs=[vmem_spec] * 2 + [any_spec] * 6,
+        out_specs=[any_spec] * 8,
         scratch_shapes=[
-            pltpu.VMEM((2, NE, CAP, dim), BF16),
-            pltpu.VMEM((2, 4, NE, CAP, dim), BF16),
-            pltpu.VMEM((tokens, dim), F32),
+            pltpu.VMEM((2, tokens, dim), BF16),
+            pltpu.VMEM((NE, NG, CAP, dim), BF16),
+            pltpu.VMEM((2, NG, CAP, dim), BF16),
+            pltpu.VMEM((2, 3, dim, hid), BF16),
+            pltpu.VMEM((dim, hid), F32),
+            pltpu.VMEM((dim, hid), F32),
+            pltpu.VMEM((hid, dim), F32),
+            pltpu.VMEM((3, dim, hid), BF16),
+            pltpu.VMEM((NG, CAP, dim), BF16),
+            pltpu.VMEM((2, NE, 4, CAP, dim), BF16),
             pltpu.VMEM((pieces, tokens // pieces, dim), F32),
-            pltpu.VMEM((pieces, tokens // pieces, dim), F32),
+            pltpu.VMEM((2, pieces, tokens // pieces, dim), F32),
             pltpu.VMEM((pieces, tokens // pieces, dim), BF16),
             pltpu.VMEM((tokens, dim), BF16),
-            pltpu.SemaphoreType.DMA((2,)),
-            pltpu.SemaphoreType.DMA((2,)),
-            pltpu.SemaphoreType.DMA((2, 3)),
-            pltpu.SemaphoreType.DMA((2, 3)),
-            pltpu.SemaphoreType.DMA((pieces,)),
-            pltpu.SemaphoreType.DMA((pieces,)),
-            pltpu.SemaphoreType.DMA((pieces,)),
-            pltpu.SemaphoreType.DMA((pieces,)),
+            dma((2,)), dma((2,)), dma((2, 3)), dma((3,)), dma, dma((1, 4)), dma((2, NE, 4)), dma,
+            dma((2, 3)), dma((2, 3)), dma((NE, 2, 3)), dma((NE, 2, 3)),
+            dma((2, pieces)), dma((2, pieces)), dma((pieces,)), dma((pieces,)),
         ],
-        cost_estimate=pl.CostEstimate(flops=4 * tokens * NG * NE * CAP * dim,
-                                      bytes_accessed=20_000_000, transcendentals=0),
-        compiler_params=pltpu.CompilerParams(collective_id=2, has_side_effects=True,
-                                             vmem_limit_bytes=64_000_000),
-    )(tok, y_back, dx_rows)
+        cost_estimate=pl.CostEstimate(flops=flops, bytes_accessed=80_000_000, transcendentals=0),
+        compiler_params=pltpu.CompilerParams(collective_id=1, has_side_effects=True,
+                                             vmem_limit_bytes=67_043_328),
+    )(code, tok, xb, q_rows, w_in, w_up, w_out, c_rows)
 
 
 def solution(mesh):
     def device_fn(x_acts, expert_ids, gate_wts, w_in, w_up, w_out, d_out):
-        dim = x_acts.shape[3]
         ids_t = jnp.swapaxes(expert_ids[:, 0], 1, 2)
         gates_t = jnp.swapaxes(gate_wts[:, 0], 1, 2)
         c_rows, xb, q_rows, code, tok = run_dispatch(x_acts, d_out, ids_t, gates_t, w_in, w_up, w_out)
-        y_back = lax.all_to_all(c_rows.reshape(NG, NE * CAP, dim), 'expert', 0, 0, tiled=True)
-        dx_rows, dw_in, dw_up, dw_out = run_backward(code, xb, q_rows, w_in, w_up, w_out)
-        y_back = y_back.reshape(c_rows.shape)
-        y_dev, dx_dev = run_collect(tok, y_back, dx_rows)
+        y_dev, dx_dev, dw_in, dw_up, dw_out = run_finish(
+            code, tok, xb, q_rows, w_in, w_up, w_out, c_rows)[:5]
         return y_dev[None], dx_dev[None], dw_in, dw_up, dw_out
 
     tok_spec = P(None, 'stage', 'expert', None)

time: 317 us -> 311 us (0.981)
  waiting for transfers between devices: 14.6 us -> 0 us
  local copies, waits for them, and re-layouts: 3.65 us -> 13 us
  starting transfers between devices: 5.09 us -> 0 us
  Pallas kernels: 293 us -> 297 us
    all_to_all x1 -> x0, waiting for transfers between devices: 14.6 us -> none  [device_fn(): lax.all_to_all(c_rows.reshape(NG, NE * CAP, dim), 'expert', 0, 0, tiled=T...]
    unnamed x4 -> x11, local copies, waits for them, and re-layouts: 3.65 us -> 13 us
    all_to_all x1 -> x0, starting transfers between devices: 5.09 us -> none  [device_fn(): lax.all_to_all(c_rows.reshape(NG, NE * CAP, dim), 'expert', 0, 0, tiled=T...]
    pallas_call x2 -> x1, Pallas kernels: 154 us -> 158 us  [run_finish(): pl.pallas_call(finish_kernel, name='finish', out_shape=(tok_shape, tok_sh...]
  transfers between devices with their start and end apart: 1 -> 0, of which waited for: 1 -> 0; matrix products, arithmetic and copies ran while one was open for 0% -> 0% of each run, Pallas kernels for 23% -> 0%
where the time goes in v5:
time: 311 us; the launch traced here: 310 us
  Pallas kernels  297 us (95%)
  local copies, waits for them, and re-layouts  13 us (4%)
    pallas_call x1, Pallas kernels, run_finish(): pl.pallas_call(finish_kernel, name='finish', out_shape=(tok_shape, tok_sh...  158 us
    pallas_call x1, Pallas kernels, run_dispatch(): pl.pallas_call(dispatch_kernel, name='dispatch', out_shape=(jax.ShapeDtyp...  139 us
    unnamed x11, local copies, waits for them, and re-layouts  13 us

profile of v5, /device:TPU:0, one launch (start us, length us, event | category | flops | bytes accessed | tf_op | source)
XLA Modules:
  0.0 310.3 jit_solution(3032567538160906633)
XLA Ops:
  0.6 138.7 %dispatch.1 = (bf16[8,4,192,640]{3,2,1,0:T(8,128)(2,1)}, bf16[8,1024,640]{2,1,0:T(8,128)(2,1)}, bf16[4,8,192,640]{3,2,1,0:T(8,128)(2,1)}, f32[8,8,1024]{2,1,0:T(8,128)}, f32[2,2,1024,128]{3,2,1,0:T(8,128)}) custom-call(bf16[2,1,1024,640]{3,2,1,0:T(8,128)(2,1)} %x_ref.1, bf16[1,1024,640]{2,1,0:T(8,128)(2,1)} %dy_ref.1, s32[2,4,1024]{2,1,0:T(4,128)} %bitcast.10, ...), custom_call_target="tpu_custom_call" | custom-call | flops 31205621760 | bytes 60000000 | tf_op jit(solution)/shard_map/dispatch/pallas_call | solution.py:272
  139.3 157.9 %finish.1 = (bf16[1024,640]{1,0:T(8,128)(2,1)}, bf16[1024,640]{1,0:T(8,128)(2,1)}, bf16[1,4,640,640]{3,2,1,0:T(8,128)(2,1)}, bf16[1,4,640,640]{3,2,1,0:T(8,128)(...) custom-call(f32[8,8,1024]{2,1,0:T(8,128)} %get-tuple-element.15.code, ...), custom_call_target="tpu_custom_call" | custom-call | flops 64424509440 | bytes 80000000 | tf_op jit(solution)/shard_map/finish/pallas_call | solution.py:603
  297.3 0.0 copy-start.2
  297.3 2.6 copy.17
  299.9 2.5 copy.18
  302.4 0.0 copy-done.2
  302.4 0.0 copy-start.1
  302.4 1.7 copy.19
  304.1 1.4 copy-done.1
  305.5 0.0 copy-start
  305.5 1.7 copy.20
  307.2 1.4 copy-done
  308.6 1.7 copy.21
Async XLA Ops:
  297.3 5.1 %copy-start.2 = (bf16[1,4,640,640]{3,2,1,0:T(8,128)(2,1)S(1)}, bf16[1,4,640,640]{3,2,1,0:T(8,128)(2,1)}, u32[]{:S(2)}) copy-start(bf16[1,4,640,640]{3,2,1,0:T(8,128)(2,1)} %get-tuple-element.32) | copy-start | bytes 9830404
  302.4 3.1 %copy-start.1 = (bf16[1,4,640,640]{3,2,1,0:T(8,128)(2,1)S(1)}, bf16[1,4,640,640]{3,2,1,0:T(8,128)(2,1)}, u32[]{:S(2)}) copy-start(bf16[1,4,640,640]{3,2,1,0:T(8,128)(2,1)} %get-tuple-element.33) | copy-start | bytes 9830404
  305.5 3.1 %copy-start = (bf16[1,4,640,640]{3,2,1,0:T(8,128)(2,1)S(1)}, bf16[1,4,640,640]{3,2,1,0:T(8,128)(2,1)}, u32[]{:S(2)}) copy-start(bf16[1,4,640,640]{3,2,1,0:T(8,128)(2,1)} %get-tuple-element.34) | copy-start | bytes 9830404

commit v6 on v5

--- a/solution.py
+++ b/solution.py
@@ -633,13 +633,47 @@
     )(code, tok, xb, q_rows, w_in, w_up, w_out, c_rows)
 
 
+def settle_kernel(*refs):
+    count = (len(refs) - 2) // 3
+    srcs, dsts, bufs = refs[:count], refs[count:2 * count], refs[2 * count:3 * count]
+    rsem, wsem = refs[3 * count:]
+    parts = [(k, i) for i in range(4) for k in range(count)]
+    reads, writes = [], []
+    for n, (k, i) in enumerate(parts):
+        reads.append(pltpu.make_async_copy(srcs[k].at[i], bufs[k].at[i], rsem.at[n]))
+        writes.append(pltpu.make_async_copy(bufs[k].at[i], dsts[k].at[i], wsem.at[n]))
+        reads[-1].start()
+    for read, write in zip(reads, writes):
+        read.wait()
+        write.start()
+    for write in writes:
+        write.wait()
+
+
+def run_settle(arrays):
+    flat = [a.reshape(4, -1, a.shape[-1]) for a in arrays]
+    any_spec = pl.BlockSpec(memory_space=pl.ANY)
+    count = len(flat)
+    outs = pl.pallas_call(
+        settle_kernel,
+        name='settle',
+        out_shape=tuple(jax.ShapeDtypeStruct(a.shape, a.dtype) for a in flat),
+        in_specs=[any_spec] * count,
+        out_specs=[any_spec] * count,
+        scratch_shapes=[pltpu.VMEM(a.shape, a.dtype) for a in flat] + [
+            pltpu.SemaphoreType.DMA((4 * count,)), pltpu.SemaphoreType.DMA((4 * count,))],
+        compiler_params=pltpu.CompilerParams(vmem_limit_bytes=64_000_000),
+    )(*flat)
+    return [out.reshape(a.shape) for out, a in zip(outs, arrays)]
+
+
 def solution(mesh):
     def device_fn(x_acts, expert_ids, gate_wts, w_in, w_up, w_out, d_out):
         ids_t = jnp.swapaxes(expert_ids[:, 0], 1, 2)
         gates_t = jnp.swapaxes(gate_wts[:, 0], 1, 2)
         c_rows, xb, q_rows, code, tok = run_dispatch(x_acts, d_out, ids_t, gates_t, w_in, w_up, w_out)
-        y_dev, dx_dev, dw_in, dw_up, dw_out = run_finish(
-            code, tok, xb, q_rows, w_in, w_up, w_out, c_rows)[:5]
+        y_dev, dx_dev, dw_in, dw_up, dw_out = run_settle(run_finish(
+            code, tok, xb, q_rows, w_in, w_up, w_out, c_rows)[:5])
         return y_dev[None], dx_dev[None], dw_in, dw_up, dw_out
 
     tok_spec = P(None, 'stage', 'expert', None)

time: 311 us -> 307 us (0.987)
  local copies, waits for them, and re-layouts: 13 us -> 0 us
  Pallas kernels: 297 us -> 306 us
    unnamed x11 -> x0, local copies, waits for them, and re-layouts: 13 us -> none
    pallas_call x0 -> x1, Pallas kernels: none -> 9.43 us  [run_settle(): pl.pallas_call(settle_kernel, name='settle', out_shape=tuple((jax.ShapeDt...]
where the time goes in v6:
time: 307 us
  Pallas kernels  306 us (100%)
    pallas_call x1, Pallas kernels, run_finish(): pl.pallas_call(finish_kernel, name='finish', out_shape=(tok_shape, tok_sh...  158 us
    pallas_call x1, Pallas kernels, run_dispatch(): pl.pallas_call(dispatch_kernel, name='dispatch', out_shape=(jax.ShapeDtyp...  139 us
    pallas_call x1, Pallas kernels, run_settle(): pl.pallas_call(settle_kernel, name='settle', out_shape=tuple((jax.ShapeDt...  9.43 us

profile of v6, /device:TPU:0, one launch (start us, length us, event | category | flops | bytes accessed | tf_op | source)
XLA Modules:
  0.0 306.9 jit_solution(799547522538185705)
XLA Ops:
  0.6 138.7 %dispatch.1 = (bf16[8,4,192,640]{3,2,1,0:T(8,128)(2,1)}, bf16[8,1024,640]{2,1,0:T(8,128)(2,1)}, bf16[4,8,192,640]{3,2,1,0:T(8,128)(2,1)}, f32[8,8,1024]{2,1,0:T(8,128)}, f32[2,2,1024,128]{3,2,1,0:T(8,128)}) custom-call(bf16[2,1,1024,640]{3,2,1,0:T(8,128)(2,1)} %x_ref.1, bf16[1,1024,640]{2,1,0:T(8,128)(2,1)} %dy_ref.1, s32[2,4,1024]{2,1,0:T(4,128)} %bitcast.26, ...), custom_call_target="tpu_custom_call" | custom-call | flops 31205621760 | bytes 60000000 | tf_op jit(solution)/shard_map/dispatch/pallas_call | solution.py:272
  139.3 157.9 %finish.1 = (bf16[1024,640]{1,0:T(8,128)(2,1)}, bf16[1024,640]{1,0:T(8,128)(2,1)}, bf16[1,4,640,640]{3,2,1,0:T(8,128)(2,1)}, bf16[1,4,640,640]{3,2,1,0:T(8,128)(...) custom-call(f32[8,8,1024]{2,1,0:T(8,128)} %get-tuple-element.20.code, ...), custom_call_target="tpu_custom_call" | custom-call | flops 64424509440 | bytes 80000000 | tf_op jit(solution)/shard_map/finish/pallas_call | solution.py:603
  297.3 9.4 %settle.1 = (bf16[4,256,640]{2,1,0:T(8,128)(2,1)}, bf16[4,256,640]{2,1,0:T(8,128)(2,1)}, bf16[4,640,640]{2,1,0:T(8,128)(2,1)}, bf16[4,640,640]{2,1,0:T(8,128)(2,1)}, bf16[4,640,640]{2,1,0:T(8,128)(2,1)}) custom-call(bf16[4,256,640]{2,1,0:T(8,128)(2,1)} %bitcast.19, bf16[4,256,640]{2,1,0:T(8,128)(2,1)} %bitcast.20, bf16[4,640,640]{2,1,0:T(8,128)(2,1)} %bitcast.16, ...), custom_call_target="tpu_custom_call" | custom-call | tf_op jit(solution)/shard_map/settle/pallas_call | solution.py:657

commit v7 on v6

--- a/solution.py
+++ b/solution.py
@@ -57,26 +57,26 @@
             send_sem=ssem.at[arr, slot], recv_sem=rsem.at[arr, h, part],
             device_id=peer, device_id_type=MESH)
 
-    def send(arr, h, part, slot, peer, src=None):
-        remote(arr, h, part, slot, peer, src).start()
-        sends.append((arr, h, part, slot, peer, src))
+    def send(arr, h, part, peer, src=None):
+        sends.append((arr, h, part, sum(done[0] == arr for done in sends), peer, src))
+        remote(*sends[-1]).start()
 
     def arrived(arr, h, part):
         remote(arr, h, part, 0, (stage, sib)).wait_recv()
 
     to_x, to_y, to_sib, to_z = (stage, xn), (stage, yn), (stage, sib), (other, me)
 
-    send(IDS, me, 0, 14, to_z, ids_ref)
-    send(GTS, me, 0, 14, to_z, gts_ref)
+    send(IDS, me, 0, to_z, ids_ref)
+    send(GTS, me, 0, to_z, gts_ref)
     for part in range(2):
-        send(XF, me, part, 14 + part, to_z, x_ref.at[1, 0, pl.ds(part * half, half)])
+        send(XF, me, part, to_z, x_ref.at[1, 0, pl.ds(part * half, half)])
     for part in range(2):
-        send(XB, me, part, 14 + part, to_z, x_ref.at[0, 0, pl.ds(part * half, half)])
+        send(XB, me, part, to_z, x_ref.at[0, 0, pl.ds(part * half, half)])
     dy_half = lambda part: dy_ref.at[0, pl.ds(part * half, half)]
-    send(DY, me, 0, 0, to_x, dy_half(0))
-    send(DY, me, 1, 2, to_y, dy_half(1))
-    send(DY, me, 0, 4, to_sib, dy_half(0))
-    send(DY, me, 1, 5, to_sib, dy_half(1))
+    send(DY, me, 0, to_x, dy_half(0))
+    send(DY, me, 1, to_y, dy_half(1))
+    send(DY, me, 0, to_sib, dy_half(0))
+    send(DY, me, 1, to_sib, dy_half(1))
     own_dy = pltpu.make_async_copy(dy_ref.at[0], buf.at[DY, me], lsem)
     own_dy.start()
 
@@ -90,54 +90,54 @@
 
     for arr in (IDS, GTS):
         arrived(arr, me, 0)
-        send(arr, me, 0, 0, to_x)
-        send(arr, me, 0, 2, to_y)
-        send(arr, me, 0, 4, to_sib)
-    send(DY, me, 1, 1, to_x, dy_half(1))
-    send(DY, me, 0, 3, to_y, dy_half(0))
+        send(arr, me, 0, to_x)
+        send(arr, me, 0, to_y)
+        send(arr, me, 0, to_sib)
+    send(DY, me, 1, to_x, dy_half(1))
+    send(DY, me, 0, to_y, dy_half(0))
 
     def first_halves(arr):
         arrived(arr, xn, 0)
         arrived(arr, yn, 1)
-        send(arr, xn, 0, 6, to_y)
-        send(arr, yn, 1, 7, to_x)
-        send(arr, xn, 0, 8, to_sib)
-        send(arr, yn, 1, 11, to_sib)
+        send(arr, xn, 0, to_y)
+        send(arr, yn, 1, to_x)
+        send(arr, xn, 0, to_sib)
+        send(arr, yn, 1, to_sib)
 
     def second_halves(arr):
         arrived(arr, xn, 1)
         arrived(arr, yn, 0)
-        send(arr, xn, 1, 9, to_sib)
-        send(arr, yn, 0, 10, to_sib)
+        send(arr, xn, 1, to_sib)
+        send(arr, yn, 0, to_sib)
 
     def diagonal(arr):
         for part in range(2):
             arrived(arr, dg, part)
-            send(arr, dg, part, 12 + part, to_sib)
+            send(arr, dg, part, to_sib)
 
     def own_sends(arr):
         for part in range(2):
             arrived(arr, me, part)
-        send(arr, me, 0, 0, to_x)
-        send(arr, me, 1, 2, to_y)
-        send(arr, me, 1, 1, to_x)
-        send(arr, me, 0, 3, to_y)
-        send(arr, me, 0, 4, to_sib)
-        send(arr, me, 1, 5, to_sib)
+        send(arr, me, 0, to_x)
+        send(arr, me, 1, to_y)
+        send(arr, me, 1, to_x)
+        send(arr, me, 0, to_y)
+        send(arr, me, 0, to_sib)
+        send(arr, me, 1, to_sib)
 
     for arr in (IDS, GTS):
         arrived(arr, xn, 0)
         arrived(arr, yn, 0)
-        send(arr, xn, 0, 6, to_y)
+        send(arr, xn, 0, to_y)
     first_halves(DY)
     for arr in (IDS, GTS):
-        send(arr, xn, 0, 8, to_sib)
-        send(arr, yn, 0, 10, to_sib)
+        send(arr, xn, 0, to_sib)
+        send(arr, yn, 0, to_sib)
     own_sends(XF)
     second_halves(DY)
     for arr in (IDS, GTS):
         arrived(arr, dg, 0)
-        send(arr, dg, 0, 12, to_sib)
+        send(arr, dg, 0, to_sib)
         for h in (sib, sib_of(xn), sib_of(yn), sib_of(dg)):
             arrived(arr, h, 0)
 
@@ -347,7 +347,8 @@
     line = xn + core * (yn - xn)
     line0 = 2 * (line // 2)
     tokens, dim = y_buf.shape
-    pieces, piece = part_out.shape[:2]
+    pieces, piece = part_out.shape[1:3]
+    held = pieces // 2
     tchunk = 256
     per_chunk = tchunk // piece
 
@@ -450,7 +451,7 @@
 
     def partial_copy(kind, i):
         return pltpu.make_async_remote_copy(
-            src_ref=part_out.at[i], dst_ref=part_in.at[kind, i], send_sem=psem.at[kind, i],
+            src_ref=part_out.at[kind, i], dst_ref=part_in.at[kind, i], send_sem=psem.at[kind, i],
             recv_sem=prsem.at[kind, i], device_id=(stage, partner), device_id_type=MESH)
 
     def z_copy(i):
@@ -465,10 +466,14 @@
             for p in range(per_chunk):
                 i = chunk * per_chunk + p
                 part = total[p * piece:(p + 1) * piece]
-                part_out[i] = part if first else part_out[i] + part
+                part_out[kind, i] = part if first else part_out[kind, i] + part
             if experts[-1] == NE - 1:
                 for p in range(per_chunk):
-                    partial_copy(kind, chunk * per_chunk + p).start()
+                    i = chunk * per_chunk + p
+                    if kind:
+                        partial_copy(kind, i).start()
+                    else:
+                        pl.when(i < held)(lambda: partial_copy(kind, i).start())
 
     def y_pass_on():
         for slot in range(3):
@@ -533,6 +538,23 @@
             for k in range(3):
                 d_hop(role, k, e).start()
 
+    @pl.loop(held, pieces)
+    def _(i):
+        partial_copy(0, i).start()
+
+    def d_ready(role, experts):
+        for e in experts:
+            for copy in d_load(role, e):
+                copy.wait()
+
+    d_fetch(0, every[:-1])
+    d_ready(0, every[:-1])
+    pass_on(1, every[:-1], True)
+    d_fetch(1, every[:-1])
+    d_fetch(0, every[-1:])
+    d_ready(0, every[-1:])
+    pass_on(1, every[-1:], False)
+
     for slot in range(3):
         y_arrived(1, slot)
     y_load(1)
@@ -549,18 +571,6 @@
     y_out = pltpu.make_async_copy(y_buf, y_ref, ysem)
     y_out.start()
 
-    def d_ready(role, experts):
-        for e in experts:
-            for copy in d_load(role, e):
-                copy.wait()
-
-    d_fetch(0, every[:-1])
-    d_ready(0, every[:-1])
-    pass_on(1, every[:-1], True)
-    d_fetch(1, every[:-1])
-    d_fetch(0, every[-1:])
-    d_ready(0, every[-1:])
-    pass_on(1, every[-1:], False)
     d_fetch(1, every[-1:])
     d_ready(1, every)
 
@@ -619,7 +629,7 @@
             pltpu.VMEM((3, dim, hid), BF16),
             pltpu.VMEM((NG, CAP, dim), BF16),
             pltpu.VMEM((2, NE, 4, CAP, dim), BF16),
-            pltpu.VMEM((pieces, tokens // pieces, dim), F32),
+            pltpu.VMEM((2, pieces, tokens // pieces, dim), F32),
             pltpu.VMEM((2, pieces, tokens // pieces, dim), F32),
             pltpu.VMEM((pieces, tokens // pieces, dim), BF16),
             pltpu.VMEM((tokens, dim), BF16),

time: 307 us -> 302 us (0.984)
  Pallas kernels: 306 us -> 301 us
    pallas_call x1, Pallas kernels: 158 us -> 153 us  [run_finish(): pl.pallas_call(finish_kernel, name='finish', out_shape=(tok_shape, tok_sh...]
where the time goes in v7:
time: 302 us
  Pallas kernels  301 us (100%)
    pallas_call x1, Pallas kernels, run_finish(): pl.pallas_call(finish_kernel, name='finish', out_shape=(tok_shape, tok_sh...  153 us
    pallas_call x1, Pallas kernels, run_dispatch(): pl.pallas_call(dispatch_kernel, name='dispatch', out_shape=(jax.ShapeDtyp...  139 us
    pallas_call x1, Pallas kernels, run_settle(): pl.pallas_call(settle_kernel, name='settle', out_shape=tuple((jax.ShapeDt...  9.43 us

profile of v7, /device:TPU:0, one launch (start us, length us, event | category | flops | bytes accessed | tf_op | source)
XLA Modules:
  0.0 302.2 jit_solution(13078254099955574870)
XLA Ops:
  0.6 138.7 %dispatch.1 = (bf16[8,4,192,640]{3,2,1,0:T(8,128)(2,1)}, bf16[8,1024,640]{2,1,0:T(8,128)(2,1)}, bf16[4,8,192,640]{3,2,1,0:T(8,128)(2,1)}, f32[8,8,1024]{2,1,0:T(8,128)}, f32[2,2,1024,128]{3,2,1,0:T(8,128)}) custom-call(bf16[2,1,1024,640]{3,2,1,0:T(8,128)(2,1)} %x_ref.1, bf16[1,1024,640]{2,1,0:T(8,128)(2,1)} %dy_ref.1, s32[2,4,1024]{2,1,0:T(4,128)} %bitcast.26, ...), custom_call_target="tpu_custom_call" | custom-call | flops 31205621760 | bytes 60000000 | tf_op jit(solution)/shard_map/dispatch/pallas_call | solution.py:272
  139.3 153.2 %finish.1 = (bf16[1024,640]{1,0:T(8,128)(2,1)}, bf16[1024,640]{1,0:T(8,128)(2,1)}, bf16[1,4,640,640]{3,2,1,0:T(8,128)(2,1)}, bf16[1,4,640,640]{3,2,1,0:T(8,128)(...) custom-call(f32[8,8,1024]{2,1,0:T(8,128)} %get-tuple-element.20.code, ...), custom_call_target="tpu_custom_call" | custom-call | flops 64424509440 | bytes 80000000 | tf_op jit(solution)/shard_map/finish/pallas_call | solution.py:613
  292.6 9.4 %settle.1 = (bf16[4,256,640]{2,1,0:T(8,128)(2,1)}, bf16[4,256,640]{2,1,0:T(8,128)(2,1)}, bf16[4,640,640]{2,1,0:T(8,128)(2,1)}, bf16[4,640,640]{2,1,0:T(8,128)(2,1)}, bf16[4,640,640]{2,1,0:T(8,128)(2,1)}) custom-call(bf16[4,256,640]{2,1,0:T(8,128)(2,1)} %bitcast.19, bf16[4,256,640]{2,1,0:T(8,128)(2,1)} %bitcast.20, bf16[4,640,640]{2,1,0:T(8,128)(2,1)} %bitcast.16, ...), custom_call_target="tpu_custom_call" | custom-call | tf_op jit(solution)/shard_map/settle/pallas_call | solution.py:667

commit v8 on v7

--- a/solution.py
+++ b/solution.py
@@ -251,8 +251,7 @@
             for copy in weights(e + 2):
                 copy.start()
 
-    diagonal(XB)
-    for h in (sib, sib_of(xn), sib_of(yn), sib_of(dg)):
+    for h in (sib, sib_of(xn), sib_of(yn), dg):
         arrived(XB, h, 0)
         arrived(XB, h, 1)
     for slot in range(2):
@@ -333,7 +332,7 @@
                   y_ref, dx_ref, dwin_ref, dwup_ref, dwout_ref, yhop_ref, dhop_ref, rows_ref,
                   xbuf, xs, qbuf, wbuf, acc_in, acc_up, acc_out, dwst, dxst, rbuf, part_out, part_in,
                   out_buf, y_buf,
-                  xsem, qsem, wsem, dwsem, dxsem, rbsem, rdsem, ysem,
+                  xsem, qsem, wsem, dwsem, dxsem, rbsem, rdsem, ysem, sidesem,
                   ssem, rsem, dsem, drsem, psem, prsem, zsem, zrsem):
     stage = lax.axis_index('stage')
     me = lax.axis_index('expert')
@@ -385,32 +384,48 @@
             src_ref=rows_ref.at[me, e], dst_ref=dhop_ref.at[role, slot, e], send_sem=dsem.at[e, role, 0],
             recv_sem=drsem.at[e, role, slot], device_id=(stage, sib), device_id_type=MESH).wait_recv()
 
+    def x_side():
+        return pltpu.make_async_remote_copy(
+            src_ref=xb_ref.at[dg], dst_ref=y_buf, send_sem=sidesem.at[0], recv_sem=sidesem.at[1],
+            device_id=(stage, sib), device_id_type=MESH)
+
     for role in range(2):
         for k in range(3):
             y_hop(role, k).start()
+        if role == 0:
+            x_side().start()
 
     def weights(e):
         return [pltpu.make_async_copy(w.at[0, e], wbuf.at[e % 2, k], wsem.at[e % 2, k])
                 for k, w in enumerate((win_ref, wup_ref, wout_ref))] + [
             pltpu.make_async_copy(q_ref.at[e], qbuf.at[e % 2], qsem.at[e % 2])]
 
-    def x_fetch(h):
-        return pltpu.make_async_copy(xb_ref.at[h], xbuf.at[h % 2], xsem.at[h % 2])
+    def shard(i):
+        j, odd = i // 2, i % 2
+        return me + (j % 2) * (xn - me) + (j // 2) * (yn - me) + odd * (sib - me)
+
+    def x_fetch(i):
+        return pltpu.make_async_copy(xb_ref.at[shard(i)], xbuf.at[i % 2], xsem.at[i % 2])
 
     x_fetch(0).start()
     for e in range(2):
         for copy in weights(e):
             copy.start()
 
-    @pl.loop(0, NG)
-    def _(h):
-        pl.when(h + 1 < NG)(lambda: x_fetch(h + 1).start())
+    def gather(h, wait, tok_rows):
         hits = slot_hits(code_ref[h], tokens)
         onehot = jnp.concatenate([jnp.where(hit, 1.0, 0.0).astype(BF16) for hit in hits], axis=0)
-        x_fetch(h).wait()
-        rows = dot(onehot, xbuf[h % 2]).astype(BF16)
+        wait()
+        rows = dot(onehot, tok_rows[...]).astype(BF16)
         for e in range(NE):
             xs[e, h] = rows[e * CAP:(e + 1) * CAP]
+
+    @pl.loop(0, NG - 1)
+    def _(i):
+        pl.when(i + 1 < NG - 1)(lambda: x_fetch(i + 1).start())
+        gather(shard(i), lambda: x_fetch(i).wait(), xbuf.at[i % 2])
+
+    gather(sib_of(dg), x_side().wait_recv, y_buf)
 
     sources = (sib, line0, line0 + 1, me)
 
@@ -584,6 +599,7 @@
             z_copy(i).start()
 
     y_out.wait()
+    x_side().wait_send()
     for copy in grad_copies(NE - 1):
         copy.wait()
     for role in range(2):
@@ -633,7 +649,7 @@
             pltpu.VMEM((2, pieces, tokens // pieces, dim), F32),
             pltpu.VMEM((pieces, tokens // pieces, dim), BF16),
             pltpu.VMEM((tokens, dim), BF16),
-            dma((2,)), dma((2,)), dma((2, 3)), dma((3,)), dma, dma((1, 4)), dma((2, NE, 4)), dma,
+            dma((2,)), dma((2,)), dma((2, 3)), dma((3,)), dma, dma((1, 4)), dma((2, NE, 4)), dma, dma((2,)),
             dma((2, 3)), dma((2, 3)), dma((NE, 2, 3)), dma((NE, 2, 3)),
             dma((2, pieces)), dma((2, pieces)), dma((pieces,)), dma((pieces,)),
         ],

time: 302 us -> 300 us (level)
  no operation moved by 1% of the time
where the time goes in v8:
time: 300 us
  Pallas kernels  299 us (100%)
    pallas_call x1, Pallas kernels, run_finish(): pl.pallas_call(finish_kernel, name='finish', out_shape=(tok_shape, tok_sh...  153 us
    pallas_call x1, Pallas kernels, run_dispatch(): pl.pallas_call(dispatch_kernel, name='dispatch', out_shape=(jax.ShapeDtyp...  136 us
    pallas_call x1, Pallas kernels, run_settle(): pl.pallas_call(settle_kernel, name='settle', out_shape=tuple((jax.ShapeDt...  9.43 us

profile of v8, /device:TPU:0, one launch (start us, length us, event | category | flops | bytes accessed | tf_op | source)
XLA Modules:
  0.0 299.6 jit_solution(881513505997117332)
XLA Ops:
  0.6 136.1 %dispatch.1 = (bf16[8,4,192,640]{3,2,1,0:T(8,128)(2,1)}, bf16[8,1024,640]{2,1,0:T(8,128)(2,1)}, bf16[4,8,192,640]{3,2,1,0:T(8,128)(2,1)}, f32[8,8,1024]{2,1,0:T(8,128)}, f32[2,2,1024,128]{3,2,1,0:T(8,128)}) custom-call(bf16[2,1,1024,640]{3,2,1,0:T(8,128)(2,1)} %x_ref.1, bf16[1,1024,640]{2,1,0:T(8,128)(2,1)} %dy_ref.1, s32[2,4,1024]{2,1,0:T(4,128)} %bitcast.26, ...), custom_call_target="tpu_custom_call" | custom-call | flops 31205621760 | bytes 60000000 | tf_op jit(solution)/shard_map/dispatch/pallas_call | solution.py:271
  136.8 153.2 %finish.1 = (bf16[1024,640]{1,0:T(8,128)(2,1)}, bf16[1024,640]{1,0:T(8,128)(2,1)}, bf16[1,4,640,640]{3,2,1,0:T(8,128)(2,1)}, bf16[1,4,640,640]{3,2,1,0:T(8,128)(...) custom-call(f32[8,8,1024]{2,1,0:T(8,128)} %get-tuple-element.20.code, ...), custom_call_target="tpu_custom_call" | custom-call | flops 64424509440 | bytes 80000000 | tf_op jit(solution)/shard_map/finish/pallas_call | solution.py:629
  290.0 9.4 %settle.1 = (bf16[4,256,640]{2,1,0:T(8,128)(2,1)}, bf16[4,256,640]{2,1,0:T(8,128)(2,1)}, bf16[4,640,640]{2,1,0:T(8,128)(2,1)}, bf16[4,640,640]{2,1,0:T(8,128)(2,1)}, bf16[4,640,640]{2,1,0:T(8,128)(2,1)}) custom-call(bf16[4,256,640]{2,1,0:T(8,128)(2,1)} %bitcast.19, bf16[4,256,640]{2,1,0:T(8,128)(2,1)} %bitcast.20, bf16[4,640,640]{2,1,0:T(8,128)(2,1)} %bitcast.16, ...), custom_call_target="tpu_custom_call" | custom-call | tf_op jit(solution)/shard_map/settle/pallas_call | solution.py:683
